TPU v7x, 32 devices: a whole 2x2x4 slice. The times are simulated.
32 devices in a mesh: cells: 8 (over y, x, core), genes: 4 (over z).
Axes of the slice: x: 2, y: 2, z: 4, core: 2. Of those that a mesh axis runs over, the one named last changes fastest.
Arguments:
- counts: int32 [8192, 4096], P('cells', 'genes'), may hold values from 0 to 26, as said below
- library: int32 [8192], P('cells'), may hold values from 2000 to 19999
Outputs:
- adjacency: float32 [4096, 4096], P('cells', 'genes')
- connectivity: float32 [4096], P('cells')
Inputs may be any that keep to these rules, and one draw needn't show every extreme that they name: Non-negative integer counts.
All inputs are finite; a program needn't handle non-finite values.
Results may differ from a plain program's by a relative error of at most 0.006.
Values may be sent and summed in bfloat16 or wider, within the bound.
No kernel may reach another device: no remote copies, remote signals or barrier semaphores. Data moves between devices by JAX's collectives and lax.ppermute only.
A program may use at most 128 MiB of HBM per device.

v0:
```python
import jax
import jax.numpy as jnp
from jax import lax
from jax.sharding import PartitionSpec as P


def normalize(counts, library):
    factor = 10000.0 / library.astype(jnp.float32)
    return jnp.log1p(counts.astype(jnp.float32) * factor[:, None]).astype(jnp.bfloat16)


def cross_product(left, right):
    return lax.dot_general(
        left, right, (((0,), (0,)), ((), ())), preferred_element_type=jnp.float32
    )


def shards(counts, library):
    own_block = normalize(counts, library)
    col_width = own_block.shape[1]
    cell_groups = lax.axis_size("cells")
    gene_total = col_width * lax.axis_size("genes")
    row_width = gene_total // cell_groups
    total_cells = float(counts.shape[0] * cell_groups)
    widened = own_block.astype(jnp.float32)
    local_sums = jnp.sum(widened, axis=0)
    local_squares = jnp.sum(widened * widened, axis=0)
    block_sums, block_squares = lax.psum((local_sums, local_squares), "cells")
    gene_sums, gene_squares = (
        lax.all_gather(block_sums, "genes", axis=0, tiled=True),
        lax.all_gather(block_squares, "genes", axis=0, tiled=True),
    )
    full_block = lax.all_gather(own_block, "genes", axis=1, tiled=True)
    gram_tile = lax.psum_scatter(
        cross_product(full_block, own_block), "cells", scatter_dimension=0, tiled=True
    )
    means = gene_sums / total_cells
    variances = gene_squares / total_cells - means * means
    scales = lax.rsqrt(variances + 1e-05)
    row_first = lax.axis_index("cells") * row_width
    col_first = lax.axis_index("genes") * col_width
    row_means = lax.dynamic_slice_in_dim(means, row_first, row_width, 0)
    col_means = lax.dynamic_slice_in_dim(means, col_first, col_width, 0)
    row_scales = lax.dynamic_slice_in_dim(scales, row_first, row_width, 0)
    col_scales = lax.dynamic_slice_in_dim(scales, col_first, col_width, 0)
    correlation = (
        (gram_tile / total_cells - row_means[:, None] * col_means[None, :])
        * row_scales[:, None]
        * col_scales[None, :]
    )
    powered = correlation**6
    row_index = row_first + jnp.arange(row_width, dtype=jnp.int32)[:, None]
    col_index = col_first + jnp.arange(col_width, dtype=jnp.int32)[None, :]
    adjacency = jnp.where(row_index == col_index, jnp.float32(0.0), powered)
    connectivity = lax.psum(jnp.sum(adjacency, axis=1), "genes")
    return (adjacency, connectivity)


def solution(mesh):
    return jax.shard_map(
        shards,
        mesh=mesh,
        in_specs=(P("cells", "genes"), P("cells")),
        out_specs=(P("cells", "genes"), P("cells")),
        check_vma=False,
    )
```

profile of v0, /device:TPU:0, one launch (start us, length us, event | category | flops | bytes accessed | tf_op | source)
XLA Modules:
  0.0 318.0 jit_solution(6613592547870994486)
XLA Ops:
  7.2 0.0 all-gather.2.cloned.1.call-start
  7.2 0.7 convert_divide_fusion
  7.9 5.6 %convert_reduce_fusion = (f32[1024]{0:T(1024)S(1)}, f32[1024]{0:T(1024)S(1)}, bf16[1024,1024]{1,0:T(8,128)(2,1)}) fusion(f32[1024]{0:T(1024)S(1)} %convert_divide_fusion, s32[1024,1024]{1,0:T(8,128)} %param.2), kind=kLoop, calls=%fused_computation.1 | loop fusion | flops 7337984 | bytes 6303744 | tf_op jit(solution)/shard_map/reduce_sum | solution.py:26
  13.5 0.0 copy-start
  13.5 0.0 all-gather.2.cloned.1.call-update
  13.5 0.0 reduce-scatter.2.cloned.1.call-start
  13.5 152.4 %all-gather.2.cloned.1.call-done = bf16[1024,4096]{1,0:T(8,128)(2,1)} async-done(((bf16[1024,1024]{1,0:T(8,128)(2,1)}), bf16[1024,4096]{1,0:T(8,128)(2,1)}) %all-gather.2.cloned.1.call-update) | async-done | bytes 8388624 | tf_op jit(solution)/shard_map/all_gather | solution.py:33
  166.0 0.0 copy-done
  166.0 14.6 %fusion.4 = f32[4096,1024]{1,0:T(8,128)} fusion(bf16[1024,4096]{1,0:T(8,128)(2,1)} %all-gather.2.cloned.1.call-done, bf16[1024,1024]{1,0:T(8,128)(2,1)S(1)} %copy-done), kind=kOutput, calls=%fused_computation.12 | convolution fusion | flops 8589934592 | bytes 27262976 | tf_op jit(solution)/shard_map/dot_general | solution.py:13
  180.6 0.0 reduce-scatter.2.cloned.1.call-update
  180.7 14.0 %all-reduce = (f32[1024]{0:T(1024)S(1)}, f32[1024]{0:T(1024)S(1)}) all-reduce(f32[1024]{0:T(1024)S(1)} %get-tuple-element.3, f32[1024]{0:T(1024)S(1)} %get-tuple-element.2), channel_id=1, replica_groups=mesh['cells'=8,'genes'=4] {'cells'}, use_global_device_ids=true, to_apply=%region_4.0 | all-reduce | flops 2048 | bytes 16384 | tf_op jit(solution)/shard_map/psum | solution.py:28
  194.7 13.2 %all_gather.10 = f32[4096]{0:T(1024)S(1)} all-gather(f32[1024]{0:T(1024)S(1)} %get-tuple-element.5), channel_id=1, replica_groups=mesh['cells'=8,'genes'=4] {'genes'}, dimensions={0}, use_global_device_ids=true | all-gather | bytes 20480 | tf_op jit(solution)/shard_map/all_gather | solution.py:30
  207.9 13.2 %all_gather.11 = f32[4096]{0:T(1024)S(1)} all-gather(f32[1024]{0:T(1024)S(1)} %get-tuple-element.4), channel_id=1, replica_groups=mesh['cells'=8,'genes'=4] {'genes'}, dimensions={0}, use_global_device_ids=true | all-gather | bytes 20480 | tf_op jit(solution)/shard_map/all_gather | solution.py:31
  221.1 0.1 dynamic_slice.12
  221.2 0.1 dynamic_slice.14
  221.3 73.9 %reduce-scatter.2.cloned.1.call-done = f32[512,1024]{1,0:T(8,128)} async-done(((f32[4096,1024]{1,0:T(8,128)}), f32[512,1024]{1,0:T(8,128)}) %reduce-scatter.2.cloned.1.call-update) | async-done | bytes 2097168 | tf_op jit(solution)/shard_map/reduce_scatter | solution.py:34
  295.2 3.8 %fusion.2 = (f32[512]{0:T(512)S(1)}, f32[512,1024]{1,0:T(8,128)}) fusion(f32[1024]{0:T(1024)S(1)} %dynamic_slice.15, f32[512]{0:T(512)S(1)} %dynamic_slice.14, f32[1024]{0:T(1024)S(1)} %dynamic_slice.13, f32[512]{0:T(512)S(1)} %dynamic_slice.12, f32[512,1024]{1,0:T(8,128)} %reduce-scatter.2.cloned.1.call-done, s32[1024]{0:T(1024)S(1)} %iota_add_fusion, ...), kind=kLoop, calls=%fused_computation.11 | loop fusion | flops 5766656 | bytes 4214784 | tf_op jit(solution)/shard_map/reduce_sum | solution.py:55
  299.0 12.2 %psum.23 = f32[512]{0:T(512)} all-reduce(f32[512]{0:T(512)S(1)} %get-tuple-element.6), channel_id=1, replica_groups=mesh['cells'=8,'genes'=4] {'genes'}, use_global_device_ids=true, to_apply=%region_6.7 | all-reduce | flops 512 | bytes 4096 | tf_op jit(solution)/shard_map/psum | solution.py:55
  (5 shorter events, 0.0 us)
Async XLA Ops:
  7.2 158.8 %all-gather.2.cloned.1.call-start = ((), (), s32[]{:S(2)}) async-start(), calls=%async_computation.1 | async-start | bytes 10485760 | tf_op jit(solution)/shard_map/all_gather | solution.py:33
  13.5 152.5 %copy-start = (bf16[1024,1024]{1,0:T(8,128)(2,1)S(1)}, bf16[1024,1024]{1,0:T(8,128)(2,1)}, u32[]{:S(2)}) copy-start(bf16[1024,1024]{1,0:T(8,128)(2,1)} %get-tuple-element.8) | copy-start | bytes 6291460
  13.5 281.7 %reduce-scatter.2.cloned.1.call-start = ((), (), s32[]{:S(2)}) async-start(), calls=%async_computation.2 | async-start | bytes 18874368 | tf_op jit(solution)/shard_map/reduce_scatter | solution.py:34
Sparse Core Ops, SparseCore 0:
  13.6 152.3 all-gather.1
  180.8 114.3 reduce-scatter.1
where the time goes:
time: 318 us
  waiting for transfers between devices  226 us (71%)
  blocking collectives  52.7 us (17%)
  matrix products  14.6 us (5%)
  between operations  14.1 us (4%)
  other arithmetic  10 us (3%)
    all_gather x1, waiting for transfers between devices, shards(): full_block = lax.all_gather(own_block, 'genes', axis=1, tiled=True)  152 us
    reduce_scatter x1, waiting for transfers between devices, shards(): lax.psum_scatter(cross_product(full_block, own_block), 'cells', scatter_d...  73.9 us
    dot_general x1, matrix products, cross_product(): lax.dot_general(left, right, (((0,), (0,)), ((), ())), preferred_element_...  14.6 us
    psum x1, blocking collectives, shards(): block_sums, block_squares = lax.psum((local_sums, local_squares), 'cells')  14 us
    all_gather x1, blocking collectives, shards(): lax.all_gather(block_sums, 'genes', axis=0, tiled=True)  13.2 us
    all_gather x1, blocking collectives, shards(): lax.all_gather(block_squares, 'genes', axis=0, tiled=True)  13.2 us
    psum x1, blocking collectives, shards(): connectivity = lax.psum(jnp.sum(adjacency, axis=1), 'genes')  12.2 us
  transfers between devices with their start and end apart: 2, of which 2 were waited for; matrix products, arithmetic and copies ran while one was open for 0% of the time, Pallas kernels for 0%

commit v1 on v0

--- a/solution.py
+++ b/solution.py
@@ -1,7 +1,14 @@
+import functools
+
 import jax
 import jax.numpy as jnp
 from jax import lax
+from jax.experimental import pallas as pl
+from jax.experimental.pallas import tpu as pltpu
 from jax.sharding import PartitionSpec as P
+
+
+AXES = ("cells", "genes")
 
 
 def normalize(counts, library):
@@ -15,7 +22,7 @@
     )
 
 
-def shards(counts, library):
+def general_shards(counts, library):
     own_block = normalize(counts, library)
     col_width = own_block.shape[1]
     cell_groups = lax.axis_size("cells")
@@ -56,9 +63,459 @@
     return (adjacency, connectivity)
 
 
+def encode(x):
+    x2 = x * x
+    return (x2 * x2 * x).astype(jnp.bfloat16)
+
+
+def decode(y):
+    y = y.astype(jnp.float32)
+    root = jnp.exp2(jnp.log2(jnp.abs(y)) * 0.2)
+    return jnp.where(y < 0, -root, root)
+
+
+def block_tiles(p, odd):
+    t = p.shape[0] // 2
+    tiles = [[p[i * t : i * t + t, c * t : c * t + t] for c in range(2)] for i in range(2)]
+    return [
+        [jnp.where(odd == 0, tiles[i][i ^ b], tiles[i][1 - (i ^ b)]) for i in range(2)]
+        for b in range(2)
+    ]
+
+
+def centred(p, sx, sy, rst, cst, cells, total):
+    mc, sc = cst[0:1], cst[1:2]
+    row_side = rst.T
+    mr, sr = row_side[:, 0:1], row_side[:, 1:2]
+    p = p - sx[:, 0:1] * mc - mr * (sy[0:1] - cells * mc)
+    return p * (sr * (1.0 / total)) * sc
+
+
+def plain(left, right):
+    return jnp.dot(left, right, preferred_element_type=jnp.float32)
+
+
+def against_rows(left, right):
+    return lax.dot_general(
+        left, right, (((1,), (1,)), ((), ())), preferred_element_type=jnp.float32
+    )
+
+
+def put_tiles(p, s_ref, jj, blk, own_ref, sends):
+    tiles = block_tiles(p, s_ref[0] % 2)
+    for b in range(2):
+        for i in range(2):
+
+            @pl.when(jj == 0)
+            def _():
+                if b == 0:
+                    own_ref[blk, i] = tiles[b][i]
+                else:
+                    sends[0][blk, i] = encode(tiles[b][i])
+
+            @pl.when(jj == 1)
+            def _():
+                sends[1 + b][blk, i] = encode(tiles[b][i])
+
+
+def local_products(x, y0, y1):
+    n = y0.shape[0]
+    right = jnp.ones((x.shape[1], 128), jnp.bfloat16)
+    left = jnp.ones((8, n), jnp.bfloat16)
+    p = plain(x[:, :n], y0) + plain(x[:, n:], y1)
+    return p, plain(x, right), plain(left, y0) + plain(left, y1)
+
+
+def diagonal_body(s_ref, xa, xb, y0, y1, rst, cst, own_ref, o1, o2, o3, acc, sxa, sya, *, total):
+    jj, s = pl.program_id(0), pl.program_id(1)
+    n_s = pl.num_programs(1)
+    x = jnp.where(s == 0, xa[...], xb[...])
+    p, sx, sy = local_products(x, y0[...], y1[...])
+
+    @pl.when(s == 0)
+    def _():
+        acc[...] = p
+        sxa[...] = sx
+        sya[...] = sy
+
+    @pl.when(s > 0)
+    def _():
+        acc[...] += p
+        sxa[...] += sx
+        sya[...] += sy
+
+    @pl.when(s == n_s - 1)
+    def _():
+        cells = 4.0 * y0.shape[0]
+        p = centred(acc[...], sxa[...], sya[...], rst[0], cst[0], cells, total)
+        put_tiles(p, s_ref, jj, 0, own_ref, (o1, o2, o3))
+
+
+def near_body(s_ref, xa, xb, y0, y1, rst, cst, own_ref, o1, o2, o3, *, total):
+    blk, jj = pl.program_id(0), pl.program_id(1)
+    x = jnp.where(blk == 0, xa[...], xb[...])
+    p, sx, sy = local_products(x, y0[...], y1[...])
+    p = centred(p, sx, sy, rst[0], cst[0], 2.0 * y0.shape[0], total)
+    put_tiles(p, s_ref, jj, blk, own_ref, (o1, o2, o3))
+
+
+def far_body(s_ref, xa, xb, y0, y1, na, nb, rst, cst, own_ref, o1, o2, o3, acc, sya, *, total):
+    blk, jj = pl.program_id(0), pl.program_id(1)
+    x = jnp.where(s_ref[2] == 0, xa[...], xb[...])
+    n = y0.shape[0]
+    left = jnp.ones((8, 2 * n), jnp.bfloat16)
+    right = jnp.ones((2 * n, 128), jnp.bfloat16)
+    sx = plain(x, right)
+
+    @pl.when(blk == 0)
+    def _():
+        acc[...] = plain(x[:, :n], y0[...]) + plain(x[:, n:], y1[...])
+        sya[...] = plain(left[:, :n], y0[...]) + plain(left[:, n:], y1[...])
+
+    other = (s_ref[0] // 2) ^ jj
+
+    @pl.when((blk == 1) & (other == 0))
+    def _():
+        acc[...] = against_rows(x, na[...])
+        sya[...] = against_rows(left, na[...])
+
+    @pl.when((blk == 1) & (other == 1))
+    def _():
+        acc[...] = against_rows(x[:, :n], nb[:, n:]) + against_rows(x[:, n:], nb[:, :n])
+        sya[...] = against_rows(left, nb[...])
+
+    p = centred(acc[...], sx, sya[...], rst[0], cst[0], 2.0 * n, total)
+    put_tiles(p, s_ref, jj, blk, own_ref, (o1, o2, o3))
+
+
+def turn_body(s_ref, own, r1, r2, r3, *outs, turns, keeps):
+    odd = s_ref[0] % 2
+    t_ref, rest = outs[0], outs[1:]
+    for n in range(own.shape[0]):
+        for i in range(2):
+            v = own[n, i] + decode(r1[n, i]) + decode(r2[n, i]) + decode(r3[n, i])
+            t_ref[n, i] = v
+            if keeps[n] is not None:
+                rest[keeps[n]][i] = encode(v)
+            if turns[n] is not None:
+                w = encode(v.T)
+                dst = rest[turns[n]]
+
+                @pl.when(odd == 0)
+                def _():
+                    dst[i] = w
+
+                @pl.when(odd == 1)
+                def _():
+                    dst[1 - i] = w
+
+
+def power(v):
+    v2 = v * v
+    return v2 * v2 * v2
+
+
+def put_slot(outs, where, i, value):
+    for j, o in enumerate(outs):
+
+        @pl.when(where == j)
+        def _():
+            o[i] = value
+
+
+def early_body(s_ref, t0, t1, ru, rd, *outs):
+    k, g = s_ref[0], s_ref[2]
+    n = t0.shape[-1]
+    for i in range(2):
+        own = power(t0[0, i])
+        same = lax.broadcasted_iota(jnp.int32, (n, n), 0) == lax.broadcasted_iota(
+            jnp.int32, (n, n), 1
+        )
+        own = jnp.where(same & (k == 0), 0.0, own).astype(jnp.bfloat16)
+        put_slot(outs, g ^ k, i, own)
+        low = power(t1[0, i] + decode(ru[i])).astype(jnp.bfloat16)
+        put_slot(outs, jnp.where(g > 0, (g - 1) ^ k, -1), i, low)
+        high = power(t1[1, i] + decode(rd[i])).astype(jnp.bfloat16)
+        put_slot(outs, jnp.where(g < s_ref[3] - 1, (g + 1) ^ k, -1), i, high)
+
+
+def late_body(s_ref, t2, r2, rf, rn, *outs):
+    k, g = s_ref[0], s_ref[2]
+    outer = (g == 0) | (g == s_ref[3] - 1)
+    for i in range(2):
+        two = power(t2[0, i] + decode(r2[i])).astype(jnp.bfloat16)
+        put_slot(outs, g ^ 2 ^ k, i, two)
+        three = power(decode(rf[i]) + decode(rn[i])).astype(jnp.bfloat16)
+        put_slot(outs, jnp.where(outer, g ^ 3 ^ k, -1), i, three)
+
+
+def place_body(s_ref, e0, e1, e2, e3, l0, l1, l2, l3, out_ref, sum_ref):
+    x = s_ref[0]
+    is_early = s_ref[1]
+    early, late = (e0, e1, e2, e3), (l0, l1, l2, l3)
+    t = e0.shape[-1]
+
+    def place(tiles):
+        for i in range(2):
+            total = jnp.zeros((t, 1), jnp.float32)
+            for c in range(4):
+                v = tiles[c ^ i][i]
+                for m in range(1, 4):
+                    v = jnp.where(x == m, tiles[c ^ i ^ m][i], v)
+                v = v.astype(jnp.float32)
+                out_ref[i * t : i * t + t, c * t : c * t + t] = v
+                total = total + jnp.sum(v, axis=1, keepdims=True)
+            sum_ref[i * t : i * t + t, :] = total
+
+    @pl.when(is_early == 1)
+    def _():
+        place(early)
+
+    @pl.when(is_early == 0)
+    def _():
+        place(late)
+
+
+def pay_body(s_ref, a, b, out_a, out_b):
+    n = a.shape[0]
+    for s, out in enumerate((out_a, out_b)):
+
+        @pl.when(pl.program_id(0) == s)
+        def _():
+            out[:, :n] = a[...].T
+            out[:, n:] = b[...].T
+
+
+def whole():
+    return pl.BlockSpec(memory_space=pltpu.VMEM)
+
+
+def scalars():
+    return pl.BlockSpec(memory_space=pltpu.SMEM)
+
+
+def folded_shards(counts, library):
+    rows, width = counts.shape
+    n_cells = lax.axis_size("cells")
+    n_genes = lax.axis_size("genes")
+    cores = n_cells // n_genes
+    total = float(rows * n_cells)
+    half_cells = rows // 2
+    half = width // cores
+    tile = half // 2
+    g = lax.axis_index("genes")
+    c = lax.axis_index("cells")
+    k, h = c // cores, c % cores
+
+    def perm(f):
+        pairs = []
+        for ci in range(n_cells):
+            for gi in range(n_genes):
+                d = f(ci // cores, ci % cores, gi)
+                if d is not None and 0 <= d[2] < n_genes:
+                    pairs.append((ci * n_genes + gi, (d[0] * cores + d[1]) * n_genes + d[2]))
+        return pairs
+
+    def send(x, f):
+        return lax.ppermute(x, AXES, perm(f))
+
+    flip = lambda k, h, g: (k, h ^ 1, g)
+    bf16, f32 = jnp.bfloat16, jnp.float32
+    shape = jax.ShapeDtypeStruct
+
+    own = normalize(counts, library)
+    oth = send(own, flip)
+    where = jnp.stack([k, h, g, jnp.int32(n_genes)]).astype(jnp.int32)
+    pay_a, pay_b = pl.pallas_call(
+        pay_body,
+        grid_spec=pltpu.PrefetchScalarGridSpec(
+            num_scalar_prefetch=1,
+            grid=(2,),
+            in_specs=[pl.BlockSpec((half_cells, half), lambda s, sc: (s, sc[1]))] * 2,
+            out_specs=[pl.BlockSpec((half, 2 * half_cells), lambda s, sc: (0, 0))] * 2,
+        ),
+        out_shape=[shape((half, 2 * half_cells), bf16)] * 2,
+        name="turn_payload",
+    )(where, own, oth)
+    up1 = send(pay_a, lambda k, h, g: (k, h, g + 1))
+    dn1 = send(pay_b, lambda k, h, g: (k, h, g - 1))
+    end = jnp.where(g == 0, pay_b, pay_a)
+    last = n_genes - 1
+    near = send(
+        end, lambda k, h, g: (k, h, 1) if g == 0 else ((k, h, g - 1) if g == last else None)
+    )
+    widened = own.astype(f32)
+    local = jnp.stack([jnp.sum(widened, axis=0), jnp.sum(widened * widened, axis=0)])
+    sums = lax.psum(local, "cells")
+    means = sums[0] / total
+    variances = sums[1] / total - means * means
+    mine = jnp.stack([means, lax.rsqrt(variances + 1e-05)])
+    afar = [send(mine, lambda k, h, g, d=d: (k, h, g ^ d)) for d in (1, 2, 3)]
+    widen = ((0, 0), (0, 6), (0, 0))
+    own_stats = jnp.pad(mine[None], widen)
+    stats = jnp.pad(jnp.stack([mine] + afar), widen)
+
+    def block_outs(n, m):
+        spec = pl.BlockSpec((n, 2, tile, tile), m)
+        return [spec] * 4
+
+    def out_shapes(n):
+        return [shape((n, 2, tile, tile), f32)] + [shape((n, 2, tile, tile), bf16)] * 3
+
+    col = lambda jj, sc: sc[1] ^ (sc[0] // 2) ^ jj
+    y_spec = pl.BlockSpec((half_cells, half), lambda jj, s, sc: (s, col(jj, sc)))
+    w0 = pl.pallas_call(
+        functools.partial(diagonal_body, total=total),
+        grid_spec=pltpu.PrefetchScalarGridSpec(
+            num_scalar_prefetch=1,
+            grid=(2, 2),
+            in_specs=[
+                pl.BlockSpec((half, 2 * half_cells), lambda jj, s, sc: (0, 0)),
+                pl.BlockSpec((half, 2 * half_cells), lambda jj, s, sc: (0, 0)),
+                y_spec,
+                y_spec,
+                pl.BlockSpec((1, 8, half), lambda jj, s, sc: (0, 0, sc[1])),
+                pl.BlockSpec((1, 8, half), lambda jj, s, sc: (0, 0, col(jj, sc))),
+            ],
+            out_specs=block_outs(1, lambda jj, s, sc: (0, 0, 0, 0)),
+            scratch_shapes=[
+                pltpu.VMEM((half, half), f32),
+                pltpu.VMEM((half, 128), f32),
+                pltpu.VMEM((8, half), f32),
+            ],
+        ),
+        out_shape=out_shapes(1),
+        name="diagonal_block",
+    )(where, pay_a, pay_b, own, oth, own_stats, own_stats)
+
+    up2 = send(up1, lambda k, h, g: (k, h, g + 1) if g > 0 else None)
+    dn2 = send(dn1, lambda k, h, g: (k, h, g - 1) if g < last else None)
+    near_other = send(near, flip)
+
+    x_spec = pl.BlockSpec((half, 2 * half_cells), lambda b, jj, sc: (0, 0))
+    lower = jnp.where(g > 0, g ^ (g - 1), 0)
+    higher = jnp.where(g < last, g ^ (g + 1), 0)
+    scal1 = jnp.stack([k, h, lower, higher]).astype(jnp.int32)
+    y_spec = pl.BlockSpec((half_cells, half), lambda b, jj, sc: (b, col(jj, sc)))
+    w1 = pl.pallas_call(
+        functools.partial(near_body, total=total),
+        grid_spec=pltpu.PrefetchScalarGridSpec(
+            num_scalar_prefetch=1,
+            grid=(2, 2),
+            in_specs=[
+                x_spec,
+                x_spec,
+                y_spec,
+                y_spec,
+                pl.BlockSpec((1, 8, half), lambda b, jj, sc: (sc[2 + b], 0, sc[1])),
+                pl.BlockSpec((1, 8, half), lambda b, jj, sc: (0, 0, col(jj, sc))),
+            ],
+            out_specs=block_outs(2, lambda b, jj, sc: (0, 0, 0, 0)),
+        ),
+        out_shape=out_shapes(2),
+        name="near_blocks",
+    )(scal1, up1, dn1, own, oth, stats, stats)
+
+    low_half = (g < n_genes // 2).astype(jnp.int32)
+    scal2 = jnp.stack([k, h, low_half, jnp.int32(0)]).astype(jnp.int32)
+    y_spec = pl.BlockSpec((half_cells, half), lambda b, jj, sc: (sc[2], col(jj, sc)))
+    w2 = pl.pallas_call(
+        functools.partial(far_body, total=total),
+        grid_spec=pltpu.PrefetchScalarGridSpec(
+            num_scalar_prefetch=1,
+            grid=(2, 2),
+            in_specs=[
+                x_spec,
+                x_spec,
+                y_spec,
+                y_spec,
+                x_spec,
+                x_spec,
+                pl.BlockSpec((1, 8, half), lambda b, jj, sc: (2, 0, sc[1])),
+                pl.BlockSpec((1, 8, half), lambda b, jj, sc: (b, 0, col(jj, sc))),
+            ],
+            out_specs=block_outs(2, lambda b, jj, sc: (0, 0, 0, 0)),
+            scratch_shapes=[pltpu.VMEM((half, half), f32), pltpu.VMEM((8, half), f32)],
+        ),
+        out_shape=out_shapes(2),
+        name="far_blocks",
+    )(scal2, up2, dn2, own, oth, near, near_other, stats, stats)
+
+    def reduce_tiles(w):
+        return [w[0]] + [send(w[j], lambda k, h, g, j=j: (k ^ j, h, g)) for j in (1, 2, 3)]
+
+    small = shape((2, tile, tile), bf16)
+
+    def turn(parts, turns, keeps):
+        n = parts[0].shape[0]
+        n_out = sum(v is not None for v in turns + keeps)
+        return pl.pallas_call(
+            functools.partial(turn_body, turns=turns, keeps=keeps),
+            in_specs=[scalars()] + [whole()] * 4,
+            out_specs=[whole()] * (1 + n_out),
+            out_shape=[shape((n, 2, tile, tile), f32)] + [small] * n_out,
+            name="sum_tiles",
+        )(where, *parts)
+
+    (t0,) = turn(reduce_tiles(w0), [None], [None])
+    t1, e_up, e_dn = turn(reduce_tiles(w1), [0, 1], [None, None])
+    t2, e_two, e_three, k_three = turn(reduce_tiles(w2), [0, 1], [None, 2])
+
+    side = lambda f: (lambda k, h, g: (k, h ^ (k // 2), f(g)) if f(g) is not None else None)
+    rd = send(e_up, side(lambda g: g - 1))
+    ru = send(e_dn, side(lambda g: g + 1))
+    r2 = send(e_two, side(lambda g: g ^ 2))
+    inner = lambda g: 0 < g < last
+    r3f = send(e_three, side(lambda g: (g ^ 2) if inner(g) else None))
+    r3n = send(k_three, lambda k, h, g: (k, h, g ^ 1) if inner(g) else None)
+
+    early = pl.pallas_call(
+        early_body,
+        in_specs=[scalars()] + [whole()] * 4,
+        out_specs=[whole()] * 4,
+        out_shape=[small] * 4,
+        name="early_tiles",
+    )(where, t0, t1, ru, rd)
+    late = pl.pallas_call(
+        late_body,
+        in_specs=[scalars()] + [whole()] * 4,
+        out_specs=[whole()] * 4,
+        out_shape=[small] * 4,
+        name="late_tiles",
+    )(where, t2, r2, r3f, r3n)
+
+    is_early = lambda q, g: -1 <= q - g <= 1
+    got_early, got_late = [early[0]], [late[0]]
+    for j in range(1, 4):
+        got_early.append(
+            send(early[j], lambda k, h, g, j=j: (k ^ j, h, g) if is_early(k ^ j, g) else None)
+        )
+        got_late.append(
+            send(late[j], lambda k, h, g, j=j: (k ^ j, h, g) if not is_early(k ^ j, g) else None)
+        )
+    scal3 = jnp.stack([(2 * h) ^ k, (jnp.abs(k - g) <= 1).astype(jnp.int32)]).astype(jnp.int32)
+    adjacency, row_sums = pl.pallas_call(
+        place_body,
+        in_specs=[scalars()] + [whole()] * 8,
+        out_specs=[whole()] * 2,
+        out_shape=[shape((half, width), f32), shape((half, 1), f32)],
+        name="place_tiles",
+    )(scal3, *got_early, *got_late)
+    part = row_sums[:, 0]
+    peers = [send(part, lambda k, h, g, d=d: (k, h, g ^ d)) for d in (1, 2, 3)]
+    connectivity = (part + peers[0]) + (peers[1] + peers[2])
+    return (adjacency, connectivity)
+
+
+def folded(counts, library):
+    return folded_shards(counts, library)
+
+
 def solution(mesh):
+    cells, genes = mesh.shape["cells"], mesh.shape["genes"]
+    folds = genes == 4 and cells == 2 * genes
     return jax.shard_map(
-        shards,
+        folded if folds else general_shards,
         mesh=mesh,
         in_specs=(P("cells", "genes"), P("cells")),
         out_specs=(P("cells", "genes"), P("cells")),

time: 318 us -> 204 us (0.64)
  waiting for transfers between devices: 226 us -> 46.4 us
  starting transfers between devices: 0.08 us -> 67.9 us
  Pallas kernels: 0 us -> 58.3 us
  blocking collectives: 52.7 us -> 13.4 us
  matrix products: 14.6 us -> 0 us
  between operations: 14.1 us -> 1.05 us
  local copies, waits for them, and re-layouts: 0.17 us -> 3.88 us
    all_gather x1 -> x0, waiting for transfers between devices: 152 us -> none  [shards(): full_block = lax.all_gather(own_block, 'genes', axis=1, tiled=True)]
    reduce_scatter x1 -> x0, waiting for transfers between devices: 73.9 us -> none  [shards(): lax.psum_scatter(cross_product(full_block, own_block), 'cells', scatter_d...]
    ppermute x0 -> x33, starting transfers between devices: none -> 67.9 us  [send(): return lax.ppermute(x, AXES, perm(f))]
    pallas_call x0 -> x10, Pallas kernels: none -> 58.3 us  [the longest x1 12.8 us: folded_shards(): pl.pallas_call(functools.partial(far_body, total=total), grid_spec=pltpu....]
    ppermute x0 -> x33, waiting for transfers between devices: none -> 46.4 us  [send(): return lax.ppermute(x, AXES, perm(f))]
    all_gather x2 -> x0, blocking collectives: 26.4 us -> none  [the longest x1 13.2 us: shards(): lax.all_gather(block_sums, 'genes', axis=0, tiled=True)]
    dot_general x1 -> x0, matrix products: 14.6 us -> none  [cross_product(): lax.dot_general(left, right, (((0,), (0,)), ((), ())), preferred_element_...]
    psum x2 -> x1, blocking collectives: 26.3 us -> 13.4 us  [folded_shards(): sums = lax.psum(local, 'cells')]
  transfers between devices with their start and end apart: 2 -> 33, of which waited for: 2 -> 11; matrix products, arithmetic and copies ran while one was open for 0% -> 3% of each run, Pallas kernels for 0% -> 25%
where the time goes in v1:
time: 204 us; the launch traced here: 203 us
  starting transfers between devices  67.9 us (33%)
  Pallas kernels  58.3 us (29%)
  waiting for transfers between devices  46.4 us (23%)
  blocking collectives  13.4 us (7%)
  other arithmetic  12.2 us (6%)
  local copies, waits for them, and re-layouts  3.88 us (2%)
    ppermute x33, starting transfers between devices, send(): return lax.ppermute(x, AXES, perm(f))  67.9 us
    ppermute x33, waiting for transfers between devices, send(): return lax.ppermute(x, AXES, perm(f))  46.4 us
    psum x1, blocking collectives, folded_shards(): sums = lax.psum(local, 'cells')  13.4 us
    pallas_call x1, Pallas kernels, folded_shards(): pl.pallas_call(functools.partial(far_body, total=total), grid_spec=pltpu....  12.8 us
    pallas_call x3, Pallas kernels, turn(): pl.pallas_call(functools.partial(turn_body, turns=turns, keeps=keeps), in...  11 us
    pallas_call x1, Pallas kernels, folded_shards(): pl.pallas_call(functools.partial(near_body, total=total), grid_spec=pltpu...  10.5 us
    pallas_call x1, Pallas kernels, folded_shards(): pl.pallas_call(functools.partial(diagonal_body, total=total), grid_spec=p...  10.2 us
    reduce_sum x1, other arithmetic, folded_shards(): jnp.sum(widened, axis=0)  4.25 us
  transfers between devices with their start and end apart: 33, of which 11 were waited for; matrix products, arithmetic and copies ran while one was open for 3% of the time, Pallas kernels for 25%

profile of v1, /device:TPU:0, one launch (start us, length us, event | category | flops | bytes accessed | tf_op | source)
XLA Modules:
  0.0 203.2 jit_solution(3695754417310463779)
XLA Ops:
  1.3 4.2 %convert_reduce_fusion = (f32[1024]{0:T(1024)S(1)}, f32[1024]{0:T(1024)S(1)}, bf16[1024,1024]{1,0:T(8,128)(2,1)S(1)}) fusion(f32[1024]{0:T(1024)S(1)} %convert_divide_fusion, s32[1024,1024]{1,0:T(8,128)} %param.2), kind=kLoop, calls=%fused_computation.1 | loop fusion | flops 7337984 | bytes 6303744 | tf_op jit(solution)/shard_map/reduce_sum | solution.py:348
  6.8 3.3 %collective-permute-done.b.y1 = bf16[1024,1024]{1,0:T(8,128)(2,1)} collective-permute-done((bf16[1024,1024]{1,0:T(8,128)(2,1)S(1)}, bf16[1024,1024]{1,0:T(8,128)(2,1)}, u32[]{:S(2)}, u32[]{:S(2)}) %collective-permute-start) | collective-permute-done | bytes 2097184 | tf_op jit(solution)/shard_map/ppermute | solution.py:320
  10.1 4.0 %turn_payload.1 = (bf16[512,1024]{1,0:T(8,128)(2,1)}, bf16[512,1024]{1,0:T(8,128)(2,1)}) custom-call(s32[4]{0:T(128)} %pad_add_fusion.1.s_ref, bf16[1024,1024]{1,0:T(8,128)(2,1)} %copy-done, bf16[1024,1024]{1,0:T(8,128)(2,1)} %collective-permute-done.b.y1), custom_call_target="tpu_custom_call" | custom-call | tf_op jit(solution)/shard_map/turn_payload/pallas_call | solution.py:329
  14.0 5.8 %collective-permute-start.4 = (bf16[512,1024]{1,0:T(8,128)(2,1)}, bf16[512,1024]{1,0:T(8,128)(2,1)}, u32[]{:S(2)}, u32[]{:S(2)}) collective-permute-start(bf16[512,1024]{1,0:T(8,128)(2,1)} %get-tuple-element.33.xa), channel_id=1, source_target_pairs={{0,1},{1,2},{2,3},{4,5},{5,6},{6,7},{8,9},{9,10},{10,11},{12,13},{... | collective-permute-start | bytes 3145736 | tf_op jit(solution)/shard_map/ppermute | solution.py:320
  23.4 4.6 %collective-permute-start.19 = (bf16[512,1024]{1,0:T(8,128)(2,1)}, bf16[512,1024]{1,0:T(8,128)(2,1)S(1)}, u32[]{:S(2)}, u32[]{:S(2)}) collective-permute-start(bf16[512,1024]{1,0:T(8,128)(2,1)} %broadcast_select_fusion), channel_id=1, source_target_pairs={{0,1},{3,2},{4,5},{7,6},{8,9},{11,10},{12,13},{15,14},{16,17},{19,... | collective-permute-start | bytes 3145736 | tf_op jit(solution)/shard_map/ppermute | solution.py:320
  28.1 13.4 %psum.7 = f32[2,1024]{1,0:T(2,128)S(1)} all-reduce(f32[2,1024]{1,0:T(2,128)S(1)} %pad_maximum_fusion), channel_id=1, replica_groups=mesh['cells'=8,'genes'=4] {'cells'}, use_global_device_ids=true, to_apply=%region_2.3 | all-reduce | flops 2048 | bytes 16384 | tf_op jit(solution)/shard_map/psum | solution.py:349
  43.4 3.5 %collective-permute-done.5.xb = bf16[512,1024]{1,0:T(8,128)(2,1)} collective-permute-done((bf16[512,1024]{1,0:T(8,128)(2,1)}, bf16[512,1024]{1,0:T(8,128)(2,1)}, u32[]{:S(2)}, u32[]{:S(2)}) %collective-permute-start.5) | collective-permute-done | bytes 1048608 | tf_op jit(solution)/shard_map/ppermute | solution.py:320
  48.2 16.1 %collective-permute-done.19.na = bf16[512,1024]{1,0:T(8,128)(2,1)S(1)} collective-permute-done((bf16[512,1024]{1,0:T(8,128)(2,1)}, bf16[512,1024]{1,0:T(8,128)(2,1)S(1)}, u32[]{:S(2)}, u32[]{:S(2)}) %collective-permute-start.19) | collective-permute-done | bytes 1048608 | tf_op jit(solution)/shard_map/ppermute | solution.py:320
  64.4 5.8 %collective-permute-start.8 = (f32[2,1024]{1,0:T(2,128)S(1)}, f32[2,1024]{1,0:T(2,128)S(1)}, u32[]{:S(2)}, u32[]{:S(2)}) collective-permute-start(f32[2,1024]{1,0:T(2,128)S(1)} %get-tuple-element.67), channel_id=1, source_target_pairs={{0,3},{1,2},{2,1},{3,0},{4,7},{5,6},{6,5},{7,4},{8,11},{9,10},{10,... | collective-permute-start | bytes 24584 | tf_op jit(solution)/shard_map/ppermute | solution.py:320
  76.7 10.5 %near_blocks.1 = (f32[2,2,256,256]{3,2,1,0:T(8,128)}, bf16[2,2,256,256]{3,2,1,0:T(8,128)(2,1)}, bf16[2,2,256,256]{3,2,1,0:T(8,128)(2,1)}, bf16[2,2,256,256]{3,2,1,0:T(8,128)(2,1)}) custom-call(s32[4]{0:T(128)} %pad_add_fusion.3.s_ref, bf16[512,1024]{1,0:T(8,128)(2,1)} %collective-permute-done.4.xa, bf16[512,1024]{1,0:T(8,128)(2,1)} %collective-permute-done.5.xb, ...), custom_call_target="tpu_custom_call" | custom-call | tf_op jit(solution)/shard_map/near_blocks/pallas_call | solution.py:400
  92.3 12.8 %far_blocks.1 = (f32[2,2,256,256]{3,2,1,0:T(8,128)}, bf16[2,2,256,256]{3,2,1,0:T(8,128)(2,1)}, bf16[2,2,256,256]{3,2,1,0:T(8,128)(2,1)}, bf16[2,2,256,256]{3,2,1,0:T(8,128)(2,1)}) custom-call(s32[4]{0:T(128)} %pad_add_fusion.4.s_ref, bf16[512,1024]{1,0:T(8,128)(2,1)} %copy-done.2, bf16[512,1024]{1,0:T(8,128)(2,1)} %copy-done.3, bf16[1024,1024]{1,0:T(8,128)(2,1)} %copy-done, ...), custom_call_target="tpu_custom_call" | custom-call | tf_op jit(solution)/shard_map/far_blocks/pallas_call | solution.py:422
  109.2 10.2 %diagonal_block.1 = (f32[1,2,256,256]{3,2,1,0:T(8,128)}, bf16[1,2,256,256]{3,2,1,0:T(8,128)(2,1)}, bf16[1,2,256,256]{3,2,1,0:T(8,128)(2,1)}, bf16[1,2,256,256]{3,2,1,0:T(8,128)(2,1)}) custom-call(s32[4]{0:T(128)} %pad_add_fusion.1.s_ref, bf16[512,1024]{1,0:T(8,128)(2,1)} %get-tuple-element.33.xa, bf16[512,1024]{1,0:T(8,128)(2,1)} %get-tuple-element.34.xb, ...), custom_call_target="tpu_custom_call" | custom-call | tf_op jit(solution)/shard_map/diagonal_block/pallas_call | solution.py:367
  122.4 4.2 %sum_tiles.4 = (f32[2,2,256,256]{3,2,1,0:T(8,128)}, bf16[2,256,256]{2,1,0:T(8,128)(2,1)}, bf16[2,256,256]{2,1,0:T(8,128)(2,1)}) custom-call(s32[4]{0:T(128)} %pad_add_fusion.1.s_ref, f32[2,2,256,256]{3,2,1,0:T(8,128)} %get-tuple-element.39.own, bf16[2,2,256,256]{3,2,1,0:T(8,128)(2,1)} %collective-permute-done.9.r1, ...), custom_call_target="tpu_custom_call" | custom-call | tf_op jit(solution)/shard_map/sum_tiles/pallas_call | solution.py:452
  127.3 8.8 %collective-permute-done.22.r2 = bf16[2,2,256,256]{3,2,1,0:T(8,128)(2,1)S(1)} collective-permute-done((bf16[2,2,256,256]{3,2,1,0:T(8,128)(2,1)}, bf16[2,2,256,256]{3,2,1,0:T(8,128)(2,1)S(1)}, u32[]{:S(2)}, u32[]{:S(2)}) %collective-permute-start.22) | collective-permute-done | bytes 524320 | tf_op jit(solution)/shard_map/ppermute | solution.py:320
  136.1 4.0 %collective-permute-start.12 = (bf16[2,256,256]{2,1,0:T(8,128)(2,1)}, bf16[2,256,256]{2,1,0:T(8,128)(2,1)S(1)}, u32[]{:S(2)}, u32[]{:S(2)}) collective-permute-start(bf16[2,256,256]{2,1,0:T(8,128)(2,1)} %get-tuple-element.44), channel_id=1, source_target_pairs={{0,1},{1,2},{2,3},{4,5},{5,6},{6,7},{8,9},{9,10},{10,11},{12,13},{... | collective-permute-start | bytes 786440 | tf_op jit(solution)/shard_map/ppermute | solution.py:320
  141.4 4.2 %sum_tiles.5 = (f32[2,2,256,256]{3,2,1,0:T(8,128)}, bf16[2,256,256]{2,1,0:T(8,128)(2,1)}, bf16[2,256,256]{2,1,0:T(8,128)(2,1)}, bf16[2,256,256]{2,1,0:T(8,128)(2,1)}) custom-call(s32[4]{0:T(128)} %pad_add_fusion.1.s_ref, f32[2,2,256,256]{3,2,1,0:T(8,128)} %get-tuple-element.50.own, bf16[2,2,256,256]{3,2,1,0:T(8,128)(2,1)} %copy-done.4, ...), custom_call_target="tpu_custom_call" | custom-call | tf_op jit(solution)/shard_map/sum_tiles/pallas_call | solution.py:452
  145.7 3.0 %collective-permute-start.24 = (bf16[2,256,256]{2,1,0:T(8,128)(2,1)}, bf16[2,256,256]{2,1,0:T(8,128)(2,1)S(1)}, u32[]{:S(2)}, u32[]{:S(2)}) collective-permute-start(bf16[2,256,256]{2,1,0:T(8,128)(2,1)} %get-tuple-element.55), channel_id=1, source_target_pairs={{0,2},{1,3},{2,0},{3,1},{4,6},{5,7},{6,4},{7,5},{8,10},{9,11},{10,... | collective-permute-start | bytes 786440 | tf_op jit(solution)/shard_map/ppermute | solution.py:320
  154.7 3.2 %early_tiles.1 = (bf16[2,256,256]{2,1,0:T(8,128)(2,1)}, bf16[2,256,256]{2,1,0:T(8,128)(2,1)}, bf16[2,256,256]{2,1,0:T(8,128)(2,1)}, bf16[2,256,256]{2,1,0:T(8,128)(2,1)}) custom-call(s32[4]{0:T(128)} %pad_add_fusion.1.s_ref, f32[1,2,256,256]{3,2,1,0:T(8,128)} %sum_tiles.3.t0, f32[2,2,256,256]{3,2,1,0:T(8,128)} %get-tuple-element.43.t1, ...), custom_call_target="tpu_custom_call" | custom-call | tf_op jit(solution)/shard_map/early_tiles/pallas_call | solution.py:472
  162.5 2.7 %collective-permute-done.26.rn = bf16[2,256,256]{2,1,0:T(8,128)(2,1)S(1)} collective-permute-done((bf16[2,256,256]{2,1,0:T(8,128)(2,1)}, bf16[2,256,256]{2,1,0:T(8,128)(2,1)S(1)}, u32[]{:S(2)}, u32[]{:S(2)}) %collective-permute-start.26) | collective-permute-done | bytes 262176 | tf_op jit(solution)/shard_map/ppermute | solution.py:320
  165.9 3.2 %late_tiles.1 = (bf16[2,256,256]{2,1,0:T(8,128)(2,1)}, bf16[2,256,256]{2,1,0:T(8,128)(2,1)}, bf16[2,256,256]{2,1,0:T(8,128)(2,1)}, bf16[2,256,256]{2,1,0:T(8,128)(2,1)}) custom-call(s32[4]{0:T(128)} %pad_add_fusion.1.s_ref, f32[2,2,256,256]{3,2,1,0:T(8,128)} %get-tuple-element.54.t2, bf16[2,256,256]{2,1,0:T(8,128)(2,1)} %copy-done.16, ...), custom_call_target="tpu_custom_call" | custom-call | tf_op jit(solution)/shard_map/late_tiles/pallas_call | solution.py:479
  169.8 11.4 %collective-permute-start.28 = (bf16[2,256,256]{2,1,0:T(8,128)(2,1)}, bf16[2,256,256]{2,1,0:T(8,128)(2,1)S(1)}, u32[]{:S(2)}, u32[]{:S(2)}) collective-permute-start(bf16[2,256,256]{2,1,0:T(8,128)(2,1)} %get-tuple-element.60), channel_id=1, source_target_pairs={{0,16},{4,20},{8,24},{9,25},{12,28},{13,29},{18,2},{19,3},{22,6},{... | collective-permute-start | bytes 786440 | tf_op jit(solution)/shard_map/ppermute | solution.py:320
  181.2 2.7 %collective-permute-start.29 = (bf16[2,256,256]{2,1,0:T(8,128)(2,1)}, bf16[2,256,256]{2,1,0:T(8,128)(2,1)S(1)}, u32[]{:S(2)}, u32[]{:S(2)}) collective-permute-start(bf16[2,256,256]{2,1,0:T(8,128)(2,1)} %get-tuple-element.61), channel_id=1, source_target_pairs={{0,24},{1,25},{4,28},{5,29},{8,16},{12,20},{19,11},{23,15},{26,2},... | collective-permute-start | bytes 786440 | tf_op jit(solution)/shard_map/ppermute | solution.py:320
  184.7 7.1 %collective-permute-done.28.l2 = bf16[2,256,256]{2,1,0:T(8,128)(2,1)S(1)} collective-permute-done((bf16[2,256,256]{2,1,0:T(8,128)(2,1)}, bf16[2,256,256]{2,1,0:T(8,128)(2,1)S(1)}, u32[]{:S(2)}, u32[]{:S(2)}) %collective-permute-start.28) | collective-permute-done | bytes 262176 | tf_op jit(solution)/shard_map/ppermute | solution.py:320
  192.6 3.4 %place_tiles.1 = (f32[512,1024]{1,0:T(8,128)}, f32[512,1]{1,0:T(8,128)}) custom-call(s32[2]{0:T(128)} %pad_add_fusion.s_ref, bf16[2,256,256]{2,1,0:T(8,128)(2,1)} %get-tuple-element.46.e0, bf16[2,256,256]{2,1,0:T(8,128)(2,1)} %copy-done.7, bf16[2,256,256]{2,1,0:T(8,128)(2,1)} %copy-done.8, bf16[2,256,256]{2,1,0:T(8,128)(2,1)} %copy-done.9, ...), custom_call_target="tpu_custom_call" | custom-call | tf_op jit(solution)/shard_map/place_tiles/pallas_call | solution.py:497
  (109 shorter events, 49.9 us)
Async XLA Ops:
  14.0 28.7 %collective-permute-start.4 = (bf16[512,1024]{1,0:T(8,128)(2,1)}, bf16[512,1024]{1,0:T(8,128)(2,1)}, u32[]{:S(2)}, u32[]{:S(2)}) collective-permute-start(bf16[512,1024]{1,0:T(8,128)(2,1)} %get-tuple-element.33.xa), channel_id=1, source_target_pairs={{0,1},{1,2},{2,3},{4,5},{5,6},{6,7},{8,9},{9,10},{10,11},{12,13},{... | collective-permute-start | bytes 3145736 | tf_op jit(solution)/shard_map/ppermute | solution.py:320
  19.8 27.1 %collective-permute-start.5 = (bf16[512,1024]{1,0:T(8,128)(2,1)}, bf16[512,1024]{1,0:T(8,128)(2,1)}, u32[]{:S(2)}, u32[]{:S(2)}) collective-permute-start(bf16[512,1024]{1,0:T(8,128)(2,1)} %get-tuple-element.34.xb), channel_id=1, source_target_pairs={{1,0},{2,1},{3,2},{5,4},{6,5},{7,6},{9,8},{10,9},{11,10},{13,12},{... | collective-permute-start | bytes 3145736 | tf_op jit(solution)/shard_map/ppermute | solution.py:320
  23.4 40.9 %collective-permute-start.19 = (bf16[512,1024]{1,0:T(8,128)(2,1)}, bf16[512,1024]{1,0:T(8,128)(2,1)S(1)}, u32[]{:S(2)}, u32[]{:S(2)}) collective-permute-start(bf16[512,1024]{1,0:T(8,128)(2,1)} %broadcast_select_fusion), channel_id=1, source_target_pairs={{0,1},{3,2},{4,5},{7,6},{8,9},{11,10},{12,13},{15,14},{16,17},{19,... | collective-permute-start | bytes 3145736 | tf_op jit(solution)/shard_map/ppermute | solution.py:320
  42.7 48.1 %collective-permute-start.17 = (bf16[512,1024]{1,0:T(8,128)(2,1)}, bf16[512,1024]{1,0:T(8,128)(2,1)S(1)}, u32[]{:S(2)}, u32[]{:S(2)}) collective-permute-start(bf16[512,1024]{1,0:T(8,128)(2,1)} %collective-permute-done.4.xa), channel_id=1, source_target_pairs={{1,2},{2,3},{5,6},{6,7},{9,10},{10,11},{13,14},{14,15},{17,18},{18... | collective-permute-start | bytes 3145736 | tf_op jit(solution)/shard_map/ppermute | solution.py:320
  46.9 44.4 %collective-permute-start.18 = (bf16[512,1024]{1,0:T(8,128)(2,1)}, bf16[512,1024]{1,0:T(8,128)(2,1)S(1)}, u32[]{:S(2)}, u32[]{:S(2)}) collective-permute-start(bf16[512,1024]{1,0:T(8,128)(2,1)} %collective-permute-done.5.xb), channel_id=1, source_target_pairs={{1,0},{2,1},{5,4},{6,5},{9,8},{10,9},{13,12},{14,13},{17,16},{18,1... | collective-permute-start | bytes 3145736 | tf_op jit(solution)/shard_map/ppermute | solution.py:320
  64.4 27.0 %collective-permute-start.20 = (bf16[512,1024]{1,0:T(8,128)(2,1)S(1)}, bf16[512,1024]{1,0:T(8,128)(2,1)}, u32[]{:S(2)}, u32[]{:S(2)}) collective-permute-start(bf16[512,1024]{1,0:T(8,128)(2,1)S(1)} %collective-permute-done.19.na), channel_id=1, source_target_pairs={{0,4},{1,5},{2,6},{3,7},{4,0},{5,1},{6,2},{7,3},{8,12},{9,13},{10,... | collective-permute-start | bytes 3145736 | tf_op jit(solution)/shard_map/ppermute | solution.py:320
  87.2 20.9 %collective-permute-start.9 = (bf16[2,2,256,256]{3,2,1,0:T(8,128)(2,1)}, bf16[2,2,256,256]{3,2,1,0:T(8,128)(2,1)}, u32[]{:S(2)}, u32[]{:S(2)}) collective-permute-start(bf16[2,2,256,256]{3,2,1,0:T(8,128)(2,1)} %get-tuple-element.40), channel_id=1, source_target_pairs={{0,8},{1,9},{2,10},{3,11},{4,12},{5,13},{6,14},{7,15},{8,0},{9,1},... | collective-permute-start | bytes 1572872 | tf_op jit(solution)/shard_map/ppermute | solution.py:320
  89.3 30.2 %collective-permute-start.10 = (bf16[2,2,256,256]{3,2,1,0:T(8,128)(2,1)}, bf16[2,2,256,256]{3,2,1,0:T(8,128)(2,1)}, u32[]{:S(2)}, u32[]{:S(2)}) collective-permute-start(bf16[2,2,256,256]{3,2,1,0:T(8,128)(2,1)} %get-tuple-element.41), channel_id=1, source_target_pairs={{0,16},{1,17},{2,18},{3,19},{4,20},{5,21},{6,22},{7,23},{8,24},{9,... | collective-permute-start | bytes 1572872 | tf_op jit(solution)/shard_map/ppermute | solution.py:320
  90.8 30.2 %collective-permute-start.11 = (bf16[2,2,256,256]{3,2,1,0:T(8,128)(2,1)}, bf16[2,2,256,256]{3,2,1,0:T(8,128)(2,1)}, u32[]{:S(2)}, u32[]{:S(2)}) collective-permute-start(bf16[2,2,256,256]{3,2,1,0:T(8,128)(2,1)} %get-tuple-element.42), channel_id=1, source_target_pairs={{0,24},{1,25},{2,26},{3,27},{4,28},{5,29},{6,30},{7,31},{8,16},{9,... | collective-permute-start | bytes 1572872 | tf_op jit(solution)/shard_map/ppermute | solution.py:320
  105.1 21.5 %collective-permute-start.21 = (bf16[2,2,256,256]{3,2,1,0:T(8,128)(2,1)}, bf16[2,2,256,256]{3,2,1,0:T(8,128)(2,1)S(1)}, u32[]{:S(2)}, u32[]{:S(2)}) collective-permute-start(bf16[2,2,256,256]{3,2,1,0:T(8,128)(2,1)} %get-tuple-element.51), channel_id=1, source_target_pairs={{0,8},{1,9},{2,10},{3,11},{4,12},{5,13},{6,14},{7,15},{8,0},{9,1},... | collective-permute-start | bytes 1572872 | tf_op jit(solution)/shard_map/ppermute | solution.py:320
  106.6 29.5 %collective-permute-start.22 = (bf16[2,2,256,256]{3,2,1,0:T(8,128)(2,1)}, bf16[2,2,256,256]{3,2,1,0:T(8,128)(2,1)S(1)}, u32[]{:S(2)}, u32[]{:S(2)}) collective-permute-start(bf16[2,2,256,256]{3,2,1,0:T(8,128)(2,1)} %get-tuple-element.52), channel_id=1, source_target_pairs={{0,16},{1,17},{2,18},{3,19},{4,20},{5,21},{6,22},{7,23},{8,24},{9,... | collective-permute-start | bytes 1572872 | tf_op jit(solution)/shard_map/ppermute | solution.py:320
  108.1 32.0 %collective-permute-start.23 = (bf16[2,2,256,256]{3,2,1,0:T(8,128)(2,1)}, bf16[2,2,256,256]{3,2,1,0:T(8,128)(2,1)S(1)}, u32[]{:S(2)}, u32[]{:S(2)}) collective-permute-start(bf16[2,2,256,256]{3,2,1,0:T(8,128)(2,1)} %get-tuple-element.53), channel_id=1, source_target_pairs={{0,24},{1,25},{2,26},{3,27},{4,28},{5,29},{6,30},{7,31},{8,16},{9,... | collective-permute-start | bytes 1572872 | tf_op jit(solution)/shard_map/ppermute | solution.py:320
  119.5 26.2 %collective-permute-start.1 = (bf16[1,2,256,256]{3,2,1,0:T(8,128)(2,1)}, bf16[1,2,256,256]{3,2,1,0:T(8,128)(2,1)S(1)}, u32[]{:S(2)}, u32[]{:S(2)}) collective-permute-start(bf16[1,2,256,256]{3,2,1,0:T(8,128)(2,1)} %get-tuple-element.36), channel_id=1, source_target_pairs={{0,8},{1,9},{2,10},{3,11},{4,12},{5,13},{6,14},{7,15},{8,0},{9,1},... | collective-permute-start | bytes 786440 | tf_op jit(solution)/shard_map/ppermute | solution.py:320
  121.0 27.7 %collective-permute-start.2 = (bf16[1,2,256,256]{3,2,1,0:T(8,128)(2,1)}, bf16[1,2,256,256]{3,2,1,0:T(8,128)(2,1)S(1)}, u32[]{:S(2)}, u32[]{:S(2)}) collective-permute-start(bf16[1,2,256,256]{3,2,1,0:T(8,128)(2,1)} %get-tuple-element.37), channel_id=1, source_target_pairs={{0,16},{1,17},{2,18},{3,19},{4,20},{5,21},{6,22},{7,23},{8,24},{9,... | collective-permute-start | bytes 786440 | tf_op jit(solution)/shard_map/ppermute | solution.py:320
  126.7 23.4 %collective-permute-start.3 = (bf16[1,2,256,256]{3,2,1,0:T(8,128)(2,1)}, bf16[1,2,256,256]{3,2,1,0:T(8,128)(2,1)S(1)}, u32[]{:S(2)}, u32[]{:S(2)}) collective-permute-start(bf16[1,2,256,256]{3,2,1,0:T(8,128)(2,1)} %get-tuple-element.38), channel_id=1, source_target_pairs={{0,24},{1,25},{2,26},{3,27},{4,28},{5,29},{6,30},{7,31},{8,16},{9,... | collective-permute-start | bytes 786440 | tf_op jit(solution)/shard_map/ppermute | solution.py:320
  136.1 17.8 %collective-permute-start.12 = (bf16[2,256,256]{2,1,0:T(8,128)(2,1)}, bf16[2,256,256]{2,1,0:T(8,128)(2,1)S(1)}, u32[]{:S(2)}, u32[]{:S(2)}) collective-permute-start(bf16[2,256,256]{2,1,0:T(8,128)(2,1)} %get-tuple-element.44), channel_id=1, source_target_pairs={{0,1},{1,2},{2,3},{4,5},{5,6},{6,7},{8,9},{9,10},{10,11},{12,13},{... | collective-permute-start | bytes 786440 | tf_op jit(solution)/shard_map/ppermute | solution.py:320
  140.1 13.8 %collective-permute-start.13 = (bf16[2,256,256]{2,1,0:T(8,128)(2,1)}, bf16[2,256,256]{2,1,0:T(8,128)(2,1)S(1)}, u32[]{:S(2)}, u32[]{:S(2)}) collective-permute-start(bf16[2,256,256]{2,1,0:T(8,128)(2,1)} %get-tuple-element.45), channel_id=1, source_target_pairs={{1,0},{2,1},{3,2},{5,4},{6,5},{7,6},{9,8},{10,9},{11,10},{13,12},{... | collective-permute-start | bytes 786440 | tf_op jit(solution)/shard_map/ppermute | solution.py:320
  145.7 15.5 %collective-permute-start.24 = (bf16[2,256,256]{2,1,0:T(8,128)(2,1)}, bf16[2,256,256]{2,1,0:T(8,128)(2,1)S(1)}, u32[]{:S(2)}, u32[]{:S(2)}) collective-permute-start(bf16[2,256,256]{2,1,0:T(8,128)(2,1)} %get-tuple-element.55), channel_id=1, source_target_pairs={{0,2},{1,3},{2,0},{3,1},{4,6},{5,7},{6,4},{7,5},{8,10},{9,11},{10,... | collective-permute-start | bytes 786440 | tf_op jit(solution)/shard_map/ppermute | solution.py:320
  150.0 15.2 %collective-permute-start.26 = (bf16[2,256,256]{2,1,0:T(8,128)(2,1)}, bf16[2,256,256]{2,1,0:T(8,128)(2,1)S(1)}, u32[]{:S(2)}, u32[]{:S(2)}) collective-permute-start(bf16[2,256,256]{2,1,0:T(8,128)(2,1)} %get-tuple-element.57), channel_id=1, source_target_pairs={{1,0},{2,3},{5,4},{6,7},{9,8},{10,11},{13,12},{14,15},{17,16},{18,... | collective-permute-start | bytes 786440 | tf_op jit(solution)/shard_map/ppermute | solution.py:320
  158.0 23.2 %collective-permute-start.14 = (bf16[2,256,256]{2,1,0:T(8,128)(2,1)}, bf16[2,256,256]{2,1,0:T(8,128)(2,1)S(1)}, u32[]{:S(2)}, u32[]{:S(2)}) collective-permute-start(bf16[2,256,256]{2,1,0:T(8,128)(2,1)} %get-tuple-element.47), channel_id=1, source_target_pairs={{0,8},{1,9},{2,10},{4,12},{5,13},{6,14},{8,0},{9,1},{12,4},{13,5},... | collective-permute-start | bytes 786440 | tf_op jit(solution)/shard_map/ppermute | solution.py:320
  159.9 24.8 %collective-permute-start.15 = (bf16[2,256,256]{2,1,0:T(8,128)(2,1)}, bf16[2,256,256]{2,1,0:T(8,128)(2,1)S(1)}, u32[]{:S(2)}, u32[]{:S(2)}) collective-permute-start(bf16[2,256,256]{2,1,0:T(8,128)(2,1)} %get-tuple-element.48), channel_id=1, source_target_pairs={{1,17},{2,18},{3,19},{5,21},{6,22},{7,23},{10,26},{11,27},{14,30},... | collective-permute-start | bytes 786440 | tf_op jit(solution)/shard_map/ppermute | solution.py:320
  161.2 23.4 %collective-permute-start.16 = (bf16[2,256,256]{2,1,0:T(8,128)(2,1)}, bf16[2,256,256]{2,1,0:T(8,128)(2,1)S(1)}, u32[]{:S(2)}, u32[]{:S(2)}) collective-permute-start(bf16[2,256,256]{2,1,0:T(8,128)(2,1)} %get-tuple-element.49), channel_id=1, source_target_pairs={{2,26},{3,27},{6,30},{7,31},{9,17},{10,18},{11,19},{13,21},{14,22}... | collective-permute-start | bytes 786440 | tf_op jit(solution)/shard_map/ppermute | solution.py:320
  169.1 15.5 %collective-permute-start.27 = (bf16[2,256,256]{2,1,0:T(8,128)(2,1)}, bf16[2,256,256]{2,1,0:T(8,128)(2,1)S(1)}, u32[]{:S(2)}, u32[]{:S(2)}) collective-permute-start(bf16[2,256,256]{2,1,0:T(8,128)(2,1)} %get-tuple-element.59), channel_id=1, source_target_pairs={{3,11},{7,15},{10,2},{11,3},{14,6},{15,7},{16,24},{17,25},{20,28},... | collective-permute-start | bytes 786440 | tf_op jit(solution)/shard_map/ppermute | solution.py:320
  169.8 22.0 %collective-permute-start.28 = (bf16[2,256,256]{2,1,0:T(8,128)(2,1)}, bf16[2,256,256]{2,1,0:T(8,128)(2,1)S(1)}, u32[]{:S(2)}, u32[]{:S(2)}) collective-permute-start(bf16[2,256,256]{2,1,0:T(8,128)(2,1)} %get-tuple-element.60), channel_id=1, source_target_pairs={{0,16},{4,20},{8,24},{9,25},{12,28},{13,29},{18,2},{19,3},{22,6},{... | collective-permute-start | bytes 786440 | tf_op jit(solution)/shard_map/ppermute | solution.py:320
  (30 other events, 166.7 us)

commit v2 on v1

v2 whole, which is shorter than its diff:
```python
import functools

import jax
import jax.numpy as jnp
from jax import lax
from jax.experimental import pallas as pl
from jax.experimental.pallas import tpu as pltpu
from jax.sharding import PartitionSpec as P


AXES = ("cells", "genes")


def normalize(counts, library):
    factor = 10000.0 / library.astype(jnp.float32)
    return jnp.log1p(counts.astype(jnp.float32) * factor[:, None]).astype(jnp.bfloat16)


def cross_product(left, right):
    return lax.dot_general(
        left, right, (((0,), (0,)), ((), ())), preferred_element_type=jnp.float32
    )


def general_shards(counts, library):
    own_block = normalize(counts, library)
    col_width = own_block.shape[1]
    cell_groups = lax.axis_size("cells")
    gene_total = col_width * lax.axis_size("genes")
    row_width = gene_total // cell_groups
    total_cells = float(counts.shape[0] * cell_groups)
    widened = own_block.astype(jnp.float32)
    local_sums = jnp.sum(widened, axis=0)
    local_squares = jnp.sum(widened * widened, axis=0)
    block_sums, block_squares = lax.psum((local_sums, local_squares), "cells")
    gene_sums, gene_squares = (
        lax.all_gather(block_sums, "genes", axis=0, tiled=True),
        lax.all_gather(block_squares, "genes", axis=0, tiled=True),
    )
    full_block = lax.all_gather(own_block, "genes", axis=1, tiled=True)
    gram_tile = lax.psum_scatter(
        cross_product(full_block, own_block), "cells", scatter_dimension=0, tiled=True
    )
    means = gene_sums / total_cells
    variances = gene_squares / total_cells - means * means
    scales = lax.rsqrt(variances + 1e-05)
    row_first = lax.axis_index("cells") * row_width
    col_first = lax.axis_index("genes") * col_width
    row_means = lax.dynamic_slice_in_dim(means, row_first, row_width, 0)
    col_means = lax.dynamic_slice_in_dim(means, col_first, col_width, 0)
    row_scales = lax.dynamic_slice_in_dim(scales, row_first, row_width, 0)
    col_scales = lax.dynamic_slice_in_dim(scales, col_first, col_width, 0)
    correlation = (
        (gram_tile / total_cells - row_means[:, None] * col_means[None, :])
        * row_scales[:, None]
        * col_scales[None, :]
    )
    powered = correlation**6
    row_index = row_first + jnp.arange(row_width, dtype=jnp.int32)[:, None]
    col_index = col_first + jnp.arange(col_width, dtype=jnp.int32)[None, :]
    adjacency = jnp.where(row_index == col_index, jnp.float32(0.0), powered)
    connectivity = lax.psum(jnp.sum(adjacency, axis=1), "genes")
    return (adjacency, connectivity)


def encode(x):
    return (x * jnp.abs(x) * (x * x)).astype(jnp.bfloat16)


def decode(y):
    y = y.astype(jnp.float32)
    root = lax.rsqrt(lax.rsqrt(jnp.abs(y)))
    return jnp.where(y < 0, -root, root)


def plain(left, right):
    return jnp.dot(left, right, preferred_element_type=jnp.float32)


def put_tiles(products, sums, s_ref, jj, blk, rst, cst, cells, total, own_ref, sends):
    odd = s_ref[CHIP] % 2
    row_side = rst.T
    mr, sr = row_side[:, 0:1], row_side[:, 1:2] * (1.0 / total)
    sx = sums(rst).reshape(1, -1)
    sx = jnp.broadcast_to(sx, (8, sx.shape[1])).T[:, 0:1]
    mc, sc = cst[0:1], cst[1:2]
    rest = sums(cst) - cells * mc
    t = sr.shape[0] // 2
    tiles = [[None, None], [None, None]]
    for c in range(2):
        lanes = slice(c * t, c * t + t)
        p = products(c)
        p = (p - sx * mc[:, lanes] - mr * rest[:, lanes]) * sr * sc[:, lanes]
        tiles[0][c], tiles[1][c] = p[:t], p[t:]
    for b in range(2):
        for i in range(2):
            tile = jnp.where(odd == 0, tiles[i][i ^ b], tiles[i][1 - (i ^ b)])
            coded = encode(tile)

            @pl.when(jj == 0)
            def _():
                if b == 0:
                    own_ref[blk, i] = tile
                else:
                    sends[0][blk, i] = coded

            @pl.when(jj == 1)
            def _():
                sends[1 + b][blk, i] = coded


def diagonal_body(s_ref, xa, xb, y0, y1, rst, cst, own_ref, o1, o2, o3, xs, ys, *, total):
    jj = pl.program_id(0)
    n = y0.shape[0] // 2
    t = y0.shape[1] // 2

    @pl.when(jj == 0)
    def _():
        xs[:, : 2 * n] = xa[...]
        xs[:, 2 * n :] = xb[...]

    for q in range(2):
        ys[2 * q * n : (2 * q + 1) * n] = y0[q * n : q * n + n]
        ys[(2 * q + 1) * n : (2 * q + 2) * n] = y1[q * n : q * n + n]
    put_tiles(
        lambda c: plain(xs[...], ys[:, c * t : c * t + t]),
        lambda st: st[2:3] + st[3:4],
        s_ref, jj, 0, rst[0], cst[0], 4.0 * n, total, own_ref, (o1, o2, o3),
    )


def near_body(s_ref, xa, xb, y0, y1, rst, cst, own_ref, o1, o2, o3, xs, ys, *, total):
    blk, jj = pl.program_id(0), pl.program_id(1)
    n = y0.shape[0]
    t = y0.shape[1] // 2

    @pl.when((jj == 0) & (blk == 0))
    def _():
        xs[...] = xa[...]

    @pl.when((jj == 0) & (blk == 1))
    def _():
        xs[...] = xb[...]

    ys[:n] = y0[...]
    ys[n:] = y1[...]
    put_tiles(
        lambda c: plain(xs[...], ys[:, c * t : c * t + t]),
        lambda st: jnp.where(blk == 0, st[2:3], st[3:4]),
        s_ref, jj, blk, rst[0], cst[0], 2.0 * n, total, own_ref, (o1, o2, o3),
    )


def far_body(s_ref, xa, xb, y0, y1, na, nb, rst, cst, own_ref, o1, o2, o3, xs, ys, *, total):
    blk, jj = pl.program_id(0), pl.program_id(1)
    n = y0.shape[0]
    t = y0.shape[1] // 2
    low = s_ref[LOW]

    @pl.when((jj == 0) & (blk == 0) & (low == 0))
    def _():
        xs[...] = xa[...]

    @pl.when((jj == 0) & (blk == 0) & (low == 1))
    def _():
        xs[...] = xb[...]

    other = (s_ref[CHIP] // 2) ^ jj

    @pl.when(blk == 0)
    def _():
        ys[:n] = y0[...]
        ys[n:] = y1[...]

    @pl.when((blk == 1) & (other == 0))
    def _():
        ys[...] = na[...]

    @pl.when((blk == 1) & (other == 1))
    def _():
        ys[:n] = nb[n:]
        ys[n:] = nb[:n]

    put_tiles(
        lambda c: plain(xs[...], ys[:, c * t : c * t + t]),
        lambda st: jnp.where(low == 0, st[2:3], st[3:4]),
        s_ref, jj, blk, rst[0], cst[0], 2.0 * n, total, own_ref, (o1, o2, o3),
    )


CHIP, CORE, PLANE, PLANES, LOW, LOWER, _, SHIFT, EARLY = range(9)


def turn_body(s_ref, own, r1, r2, r3, *outs, turns, keeps):
    odd = s_ref[CHIP] % 2
    t_ref, rest = outs[0], outs[1:]
    for n in range(own.shape[0]):
        for i in range(2):
            v = own[n, i] + decode(r1[n, i]) + decode(r2[n, i]) + decode(r3[n, i])
            t_ref[n, i] = v
            if keeps[n] is not None:
                rest[keeps[n]][i] = encode(v)
            if turns[n] is not None:
                w = encode(v.T)
                dst = rest[turns[n]]

                @pl.when(odd == 0)
                def _():
                    dst[i] = w

                @pl.when(odd == 1)
                def _():
                    dst[1 - i] = w


def power(v):
    v2 = v * v
    return v2 * v2 * v2


def put_slot(outs, where, i, value):
    for j, o in enumerate(outs):

        @pl.when(where == j)
        def _():
            o[i] = value


def early_body(s_ref, t0, t1, ru, rd, *outs):
    k, g = s_ref[CHIP], s_ref[PLANE]
    n = t0.shape[-1]
    for i in range(2):
        own = power(t0[0, i])
        same = lax.broadcasted_iota(jnp.int32, (n, n), 0) == lax.broadcasted_iota(
            jnp.int32, (n, n), 1
        )
        own = jnp.where(same & (k == 0), 0.0, own).astype(jnp.bfloat16)
        put_slot(outs, g ^ k, i, own)
        low = power(t1[0, i] + decode(ru[i])).astype(jnp.bfloat16)
        put_slot(outs, jnp.where(g > 0, (g - 1) ^ k, -1), i, low)
        high = power(t1[1, i] + decode(rd[i])).astype(jnp.bfloat16)
        put_slot(outs, jnp.where(g < s_ref[PLANES] - 1, (g + 1) ^ k, -1), i, high)


def late_body(s_ref, t2, r2, rf, rn, *outs):
    k, g = s_ref[CHIP], s_ref[PLANE]
    outer = (g == 0) | (g == s_ref[PLANES] - 1)
    for i in range(2):
        two = power(t2[0, i] + decode(r2[i])).astype(jnp.bfloat16)
        put_slot(outs, g ^ 2 ^ k, i, two)
        three = power(decode(rf[i]) + decode(rn[i])).astype(jnp.bfloat16)
        put_slot(outs, jnp.where(outer, g ^ 3 ^ k, -1), i, three)


def place_body(s_ref, e0, e1, e2, e3, l0, l1, l2, l3, out_ref, sum_ref):
    x = s_ref[SHIFT]
    is_early = s_ref[EARLY]
    early, late = (e0, e1, e2, e3), (l0, l1, l2, l3)
    t = e0.shape[-1]

    def place(tiles):
        for i in range(2):
            total = jnp.zeros((t, 1), jnp.float32)
            for c in range(4):
                v = tiles[c ^ i][i]
                for m in range(1, 4):
                    v = jnp.where(x == m, tiles[c ^ i ^ m][i], v)
                v = v.astype(jnp.float32)
                out_ref[i * t : i * t + t, c * t : c * t + t] = v
                total = total + jnp.sum(v, axis=1, keepdims=True)
            sum_ref[i * t : i * t + t, :] = total

    @pl.when(is_early == 1)
    def _():
        place(early)

    @pl.when(is_early == 0)
    def _():
        place(late)


def pay_body(s_ref, a, *refs):
    out_a, out_b = refs[-2:]
    n = a.shape[0] // 2
    out_a[...] = a[:n].T
    out_b[...] = a[n:].T


def limit(mib):
    return pltpu.CompilerParams(vmem_limit_bytes=mib * 1024 * 1024)


def whole():
    return pl.BlockSpec(memory_space=pltpu.VMEM)


def scalars():
    return pl.BlockSpec(memory_space=pltpu.SMEM)


def folded_shards(counts, library):
    rows, width = counts.shape
    n_cells = lax.axis_size("cells")
    n_genes = lax.axis_size("genes")
    cores = n_cells // n_genes
    total = float(rows * n_cells)
    half_cells = rows // 2
    half = width // cores
    tile = half // 2
    g = lax.axis_index("genes")
    c = lax.axis_index("cells")
    k, h = c // cores, c % cores

    def perm(f):
        pairs = []
        for ci in range(n_cells):
            for gi in range(n_genes):
                d = f(ci // cores, ci % cores, gi)
                if d is not None and 0 <= d[2] < n_genes:
                    pairs.append((ci * n_genes + gi, (d[0] * cores + d[1]) * n_genes + d[2]))
        return pairs

    def send(x, f):
        return lax.ppermute(x, AXES, perm(f))

    flip = lambda k, h, g: (k, h ^ 1, g)
    bf16, f32 = jnp.bfloat16, jnp.float32
    shape = jax.ShapeDtypeStruct

    last = n_genes - 1
    own = normalize(counts, library)
    oth = send(own, flip)
    info = jnp.stack(
        [
            k,
            h,
            g,
            jnp.int32(n_genes),
            (g < n_genes // 2).astype(jnp.int32),
            jnp.where(g > 0, g ^ (g - 1), 0),
            jnp.where(g < last, g ^ (g + 1), 0),
            (2 * h) ^ k,
            (jnp.abs(k - g) <= 1).astype(jnp.int32),
        ]
    ).astype(jnp.int32)

    pay_in = pl.BlockSpec((rows, half), lambda i, sc: (0, sc[CORE]))
    pay_shapes = [shape((half, rows), bf16)] * 2

    def turn_payload(block, part, before):
        return pl.pallas_call(
            pay_body,
            grid_spec=pltpu.PrefetchScalarGridSpec(
                num_scalar_prefetch=1,
                grid=(1,),
                in_specs=[pay_in] + [pl.BlockSpec(memory_space=pl.ANY)] * len(before),
                out_specs=[pl.BlockSpec((half, half_cells), lambda i, sc: (0, part))] * 2,
            ),
            out_shape=pay_shapes,
            input_output_aliases={2 + n: n for n in range(len(before))},
            compiler_params=limit(8),
            name="turn_payload",
        )(info, block, *before)

    pay_a, pay_b = turn_payload(oth, 1, turn_payload(own, 0, []))
    up1 = send(pay_a, lambda k, h, g: (k, h, g + 1))
    dn1 = send(pay_b, lambda k, h, g: (k, h, g - 1))
    widened = own.astype(f32)
    halves = jnp.sum(widened.reshape(2, half_cells, width), axis=1)
    squares = jnp.sum(widened * widened, axis=0)
    chip_halves = halves + send(halves, flip)
    sums = lax.psum(jnp.stack([halves[0] + halves[1], squares]), "cells")
    means = sums[0] / total
    variances = sums[1] / total - means * means
    mine = jnp.concatenate(
        [means[None], lax.rsqrt(variances + 1e-05)[None], chip_halves, jnp.zeros((4, width), f32)]
    )
    afar = [send(mine, lambda k, h, g, d=d: (k, h, g ^ d)) for d in (1, 2, 3)]
    own_stats = mine[None]
    stats = jnp.stack([mine] + afar)
    corner = (jnp.where(g == 0, half_cells, 0), h * half)
    end = jnp.concatenate([lax.dynamic_slice(a, corner, (half_cells, half)) for a in (own, oth)])
    near = send(
        end, lambda k, h, g: (k, h, 1) if g == 0 else ((k, h, g - 1) if g == last else None)
    )

    def block_outs(n):
        spec = pl.BlockSpec((n, 2, tile, tile), lambda *_: (0, 0, 0, 0))
        return [spec] * 4

    def out_shapes(n):
        return [shape((n, 2, tile, tile), f32)] + [shape((n, 2, tile, tile), bf16)] * 3

    def stat_spec(m):
        return pl.BlockSpec((1, 8, half), m)

    col = lambda jj, sc: sc[CORE] ^ (sc[CHIP] // 2) ^ jj
    x_spec = pl.BlockSpec((half, rows), lambda jj, sc: (0, 0))
    y_spec = pl.BlockSpec((rows, half), lambda jj, sc: (0, col(jj, sc)))
    w0 = pl.pallas_call(
        functools.partial(diagonal_body, total=total),
        grid_spec=pltpu.PrefetchScalarGridSpec(
            num_scalar_prefetch=1,
            grid=(2,),
            in_specs=[
                x_spec,
                x_spec,
                y_spec,
                y_spec,
                stat_spec(lambda jj, sc: (0, 0, sc[CORE])),
                stat_spec(lambda jj, sc: (0, 0, col(jj, sc))),
            ],
            out_specs=block_outs(1),
            scratch_shapes=[pltpu.VMEM((half, 2 * rows), bf16), pltpu.VMEM((2 * rows, half), bf16)],
        ),
        out_shape=out_shapes(1),
        compiler_params=limit(24),
        name="diagonal_block",
    )(info, pay_a, pay_b, own, oth, own_stats, own_stats)

    up2 = send(up1, lambda k, h, g: (k, h, g + 1) if g > 0 else None)
    dn2 = send(dn1, lambda k, h, g: (k, h, g - 1) if g < last else None)
    near_other = send(near, flip)

    x_spec = pl.BlockSpec((half, rows), lambda b, jj, sc: (0, 0))
    scratch = [pltpu.VMEM((half, rows), bf16), pltpu.VMEM((rows, half), bf16)]
    y_spec = pl.BlockSpec((half_cells, half), lambda b, jj, sc: (b, col(jj, sc)))
    w1 = pl.pallas_call(
        functools.partial(near_body, total=total),
        grid_spec=pltpu.PrefetchScalarGridSpec(
            num_scalar_prefetch=1,
            grid=(2, 2),
            in_specs=[
                x_spec,
                x_spec,
                y_spec,
                y_spec,
                stat_spec(lambda b, jj, sc: (sc[LOWER + b], 0, sc[CORE])),
                stat_spec(lambda b, jj, sc: (0, 0, col(jj, sc))),
            ],
            out_specs=block_outs(2),
            scratch_shapes=scratch,
        ),
        out_shape=out_shapes(2),
        compiler_params=limit(20),
        name="near_blocks",
    )(info, up1, dn1, own, oth, stats, stats)

    n_spec = pl.BlockSpec((rows, half), lambda b, jj, sc: (0, 0))
    y_spec = pl.BlockSpec((half_cells, half), lambda b, jj, sc: (sc[LOW], col(jj, sc)))
    w2 = pl.pallas_call(
        functools.partial(far_body, total=total),
        grid_spec=pltpu.PrefetchScalarGridSpec(
            num_scalar_prefetch=1,
            grid=(2, 2),
            in_specs=[
                x_spec,
                x_spec,
                y_spec,
                y_spec,
                n_spec,
                n_spec,
                stat_spec(lambda b, jj, sc: (2, 0, sc[CORE])),
                stat_spec(lambda b, jj, sc: (b, 0, col(jj, sc))),
            ],
            out_specs=block_outs(2),
            scratch_shapes=scratch,
        ),
        out_shape=out_shapes(2),
        compiler_params=limit(20),
        name="far_blocks",
    )(info, up2, dn2, own, oth, near, near_other, stats, stats)

    def reduce_tiles(w):
        return [w[0]] + [send(w[j], lambda k, h, g, j=j: (k ^ j, h, g)) for j in (1, 2, 3)]

    small = shape((2, tile, tile), bf16)

    def turn(parts, turns, keeps):
        n = parts[0].shape[0]
        n_out = sum(v is not None for v in turns + keeps)
        return pl.pallas_call(
            functools.partial(turn_body, turns=turns, keeps=keeps),
            in_specs=[scalars()] + [whole()] * 4,
            out_specs=[whole()] * (1 + n_out),
            out_shape=[shape((n, 2, tile, tile), f32)] + [small] * n_out,
            compiler_params=limit(12),
            name="sum_tiles",
        )(info, *parts)

    (t0,) = turn(reduce_tiles(w0), [None], [None])
    t1, e_up, e_dn = turn(reduce_tiles(w1), [0, 1], [None, None])
    t2, e_two, e_three, k_three = turn(reduce_tiles(w2), [0, 1], [None, 2])

    side = lambda f: (lambda k, h, g: (k, h ^ (k // 2), f(g)) if f(g) is not None else None)
    rd = send(e_up, side(lambda g: g - 1))
    ru = send(e_dn, side(lambda g: g + 1))
    r2 = send(e_two, side(lambda g: g ^ 2))
    inner = lambda g: 0 < g < last
    r3f = send(e_three, side(lambda g: (g ^ 2) if inner(g) else None))
    r3n = send(k_three, lambda k, h, g: (k, h, g ^ 1) if inner(g) else None)

    early = pl.pallas_call(
        early_body,
        in_specs=[scalars()] + [whole()] * 4,
        out_specs=[whole()] * 4,
        out_shape=[small] * 4,
        compiler_params=limit(10),
        name="early_tiles",
    )(info, t0, t1, ru, rd)
    late = pl.pallas_call(
        late_body,
        in_specs=[scalars()] + [whole()] * 4,
        out_specs=[whole()] * 4,
        out_shape=[small] * 4,
        compiler_params=limit(10),
        name="late_tiles",
    )(info, t2, r2, r3f, r3n)

    is_early = lambda q, g: -1 <= q - g <= 1
    got_early, got_late = [early[0]], [late[0]]
    for j in range(1, 4):
        got_early.append(
            send(early[j], lambda k, h, g, j=j: (k ^ j, h, g) if is_early(k ^ j, g) else None)
        )
        got_late.append(
            send(late[j], lambda k, h, g, j=j: (k ^ j, h, g) if not is_early(k ^ j, g) else None)
        )
    adjacency, row_sums = pl.pallas_call(
        place_body,
        in_specs=[scalars()] + [whole()] * 8,
        out_specs=[whole()] * 2,
        out_shape=[shape((half, width), f32), shape((half, 1), f32)],
        compiler_params=limit(12),
        name="place_tiles",
    )(info, *got_early, *got_late)
    part = row_sums[:, 0]
    peers = [send(part, lambda k, h, g, d=d: (k, h, g ^ d)) for d in (1, 2, 3)]
    connectivity = (part + peers[0]) + (peers[1] + peers[2])
    return (adjacency, connectivity)


def folded(counts, library):
    return folded_shards(counts, library)


def solution(mesh):
    cells, genes = mesh.shape["cells"], mesh.shape["genes"]
    folds = genes == 4 and cells == 2 * genes
    return jax.shard_map(
        folded if folds else general_shards,
        mesh=mesh,
        in_specs=(P("cells", "genes"), P("cells")),
        out_specs=(P("cells", "genes"), P("cells")),
        check_vma=False,
    )
```

time: 204 us -> 193 us (0.946)
  Pallas kernels: 58.3 us -> 34.8 us
  waiting for transfers between devices: 46.4 us -> 61 us
  other arithmetic: 12.2 us -> 7.03 us
  starting transfers between devices: 67.9 us -> 72.3 us
  local copies, waits for them, and re-layouts: 3.88 us -> 1.28 us
    ppermute x33 -> x34, waiting for transfers between devices: 46.4 us -> 61 us  [send(): return lax.ppermute(x, AXES, perm(f))]
    pallas_call x3, Pallas kernels: 11 us -> 4.69 us  [turn(): pl.pallas_call(functools.partial(turn_body, turns=turns, keeps=keeps), in...]
    pallas_call x1, Pallas kernels: 12.8 us -> 7.43 us  [folded_shards(): pl.pallas_call(functools.partial(far_body, total=total), grid_spec=pltpu....]
    pallas_call x1, Pallas kernels: 10.2 us -> 5.76 us  [folded_shards(): pl.pallas_call(functools.partial(diagonal_body, total=total), grid_spec=p...]
    ppermute x33 -> x34, starting transfers between devices: 67.9 us -> 72.3 us  [send(): return lax.ppermute(x, AXES, perm(f))]
    unnamed x42 -> x0, local copies, waits for them, and re-layouts: 3.26 us -> none
    another operation x7 -> x2, other arithmetic: 3.2 us -> 0.02 us  [the longest x1 0.01 us: folded_shards(): sums = lax.psum(jnp.stack([halves[0] + halves[1], squares]), 'cells')]
    pallas_call x1, Pallas kernels: 10.5 us -> 7.47 us  [folded_shards(): pl.pallas_call(functools.partial(near_body, total=total), grid_spec=pltpu...]
  transfers between devices with their start and end apart: 33 -> 34, of which waited for: 11 -> 16; matrix products, arithmetic and copies ran while one was open for 3% -> 1% of each run, Pallas kernels for 25% -> 15%
where the time goes in v2:
time: 193 us; the launch traced here: 192 us
  starting transfers between devices  72.3 us (37%)
  waiting for transfers between devices  61 us (32%)
  Pallas kernels  34.8 us (18%)
  blocking collectives  14.6 us (8%)
  other arithmetic  7.03 us (4%)
    ppermute x34, starting transfers between devices, send(): return lax.ppermute(x, AXES, perm(f))  72.3 us
    ppermute x34, waiting for transfers between devices, send(): return lax.ppermute(x, AXES, perm(f))  61 us
    psum x1, blocking collectives, folded_shards(): sums = lax.psum(jnp.stack([halves[0] + halves[1], squares]), 'cells')  14.6 us
    pallas_call x1, Pallas kernels, folded_shards(): pl.pallas_call(functools.partial(near_body, total=total), grid_spec=pltpu...  7.47 us
    pallas_call x1, Pallas kernels, folded_shards(): pl.pallas_call(functools.partial(far_body, total=total), grid_spec=pltpu....  7.43 us
    pallas_call x1, Pallas kernels, folded_shards(): pl.pallas_call(functools.partial(diagonal_body, total=total), grid_spec=p...  5.76 us
    pallas_call x3, Pallas kernels, turn(): pl.pallas_call(functools.partial(turn_body, turns=turns, keeps=keeps), in...  4.69 us
    pallas_call x2, Pallas kernels, turn_payload(): pl.pallas_call(pay_body, grid_spec=pltpu.PrefetchScalarGridSpec(num_scala...  4.57 us
  transfers between devices with their start and end apart: 34, of which 16 were waited for; matrix products, arithmetic and copies ran while one was open for 1% of the time, Pallas kernels for 15%

profile of v2, /device:TPU:0, one launch (start us, length us, event | category | flops | bytes accessed | tf_op | source)
XLA Modules:
  0.0 192.0 jit_solution(13266504282331506770)
XLA Ops:
  1.3 4.1 %multiply_reduce_fusion = (f32[1024]{0:T(1024)S(1)}, bf16[1024,1024]{1,0:T(8,128)(2,1)S(1)}) fusion(f32[1024]{0:T(1024)S(1)} %convert_divide_fusion, s32[1024,1024]{1,0:T(8,128)} %param.2), kind=kLoop, calls=%fused_computation.1 | loop fusion | flops 6290432 | bytes 6299648 | tf_op jit(solution)/shard_map/reduce_sum | solution.py:370
  9.9 2.9 %turn_payload.3 = (bf16[512,1024]{1,0:T(8,128)(2,1)S(1)}, bf16[512,1024]{1,0:T(8,128)(2,1)}) custom-call(s32[9]{0:T(128)S(1)} %stack.63.s_ref, bf16[1024,1024]{1,0:T(8,128)(2,1)} %collective-permute-done.a.y1, bf16[512,1024]{1,0:T(8,128)(2,1)S(1)} %get-tuple-element.35.refs_0_, ...), custom_call_target="tpu_custom_call", output_to_operand_aliasing={{0}: (2, {}), {1}: (3, {})} | custom-call | tf_op jit(solution)/shard_map/turn_payload/pallas_call | solution.py:351
  12.8 5.8 %collective-permute-start.5 = (bf16[512,1024]{1,0:T(8,128)(2,1)S(1)}, bf16[512,1024]{1,0:T(8,128)(2,1)}, u32[]{:S(2)}, u32[]{:S(2)}) collective-permute-start(bf16[512,1024]{1,0:T(8,128)(2,1)S(1)} %get-tuple-element.37.xa), channel_id=1, source_target_pairs={{0,1},{1,2},{2,3},{4,5},{5,6},{6,7},{8,9},{9,10},{10,11},{12,13},{... | collective-permute-start | bytes 3145736 | tf_op jit(solution)/shard_map/ppermute | solution.py:324
  22.0 5.6 %collective-permute-start.20 = (bf16[1024,512]{1,0:T(8,128)(2,1)}, bf16[1024,512]{1,0:T(8,128)(2,1)}, u32[]{:S(2)}, u32[]{:S(2)}) collective-permute-start(bf16[1024,512]{1,0:T(8,128)(2,1)} %pad_maximum_fusion), channel_id=1, source_target_pairs={{0,1},{3,2},{4,5},{7,6},{8,9},{11,10},{12,13},{15,14},{16,17},{19,... | collective-permute-start | bytes 3145736 | tf_op jit(solution)/shard_map/ppermute | solution.py:324
  28.1 14.6 %psum.7 = f32[2,1024]{1,0:T(2,128)S(1)} all-reduce(f32[2,1024]{1,0:T(2,128)S(1)} %pad_maximum_fusion.2), channel_id=1, replica_groups=mesh['cells'=8,'genes'=4] {'cells'}, use_global_device_ids=true, to_apply=%region_2.3 | all-reduce | flops 2048 | bytes 16384 | tf_op jit(solution)/shard_map/psum | solution.py:372
  47.0 15.9 %collective-permute-done.20.na = bf16[1024,512]{1,0:T(8,128)(2,1)} collective-permute-done((bf16[1024,512]{1,0:T(8,128)(2,1)}, bf16[1024,512]{1,0:T(8,128)(2,1)}, u32[]{:S(2)}, u32[]{:S(2)}) %collective-permute-start.20) | collective-permute-done | bytes 1048608 | tf_op jit(solution)/shard_map/ppermute | solution.py:324
  63.1 5.9 %collective-permute-start.9 = (f32[8,1024]{1,0:T(8,128)S(1)}, f32[8,1024]{1,0:T(8,128)S(1)}, u32[]{:S(2)}, u32[]{:S(2)}) collective-permute-start(f32[8,1024]{1,0:T(8,128)S(1)} %get-tuple-element.70), channel_id=1, source_target_pairs={{0,3},{1,2},{2,1},{3,0},{4,7},{5,6},{6,5},{7,4},{8,11},{9,10},{10,... | collective-permute-start | bytes 98312 | tf_op jit(solution)/shard_map/ppermute | solution.py:324
  71.2 3.2 %collective-permute-start.7 = (f32[8,1024]{1,0:T(8,128)S(1)}, f32[8,1024]{1,0:T(8,128)S(1)}, u32[]{:S(2)}, u32[]{:S(2)}) collective-permute-start(f32[8,1024]{1,0:T(8,128)S(1)} %get-tuple-element.70), channel_id=1, source_target_pairs={{0,1},{1,0},{2,3},{3,2},{4,5},{5,4},{6,7},{7,6},{8,9},{9,8},{10,11... | collective-permute-start | bytes 98312 | tf_op jit(solution)/shard_map/ppermute | solution.py:324
  76.3 7.5 %near_blocks.1 = (f32[2,2,256,256]{3,2,1,0:T(8,128)S(1)}, bf16[2,2,256,256]{3,2,1,0:T(8,128)(2,1)S(1)}, bf16[2,2,256,256]{3,2,1,0:T(8,128)(2,1)S(1)}, bf16[2,2,256,256]{3,2,1,0:T(8,128)(2,1)S(1)}) custom-call(s32[9]{0:T(128)S(1)} %stack.63.s_ref, bf16[512,1024]{1,0:T(8,128)(2,1)} %collective-permute-done.5.xa, bf16[512,1024]{1,0:T(8,128)(2,1)} %collective-permute-done.6.xb, ...), custom_call_target="tpu_custom_call" | custom-call | tf_op jit(solution)/shard_map/near_blocks/pallas_call | solution.py:428
  87.3 7.4 %far_blocks.1 = (f32[2,2,256,256]{3,2,1,0:T(8,128)S(1)}, bf16[2,2,256,256]{3,2,1,0:T(8,128)(2,1)S(1)}, bf16[2,2,256,256]{3,2,1,0:T(8,128)(2,1)S(1)}, bf16[2,2,256,256]{3,2,1,0:T(8,128)(2,1)S(1)}) custom-call(s32[9]{0:T(128)S(1)} %stack.63.s_ref, bf16[512,1024]{1,0:T(8,128)(2,1)S(1)} %collective-permute-done.18.xa, ...), custom_call_target="tpu_custom_call" | custom-call | tf_op jit(solution)/shard_map/far_blocks/pallas_call | solution.py:451
  98.6 2.4 %collective-permute-start.24 = (bf16[2,2,256,256]{3,2,1,0:T(8,128)(2,1)S(1)}, bf16[2,2,256,256]{3,2,1,0:T(8,128)(2,1)S(1)}, u32[]{:S(2)}, u32[]{:S(2)}) collective-permute-start(bf16[2,2,256,256]{3,2,1,0:T(8,128)(2,1)S(1)} %get-tuple-element.57), channel_id=1, source_target_pairs={{0,24},{1,25},{2,26},{3,27},{4,28},{5,29},{6,30},{7,31},{8,16},{9,... | collective-permute-start | bytes 1572872 | tf_op jit(solution)/shard_map/ppermute | solution.py:324
  101.1 5.8 %diagonal_block.1 = (f32[1,2,256,256]{3,2,1,0:T(8,128)S(1)}, bf16[1,2,256,256]{3,2,1,0:T(8,128)(2,1)S(1)}, bf16[1,2,256,256]{3,2,1,0:T(8,128)(2,1)S(1)}, bf16[1,2,256,256]{3,2,1,0:T(8,128)(2,1)S(1)}) custom-call(s32[9]{0:T(128)S(1)} %stack.63.s_ref, bf16[512,1024]{1,0:T(8,128)(2,1)S(1)} %get-tuple-element.37.xa, bf16[512,1024]{1,0:T(8,128)(2,1)} %get-tuple-element.38.xb, ...), custom_call_target="tpu_custom_call" | custom-call | tf_op jit(solution)/shard_map/diagonal_block/pallas_call | solution.py:400
  106.9 2.9 %collective-permute-done.11.r2 = bf16[2,2,256,256]{3,2,1,0:T(8,128)(2,1)S(1)} collective-permute-done((bf16[2,2,256,256]{3,2,1,0:T(8,128)(2,1)S(1)}, bf16[2,2,256,256]{3,2,1,0:T(8,128)(2,1)S(1)}, u32[]{:S(2)}, u32[]{:S(2)}) %collective-permute-start.11) | collective-permute-done | bytes 524320 | tf_op jit(solution)/shard_map/ppermute | solution.py:324
  114.0 7.2 %collective-permute-done.22.r1 = bf16[2,2,256,256]{3,2,1,0:T(8,128)(2,1)S(1)} collective-permute-done((bf16[2,2,256,256]{3,2,1,0:T(8,128)(2,1)S(1)}, bf16[2,2,256,256]{3,2,1,0:T(8,128)(2,1)S(1)}, u32[]{:S(2)}, u32[]{:S(2)}) %collective-permute-start.22) | collective-permute-done | bytes 524320 | tf_op jit(solution)/shard_map/ppermute | solution.py:324
  121.2 2.4 %collective-permute-start.4 = (bf16[1,2,256,256]{3,2,1,0:T(8,128)(2,1)S(1)}, bf16[1,2,256,256]{3,2,1,0:T(8,128)(2,1)S(1)}, u32[]{:S(2)}, u32[]{:S(2)}) collective-permute-start(bf16[1,2,256,256]{3,2,1,0:T(8,128)(2,1)S(1)} %get-tuple-element.42), channel_id=1, source_target_pairs={{0,24},{1,25},{2,26},{3,27},{4,28},{5,29},{6,30},{7,31},{8,16},{9,... | collective-permute-start | bytes 786440 | tf_op jit(solution)/shard_map/ppermute | solution.py:324
  123.6 9.5 %collective-permute-done.23.r2 = bf16[2,2,256,256]{3,2,1,0:T(8,128)(2,1)S(1)} collective-permute-done((bf16[2,2,256,256]{3,2,1,0:T(8,128)(2,1)S(1)}, bf16[2,2,256,256]{3,2,1,0:T(8,128)(2,1)S(1)}, u32[]{:S(2)}, u32[]{:S(2)}) %collective-permute-start.23) | collective-permute-done | bytes 524320 | tf_op jit(solution)/shard_map/ppermute | solution.py:324
  133.1 4.4 %collective-permute-start.13 = (bf16[2,256,256]{2,1,0:T(8,128)(2,1)S(1)}, bf16[2,256,256]{2,1,0:T(8,128)(2,1)S(1)}, u32[]{:S(2)}, u32[]{:S(2)}) collective-permute-start(bf16[2,256,256]{2,1,0:T(8,128)(2,1)S(1)} %get-tuple-element.48), channel_id=1, source_target_pairs={{0,1},{1,2},{2,3},{4,5},{5,6},{6,7},{8,9},{9,10},{10,11},{12,13},{... | collective-permute-start | bytes 786440 | tf_op jit(solution)/shard_map/ppermute | solution.py:324
  140.9 2.7 %collective-permute-start.25 = (bf16[2,256,256]{2,1,0:T(8,128)(2,1)S(1)}, bf16[2,256,256]{2,1,0:T(8,128)(2,1)S(1)}, u32[]{:S(2)}, u32[]{:S(2)}) collective-permute-start(bf16[2,256,256]{2,1,0:T(8,128)(2,1)S(1)} %get-tuple-element.59), channel_id=1, source_target_pairs={{0,2},{1,3},{2,0},{3,1},{4,6},{5,7},{6,4},{7,5},{8,10},{9,11},{10,... | collective-permute-start | bytes 786440 | tf_op jit(solution)/shard_map/ppermute | solution.py:324
  147.1 4.3 %collective-permute-done.14.rd = bf16[2,256,256]{2,1,0:T(8,128)(2,1)S(1)} collective-permute-done((bf16[2,256,256]{2,1,0:T(8,128)(2,1)S(1)}, bf16[2,256,256]{2,1,0:T(8,128)(2,1)S(1)}, u32[]{:S(2)}, u32[]{:S(2)}) %collective-permute-start.14) | collective-permute-done | bytes 262176 | tf_op jit(solution)/shard_map/ppermute | solution.py:324
  157.3 2.7 %collective-permute-done.27.rn = bf16[2,256,256]{2,1,0:T(8,128)(2,1)S(1)} collective-permute-done((bf16[2,256,256]{2,1,0:T(8,128)(2,1)S(1)}, bf16[2,256,256]{2,1,0:T(8,128)(2,1)S(1)}, u32[]{:S(2)}, u32[]{:S(2)}) %collective-permute-start.27) | collective-permute-done | bytes 262176 | tf_op jit(solution)/shard_map/ppermute | solution.py:324
  161.9 11.4 %collective-permute-start.29 = (bf16[2,256,256]{2,1,0:T(8,128)(2,1)S(1)}, bf16[2,256,256]{2,1,0:T(8,128)(2,1)S(1)}, u32[]{:S(2)}, u32[]{:S(2)}) collective-permute-start(bf16[2,256,256]{2,1,0:T(8,128)(2,1)S(1)} %get-tuple-element.64), channel_id=1, source_target_pairs={{0,16},{4,20},{8,24},{9,25},{12,28},{13,29},{18,2},{19,3},{22,6},{... | collective-permute-start | bytes 786440 | tf_op jit(solution)/shard_map/ppermute | solution.py:324
  173.4 2.7 %collective-permute-start.30 = (bf16[2,256,256]{2,1,0:T(8,128)(2,1)S(1)}, bf16[2,256,256]{2,1,0:T(8,128)(2,1)S(1)}, u32[]{:S(2)}, u32[]{:S(2)}) collective-permute-start(bf16[2,256,256]{2,1,0:T(8,128)(2,1)S(1)} %get-tuple-element.65), channel_id=1, source_target_pairs={{0,24},{1,25},{4,28},{5,29},{8,16},{12,20},{19,11},{23,15},{26,2},... | collective-permute-start | bytes 786440 | tf_op jit(solution)/shard_map/ppermute | solution.py:324
  176.2 7.2 %collective-permute-done.29.l2 = bf16[2,256,256]{2,1,0:T(8,128)(2,1)S(1)} collective-permute-done((bf16[2,256,256]{2,1,0:T(8,128)(2,1)S(1)}, bf16[2,256,256]{2,1,0:T(8,128)(2,1)S(1)}, u32[]{:S(2)}, u32[]{:S(2)}) %collective-permute-start.29) | collective-permute-done | bytes 262176 | tf_op jit(solution)/shard_map/ppermute | solution.py:324
  183.4 2.3 %place_tiles.1 = (f32[512,1024]{1,0:T(8,128)}, f32[512,1]{1,0:T(8,128)S(1)}) custom-call(s32[9]{0:T(128)S(1)} %stack.63.s_ref, bf16[2,256,256]{2,1,0:T(8,128)(2,1)S(1)} %get-tuple-element.50.e0, bf16[2,256,256]{2,1,0:T(8,128)(2,1)S(1)} %collective-permute-done.15.e1, bf16[2,256,256]{2,1,0:T(8,128)(2,1)S(1)} %collective-permute-done.16.e2, ...), custom_call_target="tpu_custom_call" | custom-call | tf_op jit(solution)/shard_map/place_tiles/pallas_call | solution.py:529
  (73 shorter events, 50.1 us)
Async XLA Ops:
  12.8 29.9 %collective-permute-start.5 = (bf16[512,1024]{1,0:T(8,128)(2,1)S(1)}, bf16[512,1024]{1,0:T(8,128)(2,1)}, u32[]{:S(2)}, u32[]{:S(2)}) collective-permute-start(bf16[512,1024]{1,0:T(8,128)(2,1)S(1)} %get-tuple-element.37.xa), channel_id=1, source_target_pairs={{0,1},{1,2},{2,3},{4,5},{5,6},{6,7},{8,9},{9,10},{10,11},{12,13},{... | collective-permute-start | bytes 3145736 | tf_op jit(solution)/shard_map/ppermute | solution.py:324
  18.6 27.1 %collective-permute-start.6 = (bf16[512,1024]{1,0:T(8,128)(2,1)}, bf16[512,1024]{1,0:T(8,128)(2,1)}, u32[]{:S(2)}, u32[]{:S(2)}) collective-permute-start(bf16[512,1024]{1,0:T(8,128)(2,1)} %get-tuple-element.38.xb), channel_id=1, source_target_pairs={{1,0},{2,1},{3,2},{5,4},{6,5},{7,6},{9,8},{10,9},{11,10},{13,12},{... | collective-permute-start | bytes 3145736 | tf_op jit(solution)/shard_map/ppermute | solution.py:324
  22.0 40.8 %collective-permute-start.20 = (bf16[1024,512]{1,0:T(8,128)(2,1)}, bf16[1024,512]{1,0:T(8,128)(2,1)}, u32[]{:S(2)}, u32[]{:S(2)}) collective-permute-start(bf16[1024,512]{1,0:T(8,128)(2,1)} %pad_maximum_fusion), channel_id=1, source_target_pairs={{0,1},{3,2},{4,5},{7,6},{8,9},{11,10},{12,13},{15,14},{16,17},{19,... | collective-permute-start | bytes 3145736 | tf_op jit(solution)/shard_map/ppermute | solution.py:324
  28.0 35.0 %collective-permute-start.1 = (f32[2,1024]{1,0:T(2,128)S(1)}, f32[2,1024]{1,0:T(2,128)S(1)}, u32[]{:S(2)}, u32[]{:S(2)}) collective-permute-start(f32[2,1024]{1,0:T(2,128)S(1)} %bitcast_reduce_fusion), channel_id=1, source_target_pairs={{0,4},{1,5},{2,6},{3,7},{4,0},{5,1},{6,2},{7,3},{8,12},{9,13},{10,... | collective-permute-start | bytes 24584 | tf_op jit(solution)/shard_map/ppermute | solution.py:324
  42.7 44.2 %collective-permute-start.18 = (bf16[512,1024]{1,0:T(8,128)(2,1)}, bf16[512,1024]{1,0:T(8,128)(2,1)S(1)}, u32[]{:S(2)}, u32[]{:S(2)}) collective-permute-start(bf16[512,1024]{1,0:T(8,128)(2,1)} %collective-permute-done.5.xa), channel_id=1, source_target_pairs={{1,2},{2,3},{5,6},{6,7},{9,10},{10,11},{13,14},{14,15},{17,18},{18... | collective-permute-start | bytes 3145736 | tf_op jit(solution)/shard_map/ppermute | solution.py:324
  45.7 41.6 %collective-permute-start.19 = (bf16[512,1024]{1,0:T(8,128)(2,1)}, bf16[512,1024]{1,0:T(8,128)(2,1)S(1)}, u32[]{:S(2)}, u32[]{:S(2)}) collective-permute-start(bf16[512,1024]{1,0:T(8,128)(2,1)} %collective-permute-done.6.xb), channel_id=1, source_target_pairs={{1,0},{2,1},{5,4},{6,5},{9,8},{10,9},{13,12},{14,13},{17,16},{18,1... | collective-permute-start | bytes 3145736 | tf_op jit(solution)/shard_map/ppermute | solution.py:324
  62.9 24.5 %collective-permute-start.21 = (bf16[1024,512]{1,0:T(8,128)(2,1)}, bf16[1024,512]{1,0:T(8,128)(2,1)S(1)}, u32[]{:S(2)}, u32[]{:S(2)}) collective-permute-start(bf16[1024,512]{1,0:T(8,128)(2,1)} %collective-permute-done.20.na), channel_id=1, source_target_pairs={{0,4},{1,5},{2,6},{3,7},{4,0},{5,1},{6,2},{7,3},{8,12},{9,13},{10,... | collective-permute-start | bytes 3145736 | tf_op jit(solution)/shard_map/ppermute | solution.py:324
  83.8 14.9 %collective-permute-start.10 = (bf16[2,2,256,256]{3,2,1,0:T(8,128)(2,1)S(1)}, bf16[2,2,256,256]{3,2,1,0:T(8,128)(2,1)S(1)}, u32[]{:S(2)}, u32[]{:S(2)}) collective-permute-start(bf16[2,2,256,256]{3,2,1,0:T(8,128)(2,1)S(1)} %get-tuple-element.44), channel_id=1, source_target_pairs={{0,8},{1,9},{2,10},{3,11},{4,12},{5,13},{6,14},{7,15},{8,0},{9,1},... | collective-permute-start | bytes 1572872 | tf_op jit(solution)/shard_map/ppermute | solution.py:324
  85.3 24.4 %collective-permute-start.11 = (bf16[2,2,256,256]{3,2,1,0:T(8,128)(2,1)S(1)}, bf16[2,2,256,256]{3,2,1,0:T(8,128)(2,1)S(1)}, u32[]{:S(2)}, u32[]{:S(2)}) collective-permute-start(bf16[2,2,256,256]{3,2,1,0:T(8,128)(2,1)S(1)} %get-tuple-element.45), channel_id=1, source_target_pairs={{0,16},{1,17},{2,18},{3,19},{4,20},{5,21},{6,22},{7,23},{8,24},{9,... | collective-permute-start | bytes 1572872 | tf_op jit(solution)/shard_map/ppermute | solution.py:324
  86.9 24.0 %collective-permute-start.12 = (bf16[2,2,256,256]{3,2,1,0:T(8,128)(2,1)S(1)}, bf16[2,2,256,256]{3,2,1,0:T(8,128)(2,1)S(1)}, u32[]{:S(2)}, u32[]{:S(2)}) collective-permute-start(bf16[2,2,256,256]{3,2,1,0:T(8,128)(2,1)S(1)} %get-tuple-element.46), channel_id=1, source_target_pairs={{0,24},{1,25},{2,26},{3,27},{4,28},{5,29},{6,30},{7,31},{8,16},{9,... | collective-permute-start | bytes 1572872 | tf_op jit(solution)/shard_map/ppermute | solution.py:324
  94.8 26.4 %collective-permute-start.22 = (bf16[2,2,256,256]{3,2,1,0:T(8,128)(2,1)S(1)}, bf16[2,2,256,256]{3,2,1,0:T(8,128)(2,1)S(1)}, u32[]{:S(2)}, u32[]{:S(2)}) collective-permute-start(bf16[2,2,256,256]{3,2,1,0:T(8,128)(2,1)S(1)} %get-tuple-element.55), channel_id=1, source_target_pairs={{0,8},{1,9},{2,10},{3,11},{4,12},{5,13},{6,14},{7,15},{8,0},{9,1},... | collective-permute-start | bytes 1572872 | tf_op jit(solution)/shard_map/ppermute | solution.py:324
  96.3 36.8 %collective-permute-start.23 = (bf16[2,2,256,256]{3,2,1,0:T(8,128)(2,1)S(1)}, bf16[2,2,256,256]{3,2,1,0:T(8,128)(2,1)S(1)}, u32[]{:S(2)}, u32[]{:S(2)}) collective-permute-start(bf16[2,2,256,256]{3,2,1,0:T(8,128)(2,1)S(1)} %get-tuple-element.56), channel_id=1, source_target_pairs={{0,16},{1,17},{2,18},{3,19},{4,20},{5,21},{6,22},{7,23},{8,24},{9,... | collective-permute-start | bytes 1572872 | tf_op jit(solution)/shard_map/ppermute | solution.py:324
  98.6 38.9 %collective-permute-start.24 = (bf16[2,2,256,256]{3,2,1,0:T(8,128)(2,1)S(1)}, bf16[2,2,256,256]{3,2,1,0:T(8,128)(2,1)S(1)}, u32[]{:S(2)}, u32[]{:S(2)}) collective-permute-start(bf16[2,2,256,256]{3,2,1,0:T(8,128)(2,1)S(1)} %get-tuple-element.57), channel_id=1, source_target_pairs={{0,24},{1,25},{2,26},{3,27},{4,28},{5,29},{6,30},{7,31},{8,16},{9,... | collective-permute-start | bytes 1572872 | tf_op jit(solution)/shard_map/ppermute | solution.py:324
  109.7 31.1 %collective-permute-start.2 = (bf16[1,2,256,256]{3,2,1,0:T(8,128)(2,1)S(1)}, bf16[1,2,256,256]{3,2,1,0:T(8,128)(2,1)S(1)}, u32[]{:S(2)}, u32[]{:S(2)}) collective-permute-start(bf16[1,2,256,256]{3,2,1,0:T(8,128)(2,1)S(1)} %get-tuple-element.40), channel_id=1, source_target_pairs={{0,8},{1,9},{2,10},{3,11},{4,12},{5,13},{6,14},{7,15},{8,0},{9,1},... | collective-permute-start | bytes 786440 | tf_op jit(solution)/shard_map/ppermute | solution.py:324
  110.9 32.7 %collective-permute-start.3 = (bf16[1,2,256,256]{3,2,1,0:T(8,128)(2,1)S(1)}, bf16[1,2,256,256]{3,2,1,0:T(8,128)(2,1)S(1)}, u32[]{:S(2)}, u32[]{:S(2)}) collective-permute-start(bf16[1,2,256,256]{3,2,1,0:T(8,128)(2,1)S(1)} %get-tuple-element.41), channel_id=1, source_target_pairs={{0,16},{1,17},{2,18},{3,19},{4,20},{5,21},{6,22},{7,23},{8,24},{9,... | collective-permute-start | bytes 786440 | tf_op jit(solution)/shard_map/ppermute | solution.py:324
  121.2 23.7 %collective-permute-start.4 = (bf16[1,2,256,256]{3,2,1,0:T(8,128)(2,1)S(1)}, bf16[1,2,256,256]{3,2,1,0:T(8,128)(2,1)S(1)}, u32[]{:S(2)}, u32[]{:S(2)}) collective-permute-start(bf16[1,2,256,256]{3,2,1,0:T(8,128)(2,1)S(1)} %get-tuple-element.42), channel_id=1, source_target_pairs={{0,24},{1,25},{2,26},{3,27},{4,28},{5,29},{6,30},{7,31},{8,16},{9,... | collective-permute-start | bytes 786440 | tf_op jit(solution)/shard_map/ppermute | solution.py:324
  133.1 14.0 %collective-permute-start.13 = (bf16[2,256,256]{2,1,0:T(8,128)(2,1)S(1)}, bf16[2,256,256]{2,1,0:T(8,128)(2,1)S(1)}, u32[]{:S(2)}, u32[]{:S(2)}) collective-permute-start(bf16[2,256,256]{2,1,0:T(8,128)(2,1)S(1)} %get-tuple-element.48), channel_id=1, source_target_pairs={{0,1},{1,2},{2,3},{4,5},{5,6},{6,7},{8,9},{9,10},{10,11},{12,13},{... | collective-permute-start | bytes 786440 | tf_op jit(solution)/shard_map/ppermute | solution.py:324
  140.9 15.1 %collective-permute-start.25 = (bf16[2,256,256]{2,1,0:T(8,128)(2,1)S(1)}, bf16[2,256,256]{2,1,0:T(8,128)(2,1)S(1)}, u32[]{:S(2)}, u32[]{:S(2)}) collective-permute-start(bf16[2,256,256]{2,1,0:T(8,128)(2,1)S(1)} %get-tuple-element.59), channel_id=1, source_target_pairs={{0,2},{1,3},{2,0},{3,1},{4,6},{5,7},{6,4},{7,5},{8,10},{9,11},{10,... | collective-permute-start | bytes 786440 | tf_op jit(solution)/shard_map/ppermute | solution.py:324
  144.9 15.1 %collective-permute-start.27 = (bf16[2,256,256]{2,1,0:T(8,128)(2,1)S(1)}, bf16[2,256,256]{2,1,0:T(8,128)(2,1)S(1)}, u32[]{:S(2)}, u32[]{:S(2)}) collective-permute-start(bf16[2,256,256]{2,1,0:T(8,128)(2,1)S(1)} %get-tuple-element.61), channel_id=1, source_target_pairs={{1,0},{2,3},{5,4},{6,7},{9,8},{10,11},{13,12},{14,15},{17,16},{18,... | collective-permute-start | bytes 786440 | tf_op jit(solution)/shard_map/ppermute | solution.py:324
  152.7 20.6 %collective-permute-start.15 = (bf16[2,256,256]{2,1,0:T(8,128)(2,1)S(1)}, bf16[2,256,256]{2,1,0:T(8,128)(2,1)S(1)}, u32[]{:S(2)}, u32[]{:S(2)}) collective-permute-start(bf16[2,256,256]{2,1,0:T(8,128)(2,1)S(1)} %get-tuple-element.51), channel_id=1, source_target_pairs={{0,8},{1,9},{2,10},{4,12},{5,13},{6,14},{8,0},{9,1},{12,4},{13,5},... | collective-permute-start | bytes 786440 | tf_op jit(solution)/shard_map/ppermute | solution.py:324
  154.6 21.5 %collective-permute-start.16 = (bf16[2,256,256]{2,1,0:T(8,128)(2,1)S(1)}, bf16[2,256,256]{2,1,0:T(8,128)(2,1)S(1)}, u32[]{:S(2)}, u32[]{:S(2)}) collective-permute-start(bf16[2,256,256]{2,1,0:T(8,128)(2,1)S(1)} %get-tuple-element.52), channel_id=1, source_target_pairs={{1,17},{2,18},{3,19},{5,21},{6,22},{7,23},{10,26},{11,27},{14,30},... | collective-permute-start | bytes 786440 | tf_op jit(solution)/shard_map/ppermute | solution.py:324
  156.0 20.2 %collective-permute-start.17 = (bf16[2,256,256]{2,1,0:T(8,128)(2,1)S(1)}, bf16[2,256,256]{2,1,0:T(8,128)(2,1)S(1)}, u32[]{:S(2)}, u32[]{:S(2)}) collective-permute-start(bf16[2,256,256]{2,1,0:T(8,128)(2,1)S(1)} %get-tuple-element.53), channel_id=1, source_target_pairs={{2,26},{3,27},{6,30},{7,31},{9,17},{10,18},{11,19},{13,21},{14,22}... | collective-permute-start | bytes 786440 | tf_op jit(solution)/shard_map/ppermute | solution.py:324
  161.3 14.9 %collective-permute-start.28 = (bf16[2,256,256]{2,1,0:T(8,128)(2,1)S(1)}, bf16[2,256,256]{2,1,0:T(8,128)(2,1)S(1)}, u32[]{:S(2)}, u32[]{:S(2)}) collective-permute-start(bf16[2,256,256]{2,1,0:T(8,128)(2,1)S(1)} %get-tuple-element.63), channel_id=1, source_target_pairs={{3,11},{7,15},{10,2},{11,3},{14,6},{15,7},{16,24},{17,25},{20,28},... | collective-permute-start | bytes 786440 | tf_op jit(solution)/shard_map/ppermute | solution.py:324
  161.9 21.5 %collective-permute-start.29 = (bf16[2,256,256]{2,1,0:T(8,128)(2,1)S(1)}, bf16[2,256,256]{2,1,0:T(8,128)(2,1)S(1)}, u32[]{:S(2)}, u32[]{:S(2)}) collective-permute-start(bf16[2,256,256]{2,1,0:T(8,128)(2,1)S(1)} %get-tuple-element.64), channel_id=1, source_target_pairs={{0,16},{4,20},{8,24},{9,25},{12,28},{13,29},{18,2},{19,3},{22,6},{... | collective-permute-start | bytes 786440 | tf_op jit(solution)/shard_map/ppermute | solution.py:324
  (10 other events, 74.9 us)

commit v3 on v2

--- a/solution.py
+++ b/solution.py
@@ -151,41 +151,48 @@
     )
 
 
-def far_body(s_ref, xa, xb, y0, y1, na, nb, rst, cst, own_ref, o1, o2, o3, xs, ys, *, total):
-    blk, jj = pl.program_id(0), pl.program_id(1)
+def pick_far(s_ref, xa, xb, xs):
+    @pl.when((pl.program_id(0) == 0) & (s_ref[LOW] == 0))
+    def _():
+        xs[...] = xa[...]
+
+    @pl.when((pl.program_id(0) == 0) & (s_ref[LOW] == 1))
+    def _():
+        xs[...] = xb[...]
+
+
+def put_far(s_ref, rst, cst, outs, xs, ys, total):
+    t = ys.shape[1] // 2
+    put_tiles(
+        lambda c: plain(xs[...], ys[:, c * t : c * t + t]),
+        lambda st: jnp.where(s_ref[LOW] == 0, st[2:3], st[3:4]),
+        s_ref, pl.program_id(0), 0, rst[0], cst[0], float(xs.shape[1]), total, outs[0], outs[1:],
+    )
+
+
+def far_body(s_ref, xa, xb, y0, y1, rst, cst, own_ref, o1, o2, o3, xs, ys, *, total):
     n = y0.shape[0]
-    t = y0.shape[1] // 2
-    low = s_ref[LOW]
-
-    @pl.when((jj == 0) & (blk == 0) & (low == 0))
-    def _():
-        xs[...] = xa[...]
-
-    @pl.when((jj == 0) & (blk == 0) & (low == 1))
-    def _():
-        xs[...] = xb[...]
-
-    other = (s_ref[CHIP] // 2) ^ jj
-
-    @pl.when(blk == 0)
-    def _():
-        ys[:n] = y0[...]
-        ys[n:] = y1[...]
-
-    @pl.when((blk == 1) & (other == 0))
+    pick_far(s_ref, xa, xb, xs)
+    ys[:n] = y0[...]
+    ys[n:] = y1[...]
+    put_far(s_ref, rst, cst, (own_ref, o1, o2, o3), xs, ys, total)
+
+
+def ends_body(s_ref, xa, xb, na, nb, rst, cst, own_ref, o1, o2, o3, xs, ys, *, total):
+    n = na.shape[0] // 2
+    pick_far(s_ref, xa, xb, xs)
+    other = (s_ref[CHIP] // 2) ^ pl.program_id(0)
+
+    @pl.when(other == 0)
     def _():
         ys[...] = na[...]
 
-    @pl.when((blk == 1) & (other == 1))
+    @pl.when(other == 1)
     def _():
         ys[:n] = nb[n:]
         ys[n:] = nb[:n]
 
-    put_tiles(
-        lambda c: plain(xs[...], ys[:, c * t : c * t + t]),
-        lambda st: jnp.where(low == 0, st[2:3], st[3:4]),
-        s_ref, jj, blk, rst[0], cst[0], 2.0 * n, total, own_ref, (o1, o2, o3),
-    )
+    put_far(s_ref, rst, cst, (own_ref, o1, o2, o3), xs, ys, total)
 
 
 CHIP, CORE, PLANE, PLANES, LOW, LOWER, _, SHIFT, EARLY = range(9)
@@ -280,10 +287,12 @@
 
 
 def pay_body(s_ref, a, *refs):
-    out_a, out_b = refs[-2:]
+    out_a, out_b, out_n = refs[-3:]
     n = a.shape[0] // 2
     out_a[...] = a[:n].T
     out_b[...] = a[n:].T
+    first = pl.multiple_of(jnp.where(s_ref[PLANE] == 0, n, 0), n)
+    out_n[...] = a[pl.ds(first, n)]
 
 
 def limit(mib):
@@ -345,7 +354,7 @@
     ).astype(jnp.int32)
 
     pay_in = pl.BlockSpec((rows, half), lambda i, sc: (0, sc[CORE]))
-    pay_shapes = [shape((half, rows), bf16)] * 2
+    pay_shapes = [shape((half, rows), bf16)] * 2 + [shape((rows, half), bf16)]
 
     def turn_payload(block, part, before):
         return pl.pallas_call(
@@ -354,7 +363,8 @@
                 num_scalar_prefetch=1,
                 grid=(1,),
                 in_specs=[pay_in] + [pl.BlockSpec(memory_space=pl.ANY)] * len(before),
-                out_specs=[pl.BlockSpec((half, half_cells), lambda i, sc: (0, part))] * 2,
+                out_specs=[pl.BlockSpec((half, half_cells), lambda i, sc: (0, part))] * 2
+                + [pl.BlockSpec((half_cells, half), lambda i, sc: (part, 0))],
             ),
             out_shape=pay_shapes,
             input_output_aliases={2 + n: n for n in range(len(before))},
@@ -362,14 +372,18 @@
             name="turn_payload",
         )(info, block, *before)
 
-    pay_a, pay_b = turn_payload(oth, 1, turn_payload(own, 0, []))
+    pay_a, pay_b, end = turn_payload(oth, 1, turn_payload(own, 0, []))
     up1 = send(pay_a, lambda k, h, g: (k, h, g + 1))
     dn1 = send(pay_b, lambda k, h, g: (k, h, g - 1))
     widened = own.astype(f32)
     halves = jnp.sum(widened.reshape(2, half_cells, width), axis=1)
     squares = jnp.sum(widened * widened, axis=0)
-    chip_halves = halves + send(halves, flip)
-    sums = lax.psum(jnp.stack([halves[0] + halves[1], squares]), "cells")
+    local = jnp.concatenate([halves, squares[None]])
+    chip = local + send(local, flip)
+    chip_halves = chip[:2]
+    pair = jnp.stack([chip[0] + chip[1], chip[2]])
+    around = [send(pair, lambda k, h, g, j=j: (k ^ j, h, g)) for j in (1, 2, 3)]
+    sums = (pair + around[0]) + (around[1] + around[2])
     means = sums[0] / total
     variances = sums[1] / total - means * means
     mine = jnp.concatenate(
@@ -378,8 +392,6 @@
     afar = [send(mine, lambda k, h, g, d=d: (k, h, g ^ d)) for d in (1, 2, 3)]
     own_stats = mine[None]
     stats = jnp.stack([mine] + afar)
-    corner = (jnp.where(g == 0, half_cells, 0), h * half)
-    end = jnp.concatenate([lax.dynamic_slice(a, corner, (half_cells, half)) for a in (own, oth)])
     near = send(
         end, lambda k, h, g: (k, h, 1) if g == 0 else ((k, h, g - 1) if g == last else None)
     )
@@ -446,30 +458,32 @@
         name="near_blocks",
     )(info, up1, dn1, own, oth, stats, stats)
 
-    n_spec = pl.BlockSpec((rows, half), lambda b, jj, sc: (0, 0))
-    y_spec = pl.BlockSpec((half_cells, half), lambda b, jj, sc: (sc[LOW], col(jj, sc)))
-    w2 = pl.pallas_call(
-        functools.partial(far_body, total=total),
-        grid_spec=pltpu.PrefetchScalarGridSpec(
-            num_scalar_prefetch=1,
-            grid=(2, 2),
-            in_specs=[
-                x_spec,
-                x_spec,
-                y_spec,
-                y_spec,
-                n_spec,
-                n_spec,
-                stat_spec(lambda b, jj, sc: (2, 0, sc[CORE])),
-                stat_spec(lambda b, jj, sc: (b, 0, col(jj, sc))),
-            ],
-            out_specs=block_outs(2),
-            scratch_shapes=scratch,
-        ),
-        out_shape=out_shapes(2),
-        compiler_params=limit(20),
-        name="far_blocks",
-    )(info, up2, dn2, own, oth, near, near_other, stats, stats)
+    x_spec = pl.BlockSpec((half, rows), lambda jj, sc: (0, 0))
+    n_spec = pl.BlockSpec((rows, half), lambda jj, sc: (0, 0))
+
+    def far_call(body, others, specs, plane):
+        return pl.pallas_call(
+            functools.partial(body, total=total),
+            grid_spec=pltpu.PrefetchScalarGridSpec(
+                num_scalar_prefetch=1,
+                grid=(2,),
+                in_specs=[x_spec, x_spec]
+                + specs
+                + [
+                    stat_spec(lambda jj, sc: (2, 0, sc[CORE])),
+                    stat_spec(lambda jj, sc: (plane, 0, col(jj, sc))),
+                ],
+                out_specs=block_outs(1),
+                scratch_shapes=scratch,
+            ),
+            out_shape=out_shapes(1),
+            compiler_params=limit(20),
+            name="far_block",
+        )(info, up2, dn2, *others, stats, stats)
+
+    y_spec = pl.BlockSpec((half_cells, half), lambda jj, sc: (sc[LOW], col(jj, sc)))
+    w2 = far_call(far_body, [own, oth], [y_spec] * 2, 0)
+    w3 = far_call(ends_body, [near, near_other], [n_spec] * 2, 1)
 
     def reduce_tiles(w):
         return [w[0]] + [send(w[j], lambda k, h, g, j=j: (k ^ j, h, g)) for j in (1, 2, 3)]
@@ -490,7 +504,8 @@
 
     (t0,) = turn(reduce_tiles(w0), [None], [None])
     t1, e_up, e_dn = turn(reduce_tiles(w1), [0, 1], [None, None])
-    t2, e_two, e_three, k_three = turn(reduce_tiles(w2), [0, 1], [None, 2])
+    t2, e_two = turn(reduce_tiles(w2), [0], [None])
+    _, e_three, k_three = turn(reduce_tiles(w3), [0], [1])
 
     side = lambda f: (lambda k, h, g: (k, h ^ (k // 2), f(g)) if f(g) is not None else None)
     rd = send(e_up, side(lambda g: g - 1))

time: 193 us -> 194 us (level)
  starting transfers between devices: 72.3 us -> 89.5 us
  blocking collectives: 14.6 us -> 0 us
    ppermute x34 -> x40, starting transfers between devices: 72.3 us -> 89.5 us  [send(): return lax.ppermute(x, AXES, perm(f))]
    psum x1 -> x0, blocking collectives: 14.6 us -> none  [folded_shards(): sums = lax.psum(jnp.stack([halves[0] + halves[1], squares]), 'cells')]
    reduce_sum x1, other arithmetic: 0.34 us -> 3.96 us  [folded_shards(): halves = jnp.sum(widened.reshape(2, half_cells, width), axis=1)]
    reduce_sum x1, other arithmetic: 4.08 us -> 0.48 us  [folded_shards(): squares = jnp.sum(widened * widened, axis=0)]
    ppermute x34 -> x40, waiting for transfers between devices: 61 us -> 62.9 us  [send(): return lax.ppermute(x, AXES, perm(f))]
    pallas_call x3 -> x4, Pallas kernels: 4.69 us -> 6.02 us  [turn(): pl.pallas_call(functools.partial(turn_body, turns=turns, keeps=keeps), in...]
    pallas_call x1 -> x2, Pallas kernels: 7.43 us -> 7.3 us  [far_call(): pl.pallas_call(functools.partial(body, total=total), grid_spec=pltpu.Pref...]
  transfers between devices with their start and end apart: 34 -> 40, of which waited for: 16 -> 17; matrix products, arithmetic and copies ran while one was open for 1% -> 0% of each run, Pallas kernels for 15% -> 15%
where the time goes in v3:
time: 194 us; the launch traced here: 193 us
  starting transfers between devices  89.5 us (46%)
  waiting for transfers between devices  62.9 us (32%)
  Pallas kernels  33.6 us (17%)
  other arithmetic  6.02 us (3%)
    ppermute x40, starting transfers between devices, send(): return lax.ppermute(x, AXES, perm(f))  89.5 us
    ppermute x40, waiting for transfers between devices, send(): return lax.ppermute(x, AXES, perm(f))  62.9 us
    pallas_call x2, Pallas kernels, far_call(): pl.pallas_call(functools.partial(body, total=total), grid_spec=pltpu.Pref...  7.3 us
    pallas_call x1, Pallas kernels, folded_shards(): pl.pallas_call(functools.partial(near_body, total=total), grid_spec=pltpu...  6.77 us
    pallas_call x4, Pallas kernels, turn(): pl.pallas_call(functools.partial(turn_body, turns=turns, keeps=keeps), in...  6.02 us
    pallas_call x1, Pallas kernels, folded_shards(): pl.pallas_call(functools.partial(diagonal_body, total=total), grid_spec=p...  5.44 us
    reduce_sum x1, other arithmetic, folded_shards(): halves = jnp.sum(widened.reshape(2, half_cells, width), axis=1)  3.96 us
  transfers between devices with their start and end apart: 40, of which 17 were waited for; matrix products, arithmetic and copies ran while one was open for 0% of the time, Pallas kernels for 15%

profile of v3, /device:TPU:0, one launch (start us, length us, event | category | flops | bytes accessed | tf_op | source)
XLA Modules:
  0.0 193.2 jit_solution(10394644918638158413)
XLA Ops:
  1.3 4.0 %bitcast_reduce_fusion = (f32[2,1024]{1,0:T(2,128)S(1)}, bf16[1024,1024]{1,0:T(8,128)(2,1)S(1)}) fusion(f32[1024]{0:T(1024)S(1)} %convert_divide_fusion, s32[1024,1024]{1,0:T(8,128)} %param.2), kind=kLoop, calls=%fused_computation | loop fusion | flops 5240832 | bytes 6303744 | tf_op jit(solution)/shard_map/reduce_sum | solution.py:379
  6.9 2.8 %collective-permute-done.a.y1 = bf16[1024,1024]{1,0:T(8,128)(2,1)} collective-permute-done((bf16[1024,1024]{1,0:T(8,128)(2,1)S(1)}, bf16[1024,1024]{1,0:T(8,128)(2,1)}, u32[]{:S(2)}, u32[]{:S(2)}) %collective-permute-start) | collective-permute-done | bytes 2097184 | tf_op jit(solution)/shard_map/ppermute | solution.py:333
  9.8 2.1 %turn_payload.3 = (bf16[512,1024]{1,0:T(8,128)(2,1)S(1)}, bf16[512,1024]{1,0:T(8,128)(2,1)S(1)}, bf16[1024,512]{1,0:T(8,128)(2,1)S(1)}) custom-call(s32[9]{0:T(128)S(1)} %stack.60.s_ref, bf16[1024,1024]{1,0:T(8,128)(2,1)} %collective-permute-done.a.y1, ...), custom_call_target="tpu_custom_call", output_to_operand_aliasing={{0}: (2, {}), {1}: (3, {}), {2}: (4, {})} | custom-call | tf_op jit(solution)/shard_map/turn_payload/pallas_call | solution.py:360
  11.9 4.9 %collective-permute-start.8 = (bf16[512,1024]{1,0:T(8,128)(2,1)S(1)}, bf16[512,1024]{1,0:T(8,128)(2,1)S(1)}, u32[]{:S(2)}, u32[]{:S(2)}) collective-permute-start(bf16[512,1024]{1,0:T(8,128)(2,1)S(1)} %get-tuple-element.44.xa), channel_id=1, source_target_pairs={{0,1},{1,2},{2,3},{4,5},{5,6},{6,7},{8,9},{9,10},{10,11},{12,13},{... | collective-permute-start | bytes 3145736 | tf_op jit(solution)/shard_map/ppermute | solution.py:333
  18.1 4.6 %collective-permute-start.27 = (bf16[1024,512]{1,0:T(8,128)(2,1)S(1)}, bf16[1024,512]{1,0:T(8,128)(2,1)S(1)}, u32[]{:S(2)}, u32[]{:S(2)}) collective-permute-start(bf16[1024,512]{1,0:T(8,128)(2,1)S(1)} %get-tuple-element.67), channel_id=1, source_target_pairs={{0,1},{3,2},{4,5},{7,6},{8,9},{11,10},{12,13},{15,14},{16,17},{19,... | collective-permute-start | bytes 3145736 | tf_op jit(solution)/shard_map/ppermute | solution.py:333
  24.5 15.8 %collective-permute-done.8.xa = bf16[512,1024]{1,0:T(8,128)(2,1)S(1)} collective-permute-done((bf16[512,1024]{1,0:T(8,128)(2,1)S(1)}, bf16[512,1024]{1,0:T(8,128)(2,1)S(1)}, u32[]{:S(2)}, u32[]{:S(2)}) %collective-permute-start.8) | collective-permute-done | bytes 1048608 | tf_op jit(solution)/shard_map/ppermute | solution.py:333
  48.4 13.5 %collective-permute-done.27.na = bf16[1024,512]{1,0:T(8,128)(2,1)S(1)} collective-permute-done((bf16[1024,512]{1,0:T(8,128)(2,1)S(1)}, bf16[1024,512]{1,0:T(8,128)(2,1)S(1)}, u32[]{:S(2)}, u32[]{:S(2)}) %collective-permute-start.27) | collective-permute-done | bytes 1048608 | tf_op jit(solution)/shard_map/ppermute | solution.py:333
  62.0 5.7 %collective-permute-start.12 = (f32[8,1024]{1,0:T(8,128)S(1)}, f32[8,1024]{1,0:T(8,128)S(1)}, u32[]{:S(2)}, u32[]{:S(2)}) collective-permute-start(f32[8,1024]{1,0:T(8,128)S(1)} %get-tuple-element.82), channel_id=1, source_target_pairs={{0,3},{1,2},{2,1},{3,0},{4,7},{5,6},{6,5},{7,4},{8,11},{9,10},{10,... | collective-permute-start | bytes 98312 | tf_op jit(solution)/shard_map/ppermute | solution.py:333
  69.9 8.2 %collective-permute-start.10 = (f32[8,1024]{1,0:T(8,128)S(1)}, f32[8,1024]{1,0:T(8,128)S(1)}, u32[]{:S(2)}, u32[]{:S(2)}) collective-permute-start(f32[8,1024]{1,0:T(8,128)S(1)} %get-tuple-element.82), channel_id=1, source_target_pairs={{0,1},{1,0},{2,3},{3,2},{4,5},{5,4},{6,7},{7,6},{8,9},{9,8},{10,11... | collective-permute-start | bytes 98312 | tf_op jit(solution)/shard_map/ppermute | solution.py:333
  80.0 6.8 %near_blocks.1 = (f32[2,2,256,256]{3,2,1,0:T(8,128)S(1)}, bf16[2,2,256,256]{3,2,1,0:T(8,128)(2,1)S(1)}, bf16[2,2,256,256]{3,2,1,0:T(8,128)(2,1)S(1)}, bf16[2,2,256,256]{3,2,1,0:T(8,128)(2,1)S(1)}) custom-call(s32[9]{0:T(128)S(1)} %stack.60.s_ref, bf16[512,1024]{1,0:T(8,128)(2,1)S(1)} %collective-permute-done.8.xa, ...), custom_call_target="tpu_custom_call" | custom-call | tf_op jit(solution)/shard_map/near_blocks/pallas_call | solution.py:440
  90.3 4.1 %far_block.2 = (f32[1,2,256,256]{3,2,1,0:T(8,128)S(1)}, bf16[1,2,256,256]{3,2,1,0:T(8,128)(2,1)S(1)}, bf16[1,2,256,256]{3,2,1,0:T(8,128)(2,1)S(1)}, bf16[1,2,256,256]{3,2,1,0:T(8,128)(2,1)S(1)}) custom-call(s32[9]{0:T(128)S(1)} %stack.60.s_ref, bf16[512,1024]{1,0:T(8,128)(2,1)S(1)} %collective-permute-done.21.xa, ...), custom_call_target="tpu_custom_call" | custom-call | tf_op jit(solution)/shard_map/far_block/pallas_call | solution.py:465
  96.6 3.2 %far_block.3 = (f32[1,2,256,256]{3,2,1,0:T(8,128)S(1)}, bf16[1,2,256,256]{3,2,1,0:T(8,128)(2,1)S(1)}, bf16[1,2,256,256]{3,2,1,0:T(8,128)(2,1)S(1)}, bf16[1,2,256,256]{3,2,1,0:T(8,128)(2,1)S(1)}) custom-call(s32[9]{0:T(128)S(1)} %stack.60.s_ref, bf16[512,1024]{1,0:T(8,128)(2,1)S(1)} %collective-permute-done.21.xa, ...), custom_call_target="tpu_custom_call" | custom-call | tf_op jit(solution)/shard_map/far_block/pallas_call | solution.py:465
  103.1 10.9 %collective-permute-done.14.r2 = bf16[2,2,256,256]{3,2,1,0:T(8,128)(2,1)S(1)} collective-permute-done((bf16[2,2,256,256]{3,2,1,0:T(8,128)(2,1)S(1)}, bf16[2,2,256,256]{3,2,1,0:T(8,128)(2,1)S(1)}, u32[]{:S(2)}, u32[]{:S(2)}) %collective-permute-start.14) | collective-permute-done | bytes 524320 | tf_op jit(solution)/shard_map/ppermute | solution.py:333
  114.0 3.0 %collective-permute-start.29 = (bf16[1,2,256,256]{3,2,1,0:T(8,128)(2,1)S(1)}, bf16[1,2,256,256]{3,2,1,0:T(8,128)(2,1)S(1)}, u32[]{:S(2)}, u32[]{:S(2)}) collective-permute-start(bf16[1,2,256,256]{3,2,1,0:T(8,128)(2,1)S(1)} %get-tuple-element.69), channel_id=1, source_target_pairs={{0,8},{1,9},{2,10},{3,11},{4,12},{5,13},{6,14},{7,15},{8,0},{9,1},... | collective-permute-start | bytes 786440 | tf_op jit(solution)/shard_map/ppermute | solution.py:333
  120.0 5.4 %diagonal_block.1 = (f32[1,2,256,256]{3,2,1,0:T(8,128)S(1)}, bf16[1,2,256,256]{3,2,1,0:T(8,128)(2,1)S(1)}, bf16[1,2,256,256]{3,2,1,0:T(8,128)(2,1)S(1)}, bf16[1,2,256,256]{3,2,1,0:T(8,128)(2,1)S(1)}) custom-call(s32[9]{0:T(128)S(1)} %stack.60.s_ref, bf16[512,1024]{1,0:T(8,128)(2,1)S(1)} %get-tuple-element.44.xa, bf16[512,1024]{1,0:T(8,128)(2,1)S(1)} %get-tuple-element.45.xb, ...), custom_call_target="tpu_custom_call" | custom-call | tf_op jit(solution)/shard_map/diagonal_block/pallas_call | solution.py:412
  131.5 4.0 %collective-permute-start.16 = (bf16[2,256,256]{2,1,0:T(8,128)(2,1)S(1)}, bf16[2,256,256]{2,1,0:T(8,128)(2,1)S(1)}, u32[]{:S(2)}, u32[]{:S(2)}) collective-permute-start(bf16[2,256,256]{2,1,0:T(8,128)(2,1)S(1)} %get-tuple-element.55), channel_id=1, source_target_pairs={{0,1},{1,2},{2,3},{4,5},{5,6},{6,7},{8,9},{9,10},{10,11},{12,13},{... | collective-permute-start | bytes 786440 | tf_op jit(solution)/shard_map/ppermute | solution.py:333
  138.9 2.0 %sum_tiles.7 = (f32[1,2,256,256]{3,2,1,0:T(8,128)}, bf16[2,256,256]{2,1,0:T(8,128)(2,1)S(1)}, bf16[2,256,256]{2,1,0:T(8,128)(2,1)S(1)}) custom-call(s32[9]{0:T(128)S(1)} %stack.60.s_ref, f32[1,2,256,256]{3,2,1,0:T(8,128)S(1)} %get-tuple-element.68.own, bf16[1,2,256,256]{3,2,1,0:T(8,128)(2,1)S(1)} %collective-permute-done.29.r1, ...), custom_call_target="tpu_custom_call" | custom-call | tf_op jit(solution)/shard_map/sum_tiles/pallas_call | solution.py:496
  140.9 5.9 %collective-permute-start.26 = (bf16[2,256,256]{2,1,0:T(8,128)(2,1)S(1)}, bf16[2,256,256]{2,1,0:T(8,128)(2,1)S(1)}, u32[]{:S(2)}, u32[]{:S(2)}) collective-permute-start(bf16[2,256,256]{2,1,0:T(8,128)(2,1)S(1)} %get-tuple-element.66), channel_id=1, source_target_pairs={{0,2},{1,3},{2,0},{3,1},{4,6},{5,7},{6,4},{7,5},{8,10},{9,11},{10,... | collective-permute-start | bytes 786440 | tf_op jit(solution)/shard_map/ppermute | solution.py:333
  151.6 3.2 %collective-permute-start.18 = (bf16[2,256,256]{2,1,0:T(8,128)(2,1)S(1)}, bf16[2,256,256]{2,1,0:T(8,128)(2,1)S(1)}, u32[]{:S(2)}, u32[]{:S(2)}) collective-permute-start(bf16[2,256,256]{2,1,0:T(8,128)(2,1)S(1)} %get-tuple-element.58), channel_id=1, source_target_pairs={{0,8},{1,9},{2,10},{4,12},{5,13},{6,14},{8,0},{9,1},{12,4},{13,5},... | collective-permute-start | bytes 786440 | tf_op jit(solution)/shard_map/ppermute | solution.py:333
  157.4 2.1 %collective-permute-done.33.rn = bf16[2,256,256]{2,1,0:T(8,128)(2,1)S(1)} collective-permute-done((bf16[2,256,256]{2,1,0:T(8,128)(2,1)S(1)}, bf16[2,256,256]{2,1,0:T(8,128)(2,1)S(1)}, u32[]{:S(2)}, u32[]{:S(2)}) %collective-permute-start.33) | collective-permute-done | bytes 262176 | tf_op jit(solution)/shard_map/ppermute | solution.py:333
  161.5 14.8 %collective-permute-start.35 = (bf16[2,256,256]{2,1,0:T(8,128)(2,1)S(1)}, bf16[2,256,256]{2,1,0:T(8,128)(2,1)S(1)}, u32[]{:S(2)}, u32[]{:S(2)}) collective-permute-start(bf16[2,256,256]{2,1,0:T(8,128)(2,1)S(1)} %get-tuple-element.76), channel_id=1, source_target_pairs={{0,16},{4,20},{8,24},{9,25},{12,28},{13,29},{18,2},{19,3},{22,6},{... | collective-permute-start | bytes 786440 | tf_op jit(solution)/shard_map/ppermute | solution.py:333
  177.6 7.0 %collective-permute-done.35.l2 = bf16[2,256,256]{2,1,0:T(8,128)(2,1)S(1)} collective-permute-done((bf16[2,256,256]{2,1,0:T(8,128)(2,1)S(1)}, bf16[2,256,256]{2,1,0:T(8,128)(2,1)S(1)}, u32[]{:S(2)}, u32[]{:S(2)}) %collective-permute-start.35) | collective-permute-done | bytes 262176 | tf_op jit(solution)/shard_map/ppermute | solution.py:333
  184.6 2.3 %place_tiles.1 = (f32[512,1024]{1,0:T(8,128)}, f32[512,1]{1,0:T(8,128)S(1)}) custom-call(s32[9]{0:T(128)S(1)} %stack.60.s_ref, bf16[2,256,256]{2,1,0:T(8,128)(2,1)S(1)} %get-tuple-element.57.e0, bf16[2,256,256]{2,1,0:T(8,128)(2,1)S(1)} %collective-permute-done.18.e1, bf16[2,256,256]{2,1,0:T(8,128)(2,1)S(1)} %collective-permute-done.19.e2, ...), custom_call_target="tpu_custom_call" | custom-call | tf_op jit(solution)/shard_map/place_tiles/pallas_call | solution.py:544
  187.7 2.9 %collective-permute-start.37 = (f32[512]{0:T(512)S(1)}, f32[512]{0:T(512)S(1)}, u32[]{:S(2)}, u32[]{:S(2)}) collective-permute-start(f32[512]{0:T(512)S(1)} %reduce), channel_id=1, source_target_pairs={{0,1},{1,0},{2,3},{3,2},{4,5},{5,4},{6,7},{7,6},{8,9},{9,8},{10,11... | collective-permute-start | bytes 6152 | tf_op jit(solution)/shard_map/ppermute | solution.py:333
  (86 shorter events, 53.1 us)
Async XLA Ops:
  11.9 28.4 %collective-permute-start.8 = (bf16[512,1024]{1,0:T(8,128)(2,1)S(1)}, bf16[512,1024]{1,0:T(8,128)(2,1)S(1)}, u32[]{:S(2)}, u32[]{:S(2)}) collective-permute-start(bf16[512,1024]{1,0:T(8,128)(2,1)S(1)} %get-tuple-element.44.xa), channel_id=1, source_target_pairs={{0,1},{1,2},{2,3},{4,5},{5,6},{6,7},{8,9},{9,10},{10,11},{12,13},{... | collective-permute-start | bytes 3145736 | tf_op jit(solution)/shard_map/ppermute | solution.py:333
  16.8 29.5 %collective-permute-start.9 = (bf16[512,1024]{1,0:T(8,128)(2,1)S(1)}, bf16[512,1024]{1,0:T(8,128)(2,1)S(1)}, u32[]{:S(2)}, u32[]{:S(2)}) collective-permute-start(bf16[512,1024]{1,0:T(8,128)(2,1)S(1)} %get-tuple-element.45.xb), channel_id=1, source_target_pairs={{1,0},{2,1},{3,2},{5,4},{6,5},{7,6},{9,8},{10,9},{11,10},{13,12},{... | collective-permute-start | bytes 3145736 | tf_op jit(solution)/shard_map/ppermute | solution.py:333
  18.1 43.8 %collective-permute-start.27 = (bf16[1024,512]{1,0:T(8,128)(2,1)S(1)}, bf16[1024,512]{1,0:T(8,128)(2,1)S(1)}, u32[]{:S(2)}, u32[]{:S(2)}) collective-permute-start(bf16[1024,512]{1,0:T(8,128)(2,1)S(1)} %get-tuple-element.67), channel_id=1, source_target_pairs={{0,1},{3,2},{4,5},{7,6},{8,9},{11,10},{12,13},{15,14},{16,17},{19,... | collective-permute-start | bytes 3145736 | tf_op jit(solution)/shard_map/ppermute | solution.py:333
  40.3 48.6 %collective-permute-start.21 = (bf16[512,1024]{1,0:T(8,128)(2,1)S(1)}, bf16[512,1024]{1,0:T(8,128)(2,1)S(1)}, u32[]{:S(2)}, u32[]{:S(2)}) collective-permute-start(bf16[512,1024]{1,0:T(8,128)(2,1)S(1)} %collective-permute-done.8.xa), channel_id=1, source_target_pairs={{1,2},{2,3},{5,6},{6,7},{9,10},{10,11},{13,14},{14,15},{17,18},{18... | collective-permute-start | bytes 3145736 | tf_op jit(solution)/shard_map/ppermute | solution.py:333
  46.3 44.0 %collective-permute-start.22 = (bf16[512,1024]{1,0:T(8,128)(2,1)S(1)}, bf16[512,1024]{1,0:T(8,128)(2,1)S(1)}, u32[]{:S(2)}, u32[]{:S(2)}) collective-permute-start(bf16[512,1024]{1,0:T(8,128)(2,1)S(1)} %collective-permute-done.9.xb), channel_id=1, source_target_pairs={{1,0},{2,1},{5,4},{6,5},{9,8},{10,9},{13,12},{14,13},{17,16},{18,1... | collective-permute-start | bytes 3145736 | tf_op jit(solution)/shard_map/ppermute | solution.py:333
  61.9 33.1 %collective-permute-start.28 = (bf16[1024,512]{1,0:T(8,128)(2,1)S(1)}, bf16[1024,512]{1,0:T(8,128)(2,1)S(1)}, u32[]{:S(2)}, u32[]{:S(2)}) collective-permute-start(bf16[1024,512]{1,0:T(8,128)(2,1)S(1)} %collective-permute-done.27.na), channel_id=1, source_target_pairs={{0,4},{1,5},{2,6},{3,7},{4,0},{5,1},{6,2},{7,3},{8,12},{9,13},{10,... | collective-permute-start | bytes 3145736 | tf_op jit(solution)/shard_map/ppermute | solution.py:333
  86.8 14.9 %collective-permute-start.13 = (bf16[2,2,256,256]{3,2,1,0:T(8,128)(2,1)S(1)}, bf16[2,2,256,256]{3,2,1,0:T(8,128)(2,1)S(1)}, u32[]{:S(2)}, u32[]{:S(2)}) collective-permute-start(bf16[2,2,256,256]{3,2,1,0:T(8,128)(2,1)S(1)} %get-tuple-element.51), channel_id=1, source_target_pairs={{0,8},{1,9},{2,10},{3,11},{4,12},{5,13},{6,14},{7,15},{8,0},{9,1},... | collective-permute-start | bytes 1572872 | tf_op jit(solution)/shard_map/ppermute | solution.py:333
  87.4 26.7 %collective-permute-start.14 = (bf16[2,2,256,256]{3,2,1,0:T(8,128)(2,1)S(1)}, bf16[2,2,256,256]{3,2,1,0:T(8,128)(2,1)S(1)}, u32[]{:S(2)}, u32[]{:S(2)}) collective-permute-start(bf16[2,2,256,256]{3,2,1,0:T(8,128)(2,1)S(1)} %get-tuple-element.52), channel_id=1, source_target_pairs={{0,16},{1,17},{2,18},{3,19},{4,20},{5,21},{6,22},{7,23},{8,24},{9,... | collective-permute-start | bytes 1572872 | tf_op jit(solution)/shard_map/ppermute | solution.py:333
  88.9 28.1 %collective-permute-start.15 = (bf16[2,2,256,256]{3,2,1,0:T(8,128)(2,1)S(1)}, bf16[2,2,256,256]{3,2,1,0:T(8,128)(2,1)S(1)}, u32[]{:S(2)}, u32[]{:S(2)}) collective-permute-start(bf16[2,2,256,256]{3,2,1,0:T(8,128)(2,1)S(1)} %get-tuple-element.53), channel_id=1, source_target_pairs={{0,24},{1,25},{2,26},{3,27},{4,28},{5,29},{6,30},{7,31},{8,16},{9,... | collective-permute-start | bytes 1572872 | tf_op jit(solution)/shard_map/ppermute | solution.py:333
  94.5 24.2 %collective-permute-start.23 = (bf16[1,2,256,256]{3,2,1,0:T(8,128)(2,1)S(1)}, bf16[1,2,256,256]{3,2,1,0:T(8,128)(2,1)S(1)}, u32[]{:S(2)}, u32[]{:S(2)}) collective-permute-start(bf16[1,2,256,256]{3,2,1,0:T(8,128)(2,1)S(1)} %get-tuple-element.62), channel_id=1, source_target_pairs={{0,8},{1,9},{2,10},{3,11},{4,12},{5,13},{6,14},{7,15},{8,0},{9,1},... | collective-permute-start | bytes 786440 | tf_op jit(solution)/shard_map/ppermute | solution.py:333
  95.1 32.3 %collective-permute-start.24 = (bf16[1,2,256,256]{3,2,1,0:T(8,128)(2,1)S(1)}, bf16[1,2,256,256]{3,2,1,0:T(8,128)(2,1)S(1)}, u32[]{:S(2)}, u32[]{:S(2)}) collective-permute-start(bf16[1,2,256,256]{3,2,1,0:T(8,128)(2,1)S(1)} %get-tuple-element.63), channel_id=1, source_target_pairs={{0,16},{1,17},{2,18},{3,19},{4,20},{5,21},{6,22},{7,23},{8,24},{9,... | collective-permute-start | bytes 786440 | tf_op jit(solution)/shard_map/ppermute | solution.py:333
  101.6 27.3 %collective-permute-start.25 = (bf16[1,2,256,256]{3,2,1,0:T(8,128)(2,1)S(1)}, bf16[1,2,256,256]{3,2,1,0:T(8,128)(2,1)S(1)}, u32[]{:S(2)}, u32[]{:S(2)}) collective-permute-start(bf16[1,2,256,256]{3,2,1,0:T(8,128)(2,1)S(1)} %get-tuple-element.64), channel_id=1, source_target_pairs={{0,24},{1,25},{2,26},{3,27},{4,28},{5,29},{6,30},{7,31},{8,16},{9,... | collective-permute-start | bytes 786440 | tf_op jit(solution)/shard_map/ppermute | solution.py:333
  114.0 15.7 %collective-permute-start.29 = (bf16[1,2,256,256]{3,2,1,0:T(8,128)(2,1)S(1)}, bf16[1,2,256,256]{3,2,1,0:T(8,128)(2,1)S(1)}, u32[]{:S(2)}, u32[]{:S(2)}) collective-permute-start(bf16[1,2,256,256]{3,2,1,0:T(8,128)(2,1)S(1)} %get-tuple-element.69), channel_id=1, source_target_pairs={{0,8},{1,9},{2,10},{3,11},{4,12},{5,13},{6,14},{7,15},{8,0},{9,1},... | collective-permute-start | bytes 786440 | tf_op jit(solution)/shard_map/ppermute | solution.py:333
  117.0 14.5 %collective-permute-start.30 = (bf16[1,2,256,256]{3,2,1,0:T(8,128)(2,1)S(1)}, bf16[1,2,256,256]{3,2,1,0:T(8,128)(2,1)S(1)}, u32[]{:S(2)}, u32[]{:S(2)}) collective-permute-start(bf16[1,2,256,256]{3,2,1,0:T(8,128)(2,1)S(1)} %get-tuple-element.70), channel_id=1, source_target_pairs={{0,16},{1,17},{2,18},{3,19},{4,20},{5,21},{6,22},{7,23},{8,24},{9,... | collective-permute-start | bytes 786440 | tf_op jit(solution)/shard_map/ppermute | solution.py:333
  118.6 17.8 %collective-permute-start.31 = (bf16[1,2,256,256]{3,2,1,0:T(8,128)(2,1)S(1)}, bf16[1,2,256,256]{3,2,1,0:T(8,128)(2,1)S(1)}, u32[]{:S(2)}, u32[]{:S(2)}) collective-permute-start(bf16[1,2,256,256]{3,2,1,0:T(8,128)(2,1)S(1)} %get-tuple-element.71), channel_id=1, source_target_pairs={{0,24},{1,25},{2,26},{3,27},{4,28},{5,29},{6,30},{7,31},{8,16},{9,... | collective-permute-start | bytes 786440 | tf_op jit(solution)/shard_map/ppermute | solution.py:333
  128.9 17.8 %collective-permute-start.6 = (bf16[1,2,256,256]{3,2,1,0:T(8,128)(2,1)S(1)}, bf16[1,2,256,256]{3,2,1,0:T(8,128)(2,1)S(1)}, u32[]{:S(2)}, u32[]{:S(2)}) collective-permute-start(bf16[1,2,256,256]{3,2,1,0:T(8,128)(2,1)S(1)} %get-tuple-element.48), channel_id=1, source_target_pairs={{0,16},{1,17},{2,18},{3,19},{4,20},{5,21},{6,22},{7,23},{8,24},{9,... | collective-permute-start | bytes 786440 | tf_op jit(solution)/shard_map/ppermute | solution.py:333
  129.8 18.2 %collective-permute-start.7 = (bf16[1,2,256,256]{3,2,1,0:T(8,128)(2,1)S(1)}, bf16[1,2,256,256]{3,2,1,0:T(8,128)(2,1)S(1)}, u32[]{:S(2)}, u32[]{:S(2)}) collective-permute-start(bf16[1,2,256,256]{3,2,1,0:T(8,128)(2,1)S(1)} %get-tuple-element.49), channel_id=1, source_target_pairs={{0,24},{1,25},{2,26},{3,27},{4,28},{5,29},{6,30},{7,31},{8,16},{9,... | collective-permute-start | bytes 786440 | tf_op jit(solution)/shard_map/ppermute | solution.py:333
  131.5 18.8 %collective-permute-start.16 = (bf16[2,256,256]{2,1,0:T(8,128)(2,1)S(1)}, bf16[2,256,256]{2,1,0:T(8,128)(2,1)S(1)}, u32[]{:S(2)}, u32[]{:S(2)}) collective-permute-start(bf16[2,256,256]{2,1,0:T(8,128)(2,1)S(1)} %get-tuple-element.55), channel_id=1, source_target_pairs={{0,1},{1,2},{2,3},{4,5},{5,6},{6,7},{8,9},{9,10},{10,11},{12,13},{... | collective-permute-start | bytes 786440 | tf_op jit(solution)/shard_map/ppermute | solution.py:333
  140.9 15.2 %collective-permute-start.26 = (bf16[2,256,256]{2,1,0:T(8,128)(2,1)S(1)}, bf16[2,256,256]{2,1,0:T(8,128)(2,1)S(1)}, u32[]{:S(2)}, u32[]{:S(2)}) collective-permute-start(bf16[2,256,256]{2,1,0:T(8,128)(2,1)S(1)} %get-tuple-element.66), channel_id=1, source_target_pairs={{0,2},{1,3},{2,0},{3,1},{4,6},{5,7},{6,4},{7,5},{8,10},{9,11},{10,... | collective-permute-start | bytes 786440 | tf_op jit(solution)/shard_map/ppermute | solution.py:333
  151.6 24.7 %collective-permute-start.18 = (bf16[2,256,256]{2,1,0:T(8,128)(2,1)S(1)}, bf16[2,256,256]{2,1,0:T(8,128)(2,1)S(1)}, u32[]{:S(2)}, u32[]{:S(2)}) collective-permute-start(bf16[2,256,256]{2,1,0:T(8,128)(2,1)S(1)} %get-tuple-element.58), channel_id=1, source_target_pairs={{0,8},{1,9},{2,10},{4,12},{5,13},{6,14},{8,0},{9,1},{12,4},{13,5},... | collective-permute-start | bytes 786440 | tf_op jit(solution)/shard_map/ppermute | solution.py:333
  154.8 22.8 %collective-permute-start.19 = (bf16[2,256,256]{2,1,0:T(8,128)(2,1)S(1)}, bf16[2,256,256]{2,1,0:T(8,128)(2,1)S(1)}, u32[]{:S(2)}, u32[]{:S(2)}) collective-permute-start(bf16[2,256,256]{2,1,0:T(8,128)(2,1)S(1)} %get-tuple-element.59), channel_id=1, source_target_pairs={{1,17},{2,18},{3,19},{5,21},{6,22},{7,23},{10,26},{11,27},{14,30},... | collective-permute-start | bytes 786440 | tf_op jit(solution)/shard_map/ppermute | solution.py:333
  156.1 21.5 %collective-permute-start.20 = (bf16[2,256,256]{2,1,0:T(8,128)(2,1)S(1)}, bf16[2,256,256]{2,1,0:T(8,128)(2,1)S(1)}, u32[]{:S(2)}, u32[]{:S(2)}) collective-permute-start(bf16[2,256,256]{2,1,0:T(8,128)(2,1)S(1)} %get-tuple-element.60), channel_id=1, source_target_pairs={{2,26},{3,27},{6,30},{7,31},{9,17},{10,18},{11,19},{13,21},{14,22}... | collective-permute-start | bytes 786440 | tf_op jit(solution)/shard_map/ppermute | solution.py:333
  160.8 16.8 %collective-permute-start.34 = (bf16[2,256,256]{2,1,0:T(8,128)(2,1)S(1)}, bf16[2,256,256]{2,1,0:T(8,128)(2,1)S(1)}, u32[]{:S(2)}, u32[]{:S(2)}) collective-permute-start(bf16[2,256,256]{2,1,0:T(8,128)(2,1)S(1)} %get-tuple-element.75), channel_id=1, source_target_pairs={{3,11},{7,15},{10,2},{11,3},{14,6},{15,7},{16,24},{17,25},{20,28},... | collective-permute-start | bytes 786440 | tf_op jit(solution)/shard_map/ppermute | solution.py:333
  161.5 23.1 %collective-permute-start.35 = (bf16[2,256,256]{2,1,0:T(8,128)(2,1)S(1)}, bf16[2,256,256]{2,1,0:T(8,128)(2,1)S(1)}, u32[]{:S(2)}, u32[]{:S(2)}) collective-permute-start(bf16[2,256,256]{2,1,0:T(8,128)(2,1)S(1)} %get-tuple-element.76), channel_id=1, source_target_pairs={{0,16},{4,20},{8,24},{9,25},{12,28},{13,29},{18,2},{19,3},{22,6},{... | collective-permute-start | bytes 786440 | tf_op jit(solution)/shard_map/ppermute | solution.py:333
  (16 other events, 119.2 us)

commit v4 on v3

v4 whole, which is shorter than its diff:
```python
import functools

import jax
import jax.numpy as jnp
from jax import lax
from jax.experimental import pallas as pl
from jax.experimental.pallas import tpu as pltpu
from jax.sharding import PartitionSpec as P


AXES = ("cells", "genes")


def normalize(counts, library):
    factor = 10000.0 / library.astype(jnp.float32)
    return jnp.log1p(counts.astype(jnp.float32) * factor[:, None]).astype(jnp.bfloat16)


def cross_product(left, right):
    return lax.dot_general(
        left, right, (((0,), (0,)), ((), ())), preferred_element_type=jnp.float32
    )


def general_shards(counts, library):
    own_block = normalize(counts, library)
    col_width = own_block.shape[1]
    cell_groups = lax.axis_size("cells")
    gene_total = col_width * lax.axis_size("genes")
    row_width = gene_total // cell_groups
    total_cells = float(counts.shape[0] * cell_groups)
    widened = own_block.astype(jnp.float32)
    local_sums = jnp.sum(widened, axis=0)
    local_squares = jnp.sum(widened * widened, axis=0)
    block_sums, block_squares = lax.psum((local_sums, local_squares), "cells")
    gene_sums, gene_squares = (
        lax.all_gather(block_sums, "genes", axis=0, tiled=True),
        lax.all_gather(block_squares, "genes", axis=0, tiled=True),
    )
    full_block = lax.all_gather(own_block, "genes", axis=1, tiled=True)
    gram_tile = lax.psum_scatter(
        cross_product(full_block, own_block), "cells", scatter_dimension=0, tiled=True
    )
    means = gene_sums / total_cells
    variances = gene_squares / total_cells - means * means
    scales = lax.rsqrt(variances + 1e-05)
    row_first = lax.axis_index("cells") * row_width
    col_first = lax.axis_index("genes") * col_width
    row_means = lax.dynamic_slice_in_dim(means, row_first, row_width, 0)
    col_means = lax.dynamic_slice_in_dim(means, col_first, col_width, 0)
    row_scales = lax.dynamic_slice_in_dim(scales, row_first, row_width, 0)
    col_scales = lax.dynamic_slice_in_dim(scales, col_first, col_width, 0)
    correlation = (
        (gram_tile / total_cells - row_means[:, None] * col_means[None, :])
        * row_scales[:, None]
        * col_scales[None, :]
    )
    powered = correlation**6
    row_index = row_first + jnp.arange(row_width, dtype=jnp.int32)[:, None]
    col_index = col_first + jnp.arange(col_width, dtype=jnp.int32)[None, :]
    adjacency = jnp.where(row_index == col_index, jnp.float32(0.0), powered)
    connectivity = lax.psum(jnp.sum(adjacency, axis=1), "genes")
    return (adjacency, connectivity)


def encode(x):
    return (x * jnp.abs(x) * (x * x)).astype(jnp.bfloat16)


def decode(y):
    y = y.astype(jnp.float32)
    root = lax.rsqrt(lax.rsqrt(jnp.abs(y)))
    return jnp.where(y < 0, -root, root)


def plain(left, right):
    return jnp.dot(left, right, preferred_element_type=jnp.float32)


def put_tiles(product, sums, s_ref, blk, rst, cst, cells, total, outs):
    odd = s_ref[CHIP] % 2
    row_side = jnp.concatenate([rst, jnp.broadcast_to(sums(rst), rst.shape)]).T
    mr, sr = row_side[:, 0:1], row_side[:, 1:2] * (1.0 / total)
    sx = row_side[:, rst.shape[0] : rst.shape[0] + 1]
    half = sr.shape[0]
    t = half // 2
    base = s_ref[CORE] ^ (s_ref[CHIP] // 2)
    for jj in range(2):
        first = pl.multiple_of((base ^ jj) * half, half)
        stat = cst(first, half)
        mc, sc = stat[0:1], stat[1:2]
        rest = sums(stat) - cells * mc
        tiles = [[None, None], [None, None]]
        for c in range(2):
            lanes = slice(c * t, c * t + t)
            p = product(pl.multiple_of(first + c * t, t), t)
            p = (p - sx * mc[:, lanes] - mr * rest[:, lanes]) * sr * sc[:, lanes]
            tiles[0][c], tiles[1][c] = p[:t], p[t:]
        for b in range(2):
            for i in range(2):
                tile = jnp.where(odd == 0, tiles[i][i ^ b], tiles[i][1 - (i ^ b)])
                j = 2 * jj + b
                outs[j][blk, i] = encode(tile) if j else tile


def row_stats(s_ref, st, plane, half):
    return st[plane, :, pl.ds(pl.multiple_of(s_ref[CORE] * half, half), half)]


def column_stats(st, plane):
    return lambda first, n: st[plane, :, pl.ds(first, n)]


def diagonal_body(s_ref, xa, xb, y0, y1, st, *outs, total):
    half = xa.shape[0]
    n = y0.shape[0] // 2

    def product(first, w):
        lanes = pl.ds(first, w)
        return (
            plain(xa[:, :n], y0[:n, lanes])
            + plain(xa[:, n:], y1[:n, lanes])
            + plain(xb[:, :n], y0[n:, lanes])
            + plain(xb[:, n:], y1[n:, lanes])
        )

    put_tiles(
        product, lambda v: v[2:3] + v[3:4], s_ref, 0,
        row_stats(s_ref, st, 0, half), column_stats(st, 0), 4.0 * n, total, outs,
    )


def near_body(s_ref, xa, xb, y0, y1, st, *outs, total):
    half = xa.shape[0]
    n = y0.shape[0] // 2
    for blk, x in enumerate((xa, xb)):
        cells = slice(blk * n, blk * n + n)

        def product(first, w):
            lanes = pl.ds(first, w)
            return plain(x[:, :n], y0[cells, lanes]) + plain(x[:, n:], y1[cells, lanes])

        put_tiles(
            product, lambda v: v[2 + blk : 3 + blk], s_ref, blk,
            row_stats(s_ref, st, s_ref[LOWER + blk], half), column_stats(st, 0),
            2.0 * n, total, outs,
        )


def pick_far(s_ref, xa, xb, xs):
    @pl.when(s_ref[LOW] == 0)
    def _():
        xs[...] = xa[...]

    @pl.when(s_ref[LOW] == 1)
    def _():
        xs[...] = xb[...]


def put_far(s_ref, product, st, plane, outs, cells, half, total):
    put_tiles(
        product, lambda v: jnp.where(s_ref[LOW] == 0, v[2:3], v[3:4]), s_ref, 0,
        row_stats(s_ref, st, 2, half), column_stats(st, plane), cells, total, outs,
    )


def far_body(s_ref, xa, xb, y0, y1, st, *refs, total):
    xs, outs = refs[-1], refs[:-1]
    half = xa.shape[0]
    n = y0.shape[0] // 2
    pick_far(s_ref, xa, xb, xs)
    cells = pl.ds(pl.multiple_of(s_ref[LOW] * n, n), n)

    def product(first, w):
        lanes = pl.ds(first, w)
        return plain(xs[:, :n], y0[cells, lanes]) + plain(xs[:, n:], y1[cells, lanes])

    put_far(s_ref, product, st, 0, outs, 2.0 * n, half, total)


def ends_body(s_ref, xa, xb, na, nb, st, *refs, total):
    xs, ys, outs = refs[-2], refs[-1], refs[:-2]
    half = xa.shape[0]
    n = na.shape[0] // 2
    pick_far(s_ref, xa, xb, xs)

    @pl.when(s_ref[CORE] == 0)
    def _():
        ys[:, :half] = na[...]
        ys[:n, half:] = nb[n:]
        ys[n:, half:] = nb[:n]

    @pl.when(s_ref[CORE] == 1)
    def _():
        ys[:, half:] = na[...]
        ys[:n, :half] = nb[n:]
        ys[n:, :half] = nb[:n]

    put_far(
        s_ref, lambda first, w: plain(xs[...], ys[:, pl.ds(first, w)]), st, 1, outs,
        2.0 * n, half, total,
    )


CHIP, CORE, PLANE, PLANES, LOW, LOWER, _, SHIFT, EARLY = range(9)


def turn_body(s_ref, own, r1, r2, r3, *outs, turns, keeps):
    odd = s_ref[CHIP] % 2
    t_ref, rest = outs[0], outs[1:]
    for n in range(own.shape[0]):
        for i in range(2):
            v = own[n, i] + decode(r1[n, i]) + decode(r2[n, i]) + decode(r3[n, i])
            t_ref[n, i] = v
            if keeps[n] is not None:
                rest[keeps[n]][i] = encode(v)
            if turns[n] is not None:
                w = encode(v.T)
                dst = rest[turns[n]]

                @pl.when(odd == 0)
                def _():
                    dst[i] = w

                @pl.when(odd == 1)
                def _():
                    dst[1 - i] = w


def power(v):
    v2 = v * v
    return v2 * v2 * v2


def put_slot(outs, where, i, value):
    for j, o in enumerate(outs):

        @pl.when(where == j)
        def _():
            o[i] = value


def row_total(v):
    return jnp.sum(v.T, axis=0, keepdims=True)


def early_body(s_ref, t0, t1, ru, rd, *refs):
    outs, sums = refs[:-1], refs[-1]
    k, g = s_ref[CHIP], s_ref[PLANE]
    n = t0.shape[-1]
    sums[...] = jnp.zeros_like(sums)
    for i in range(2):
        lanes = slice(i * n, i * n + n)
        own = power(t0[0, i])
        same = lax.broadcasted_iota(jnp.int32, (n, n), 0) == lax.broadcasted_iota(
            jnp.int32, (n, n), 1
        )
        own = jnp.where(same & (k == 0), 0.0, own)
        put_slot(outs, g ^ k, i, own.astype(jnp.bfloat16))
        sums[pl.ds(g, 1), lanes] = row_total(own)
        low = power(t1[0, i] + decode(ru[i]))
        high = power(t1[1, i] + decode(rd[i]))

        @pl.when(g > 0)
        def _():
            put_slot(outs, (g - 1) ^ k, i, low.astype(jnp.bfloat16))
            sums[pl.ds(g - 1, 1), lanes] = row_total(low)

        @pl.when(g < s_ref[PLANES] - 1)
        def _():
            put_slot(outs, (g + 1) ^ k, i, high.astype(jnp.bfloat16))
            sums[pl.ds(g + 1, 1), lanes] = row_total(high)


def late_body(s_ref, t2, r2, rf, rn, before, *refs):
    outs, sums = refs[:-1], refs[-1]
    k, g = s_ref[CHIP], s_ref[PLANE]
    n = t2.shape[-1]
    outer = (g == 0) | (g == s_ref[PLANES] - 1)
    sums[...] = before[...]
    for i in range(2):
        lanes = slice(i * n, i * n + n)
        two = power(t2[0, i] + decode(r2[i]))
        put_slot(outs, g ^ 2 ^ k, i, two.astype(jnp.bfloat16))
        sums[pl.ds(g ^ 2, 1), lanes] = row_total(two)

        @pl.when(outer)
        def _():
            three = power(decode(rf[i]) + decode(rn[i]))
            put_slot(outs, g ^ 3 ^ k, i, three.astype(jnp.bfloat16))
            sums[pl.ds(g ^ 3, 1), lanes] = row_total(three)


def place_body(s_ref, e0, e1, e2, e3, l0, l1, l2, l3, out_ref):
    x = s_ref[SHIFT]
    is_early = s_ref[EARLY]
    early, late = (e0, e1, e2, e3), (l0, l1, l2, l3)
    t = e0.shape[-1]

    def place(tiles):
        for i in range(2):
            for c in range(4):
                v = tiles[c ^ i][i]
                for m in range(1, 4):
                    v = jnp.where(x == m, tiles[c ^ i ^ m][i], v)
                out_ref[i * t : i * t + t, c * t : c * t + t] = v.astype(jnp.float32)

    @pl.when(is_early == 1)
    def _():
        place(early)

    @pl.when(is_early == 0)
    def _():
        place(late)


def pay_body(s_ref, a, *refs):
    out_a, out_b, out_n = refs[-3:]
    n = a.shape[0] // 2
    out_a[...] = a[:n].T
    out_b[...] = a[n:].T
    first = pl.multiple_of(jnp.where(s_ref[PLANE] == 0, n, 0), n)
    out_n[...] = a[pl.ds(first, n)]


def hold_body(a, out):
    out[...] = a[...]


def limit(mib):
    return pltpu.CompilerParams(vmem_limit_bytes=mib * 1024 * 1024)


def whole():
    return pl.BlockSpec(memory_space=pltpu.VMEM)


def scalars():
    return pl.BlockSpec(memory_space=pltpu.SMEM)


def folded_shards(counts, library):
    rows, width = counts.shape
    n_cells = lax.axis_size("cells")
    n_genes = lax.axis_size("genes")
    cores = n_cells // n_genes
    total = float(rows * n_cells)
    half_cells = rows // 2
    half = width // cores
    tile = half // 2
    g = lax.axis_index("genes")
    c = lax.axis_index("cells")
    k, h = c // cores, c % cores

    def perm(f):
        pairs = []
        for ci in range(n_cells):
            for gi in range(n_genes):
                d = f(ci // cores, ci % cores, gi)
                if d is not None and 0 <= d[2] < n_genes:
                    pairs.append((ci * n_genes + gi, (d[0] * cores + d[1]) * n_genes + d[2]))
        return pairs

    def send(x, f):
        return lax.ppermute(x, AXES, perm(f))

    flip = lambda k, h, g: (k, h ^ 1, g)
    bf16, f32 = jnp.bfloat16, jnp.float32
    shape = jax.ShapeDtypeStruct

    last = n_genes - 1
    own = normalize(counts, library)
    oth = send(own, flip)
    info = jnp.stack(
        [
            k,
            h,
            g,
            jnp.int32(n_genes),
            (g < n_genes // 2).astype(jnp.int32),
            jnp.where(g > 0, g ^ (g - 1), 0),
            jnp.where(g < last, g ^ (g + 1), 0),
            (2 * h) ^ k,
            (jnp.abs(k - g) <= 1).astype(jnp.int32),
        ]
    ).astype(jnp.int32)

    pay_in = pl.BlockSpec((rows, half), lambda i, sc: (0, sc[CORE]))
    pay_shapes = [shape((half, rows), bf16)] * 2 + [shape((rows, half), bf16)]

    def turn_payload(block, part, before):
        return pl.pallas_call(
            pay_body,
            grid_spec=pltpu.PrefetchScalarGridSpec(
                num_scalar_prefetch=1,
                grid=(1,),
                in_specs=[pay_in] + [pl.BlockSpec(memory_space=pl.ANY)] * len(before),
                out_specs=[pl.BlockSpec((half, half_cells), lambda i, sc: (0, part))] * 2
                + [pl.BlockSpec((half_cells, half), lambda i, sc: (part, 0))],
            ),
            out_shape=pay_shapes,
            input_output_aliases={2 + n: n for n in range(len(before))},
            compiler_params=limit(8),
            name="turn_payload",
        )(info, block, *before)

    pay_a, pay_b, end = turn_payload(oth, 1, turn_payload(own, 0, []))
    up1 = send(pay_a, lambda k, h, g: (k, h, g + 1))
    dn1 = send(pay_b, lambda k, h, g: (k, h, g - 1))
    widened = own.astype(f32)
    halves = jnp.sum(widened.reshape(2, half_cells, width), axis=1)
    squares = jnp.sum(widened * widened, axis=0)
    local = jnp.concatenate([halves, squares[None]])
    chip = local + send(local, flip)
    chip_halves = chip[:2]
    pair = jnp.stack([chip[0] + chip[1], chip[2]])
    around = [send(pair, lambda k, h, g, j=j: (k ^ j, h, g)) for j in (1, 2, 3)]
    sums = (pair + around[0]) + (around[1] + around[2])
    means = sums[0] / total
    variances = sums[1] / total - means * means
    mine = jnp.concatenate(
        [means[None], lax.rsqrt(variances + 1e-05)[None], chip_halves, jnp.zeros((4, width), f32)]
    )
    afar = [send(mine, lambda k, h, g, d=d: (k, h, g ^ d)) for d in (1, 2, 3)]
    own_stats = mine[None]
    stats = jnp.stack([mine] + afar)
    near = send(
        end, lambda k, h, g: (k, h, 1) if g == 0 else ((k, h, g - 1) if g == last else None)
    )

    oth = pl.pallas_call(
        hold_body,
        in_specs=[whole()],
        out_specs=whole(),
        out_shape=shape(oth.shape, bf16),
        compiler_params=limit(8),
        name="hold",
    )(oth)

    def blocks(body, n, scratch, *operands):
        return pl.pallas_call(
            functools.partial(body, total=total),
            in_specs=[scalars()] + [whole()] * len(operands),
            out_specs=[whole()] * 4,
            out_shape=[shape((n, 2, tile, tile), f32)]
            + [shape((n, 2, tile, tile), bf16)] * 3,
            scratch_shapes=[pltpu.VMEM(v, bf16) for v in scratch],
            compiler_params=limit(24),
            name="partial_blocks",
        )(info, *operands)

    up2 = send(up1, lambda k, h, g: (k, h, g + 1) if g > 0 else None)
    dn2 = send(dn1, lambda k, h, g: (k, h, g - 1) if g < last else None)
    near_other = send(near, flip)
    kept = (half, rows)
    w0 = blocks(diagonal_body, 1, [], pay_a, pay_b, own, oth, own_stats)
    w1 = blocks(near_body, 2, [], up1, dn1, own, oth, stats)
    w2 = blocks(far_body, 1, [kept], up2, dn2, own, oth, stats)
    w3 = blocks(ends_body, 1, [kept, (rows, width)], up2, dn2, near, near_other, stats)

    def reduce_tiles(w):
        return [w[0]] + [send(w[j], lambda k, h, g, j=j: (k ^ j, h, g)) for j in (1, 2, 3)]

    small = shape((2, tile, tile), bf16)

    def turn(parts, turns, keeps):
        n = parts[0].shape[0]
        n_out = sum(v is not None for v in turns + keeps)
        return pl.pallas_call(
            functools.partial(turn_body, turns=turns, keeps=keeps),
            in_specs=[scalars()] + [whole()] * 4,
            out_specs=[whole()] * (1 + n_out),
            out_shape=[shape((n, 2, tile, tile), f32)] + [small] * n_out,
            compiler_params=limit(12),
            name="sum_tiles",
        )(info, *parts)

    (t0,) = turn(reduce_tiles(w0), [None], [None])
    t1, e_up, e_dn = turn(reduce_tiles(w1), [0, 1], [None, None])
    t2, e_two = turn(reduce_tiles(w2), [0], [None])
    _, e_three, k_three = turn(reduce_tiles(w3), [0], [1])

    side = lambda f: (lambda k, h, g: (k, h ^ (k // 2), f(g)) if f(g) is not None else None)
    rd = send(e_up, side(lambda g: g - 1))
    ru = send(e_dn, side(lambda g: g + 1))
    r2 = send(e_two, side(lambda g: g ^ 2))
    inner = lambda g: 0 < g < last
    r3f = send(e_three, side(lambda g: (g ^ 2) if inner(g) else None))
    r3n = send(k_three, lambda k, h, g: (k, h, g ^ 1) if inner(g) else None)

    def finish(body, *operands):
        return pl.pallas_call(
            body,
            in_specs=[scalars()] + [whole()] * len(operands),
            out_specs=[whole()] * 5,
            out_shape=[small] * 4 + [shape((n_genes, half), f32)],
            compiler_params=limit(10),
            name="finish_tiles",
        )(info, *operands)

    *early, early_sums = finish(early_body, t0, t1, ru, rd)
    *late, tile_sums = finish(late_body, t2, r2, r3f, r3n, early_sums)

    is_early = lambda q, g: -1 <= q - g <= 1
    got_early, got_late = [early[0]], [late[0]]
    for j in range(1, 4):
        got_early.append(
            send(early[j], lambda k, h, g, j=j: (k ^ j, h, g) if is_early(k ^ j, g) else None)
        )
        got_late.append(
            send(late[j], lambda k, h, g, j=j: (k ^ j, h, g) if not is_early(k ^ j, g) else None)
        )
    adjacency = pl.pallas_call(
        place_body,
        in_specs=[scalars()] + [whole()] * 8,
        out_specs=whole(),
        out_shape=shape((half, width), f32),
        compiler_params=limit(12),
        name="place_tiles",
    )(info, *got_early, *got_late)
    over = [send(tile_sums, lambda k, h, g, d=d: (k, h, g ^ d)) for d in (1, 2, 3)]
    chip_sums = (tile_sums + over[0]) + (over[1] + over[2])

    def rows_of(q):
        return lax.dynamic_index_in_dim(chip_sums, q, 0, keepdims=False)

    inside = [rows_of(k)] + [
        send(rows_of(k ^ j), lambda k, h, g, j=j: (k ^ j, h, g)) for j in (1, 2, 3)
    ]
    connectivity = (inside[0] + inside[1]) + (inside[2] + inside[3])
    return (adjacency, connectivity)


def folded(counts, library):
    return folded_shards(counts, library)


def solution(mesh):
    cells, genes = mesh.shape["cells"], mesh.shape["genes"]
    folds = genes == 4 and cells == 2 * genes
    return jax.shard_map(
        folded if folds else general_shards,
        mesh=mesh,
        in_specs=(P("cells", "genes"), P("cells")),
        out_specs=(P("cells", "genes"), P("cells")),
        check_vma=False,
    )
```

time: 194 us -> 198 us (1.021)
  waiting for transfers between devices: 62.9 us -> 78.2 us
  starting transfers between devices: 89.5 us -> 81.5 us
  Pallas kernels: 33.6 us -> 29 us
    ppermute x40 -> x43, waiting for transfers between devices: 62.9 us -> 78.2 us  [send(): return lax.ppermute(x, AXES, perm(f))]
    ppermute x40 -> x43, starting transfers between devices: 89.5 us -> 81.5 us  [send(): return lax.ppermute(x, AXES, perm(f))]
    pallas_call x6 -> x7, Pallas kernels: 22.1 us -> 17.9 us  [the longest x4 12.6 us: blocks(): pl.pallas_call(functools.partial(body, total=total), in_specs=[scalars()]...]
  transfers between devices with their start and end apart: 40 -> 43, of which waited for: 17 -> 20; matrix products, arithmetic and copies ran while one was open for 0% -> 1% of each run, Pallas kernels for 15% -> 12%
where the time goes in v4:
time: 198 us; the launch traced here: 196 us
  starting transfers between devices  81.5 us (41%)
  waiting for transfers between devices  78.2 us (39%)
  Pallas kernels  29 us (15%)
  other arithmetic  5.89 us (3%)
    ppermute x43, starting transfers between devices, send(): return lax.ppermute(x, AXES, perm(f))  81.5 us
    ppermute x43, waiting for transfers between devices, send(): return lax.ppermute(x, AXES, perm(f))  78.2 us
    pallas_call x4, Pallas kernels, blocks(): pl.pallas_call(functools.partial(body, total=total), in_specs=[scalars()]...  12.6 us
    pallas_call x4, Pallas kernels, turn(): pl.pallas_call(functools.partial(turn_body, turns=turns, keeps=keeps), in...  5.84 us
  transfers between devices with their start and end apart: 43, of which 20 were waited for; matrix products, arithmetic and copies ran while one was open for 1% of the time, Pallas kernels for 12%

profile of v4, /device:TPU:0, one launch (start us, length us, event | category | flops | bytes accessed | tf_op | source)
XLA Modules:
  0.0 195.8 jit_solution(3843916589449943923)
XLA Ops:
  1.3 4.0 %bitcast_reduce_fusion = (f32[2,1024]{1,0:T(2,128)S(1)}, bf16[1024,1024]{1,0:T(8,128)(2,1)S(1)}) fusion(f32[1024]{0:T(1024)S(1)} %convert_divide_fusion, s32[1024,1024]{1,0:T(8,128)} %param.2), kind=kLoop, calls=%fused_computation | loop fusion | flops 5240832 | bytes 6303744 | tf_op jit(solution)/shard_map/reduce_sum | solution.py:411
  6.9 2.8 %collective-permute-done.a = bf16[1024,1024]{1,0:T(8,128)(2,1)} collective-permute-done((bf16[1024,1024]{1,0:T(8,128)(2,1)S(1)}, bf16[1024,1024]{1,0:T(8,128)(2,1)}, u32[]{:S(2)}, u32[]{:S(2)}) %collective-permute-start) | collective-permute-done | bytes 2097184 | tf_op jit(solution)/shard_map/ppermute | solution.py:365
  11.9 4.9 %collective-permute-start.8 = (bf16[512,1024]{1,0:T(8,128)(2,1)S(1)}, bf16[512,1024]{1,0:T(8,128)(2,1)S(1)}, u32[]{:S(2)}, u32[]{:S(2)}) collective-permute-start(bf16[512,1024]{1,0:T(8,128)(2,1)S(1)} %get-tuple-element.44.xa), channel_id=1, source_target_pairs={{0,1},{1,2},{2,3},{4,5},{5,6},{6,7},{8,9},{9,10},{10,11},{12,13},{... | collective-permute-start | bytes 3145736 | tf_op jit(solution)/shard_map/ppermute | solution.py:365
  18.1 4.6 %collective-permute-start.27 = (bf16[1024,512]{1,0:T(8,128)(2,1)S(1)}, bf16[1024,512]{1,0:T(8,128)(2,1)S(1)}, u32[]{:S(2)}, u32[]{:S(2)}) collective-permute-start(bf16[1024,512]{1,0:T(8,128)(2,1)S(1)} %get-tuple-element.67), channel_id=1, source_target_pairs={{0,1},{3,2},{4,5},{7,6},{8,9},{11,10},{12,13},{15,14},{16,17},{19,... | collective-permute-start | bytes 3145736 | tf_op jit(solution)/shard_map/ppermute | solution.py:365
  29.8 10.5 %collective-permute-done.8.xa = bf16[512,1024]{1,0:T(8,128)(2,1)S(1)} collective-permute-done((bf16[512,1024]{1,0:T(8,128)(2,1)S(1)}, bf16[512,1024]{1,0:T(8,128)(2,1)S(1)}, u32[]{:S(2)}, u32[]{:S(2)}) %collective-permute-start.8) | collective-permute-done | bytes 1048608 | tf_op jit(solution)/shard_map/ppermute | solution.py:365
  41.1 2.6 %collective-permute-done.9.xb = bf16[512,1024]{1,0:T(8,128)(2,1)S(1)} collective-permute-done((bf16[512,1024]{1,0:T(8,128)(2,1)S(1)}, bf16[512,1024]{1,0:T(8,128)(2,1)S(1)}, u32[]{:S(2)}, u32[]{:S(2)}) %collective-permute-start.9) | collective-permute-done | bytes 1048608 | tf_op jit(solution)/shard_map/ppermute | solution.py:365
  44.9 17.0 %collective-permute-done.27.na = bf16[1024,512]{1,0:T(8,128)(2,1)S(1)} collective-permute-done((bf16[1024,512]{1,0:T(8,128)(2,1)S(1)}, bf16[1024,512]{1,0:T(8,128)(2,1)S(1)}, u32[]{:S(2)}, u32[]{:S(2)}) %collective-permute-start.27) | collective-permute-done | bytes 1048608 | tf_op jit(solution)/shard_map/ppermute | solution.py:365
  62.0 5.7 %collective-permute-start.12 = (f32[8,1024]{1,0:T(8,128)S(1)}, f32[8,1024]{1,0:T(8,128)S(1)}, u32[]{:S(2)}, u32[]{:S(2)}) collective-permute-start(f32[8,1024]{1,0:T(8,128)S(1)} %get-tuple-element.82), channel_id=1, source_target_pairs={{0,3},{1,2},{2,1},{3,0},{4,7},{5,6},{6,5},{7,4},{8,11},{9,10},{10,... | collective-permute-start | bytes 98312 | tf_op jit(solution)/shard_map/ppermute | solution.py:365
  69.9 3.7 %collective-permute-start.10 = (f32[8,1024]{1,0:T(8,128)S(1)}, f32[8,1024]{1,0:T(8,128)S(1)}, u32[]{:S(2)}, u32[]{:S(2)}) collective-permute-start(f32[8,1024]{1,0:T(8,128)S(1)} %get-tuple-element.82), channel_id=1, source_target_pairs={{0,1},{1,0},{2,3},{3,2},{4,5},{5,4},{6,7},{7,6},{8,9},{9,8},{10,11... | collective-permute-start | bytes 98312 | tf_op jit(solution)/shard_map/ppermute | solution.py:365
  77.2 4.0 %partial_blocks.5 = (f32[2,2,256,256]{3,2,1,0:T(8,128)S(1)}, bf16[2,2,256,256]{3,2,1,0:T(8,128)(2,1)S(1)}, bf16[2,2,256,256]{3,2,1,0:T(8,128)(2,1)S(1)}, bf16[2,2,256,256]{3,2,1,0:T(8,128)(2,1)S(1)}) custom-call(s32[9]{0:T(128)S(1)} %stack.60.s_ref, bf16[512,1024]{1,0:T(8,128)(2,1)S(1)} %collective-permute-done.8.xa, ...), custom_call_target="tpu_custom_call" | custom-call | tf_op jit(solution)/shard_map/partial_blocks/pallas_call | solution.py:441
  90.3 2.8 %partial_blocks.7 = (f32[1,2,256,256]{3,2,1,0:T(8,128)S(1)}, bf16[1,2,256,256]{3,2,1,0:T(8,128)(2,1)S(1)}, bf16[1,2,256,256]{3,2,1,0:T(8,128)(2,1)S(1)}, bf16[1,2,256,256]{3,2,1,0:T(8,128)(2,1)S(1)}) custom-call(s32[9]{0:T(128)S(1)} %stack.60.s_ref, bf16[512,1024]{1,0:T(8,128)(2,1)S(1)} %collective-permute-done.21.xa, ...), custom_call_target="tpu_custom_call" | custom-call | tf_op jit(solution)/shard_map/partial_blocks/pallas_call | solution.py:441
  93.1 3.0 %collective-permute-done.13.r1 = bf16[2,2,256,256]{3,2,1,0:T(8,128)(2,1)S(1)} collective-permute-done((bf16[2,2,256,256]{3,2,1,0:T(8,128)(2,1)S(1)}, bf16[2,2,256,256]{3,2,1,0:T(8,128)(2,1)S(1)}, u32[]{:S(2)}, u32[]{:S(2)}) %collective-permute-start.13) | collective-permute-done | bytes 524320 | tf_op jit(solution)/shard_map/ppermute | solution.py:365
  96.1 2.5 %collective-permute-start.25 = (bf16[1,2,256,256]{3,2,1,0:T(8,128)(2,1)S(1)}, bf16[1,2,256,256]{3,2,1,0:T(8,128)(2,1)S(1)}, u32[]{:S(2)}, u32[]{:S(2)}) collective-permute-start(bf16[1,2,256,256]{3,2,1,0:T(8,128)(2,1)S(1)} %get-tuple-element.64), channel_id=1, source_target_pairs={{0,24},{1,25},{2,26},{3,27},{4,28},{5,29},{6,30},{7,31},{8,16},{9,... | collective-permute-start | bytes 786440 | tf_op jit(solution)/shard_map/ppermute | solution.py:365
  98.6 13.1 %collective-permute-done.14.r2 = bf16[2,2,256,256]{3,2,1,0:T(8,128)(2,1)S(1)} collective-permute-done((bf16[2,2,256,256]{3,2,1,0:T(8,128)(2,1)S(1)}, bf16[2,2,256,256]{3,2,1,0:T(8,128)(2,1)S(1)}, u32[]{:S(2)}, u32[]{:S(2)}) %collective-permute-start.14) | collective-permute-done | bytes 524320 | tf_op jit(solution)/shard_map/ppermute | solution.py:365
  115.5 3.4 %partial_blocks.4 = (f32[1,2,256,256]{3,2,1,0:T(8,128)S(1)}, bf16[1,2,256,256]{3,2,1,0:T(8,128)(2,1)S(1)}, bf16[1,2,256,256]{3,2,1,0:T(8,128)(2,1)S(1)}, bf16[1,2,256,256]{3,2,1,0:T(8,128)(2,1)S(1)}) custom-call(s32[9]{0:T(128)S(1)} %stack.60.s_ref, bf16[512,1024]{1,0:T(8,128)(2,1)S(1)} %get-tuple-element.44.xa, bf16[512,1024]{1,0:T(8,128)(2,1)S(1)} %get-tuple-element.45.xb, ...), custom_call_target="tpu_custom_call" | custom-call | tf_op jit(solution)/shard_map/partial_blocks/pallas_call | solution.py:441
  118.9 3.9 %collective-permute-done.24.r2 = bf16[1,2,256,256]{3,2,1,0:T(8,128)(2,1)S(1)} collective-permute-done((bf16[1,2,256,256]{3,2,1,0:T(8,128)(2,1)S(1)}, bf16[1,2,256,256]{3,2,1,0:T(8,128)(2,1)S(1)}, u32[]{:S(2)}, u32[]{:S(2)}) %collective-permute-start.24) | collective-permute-done | bytes 262176 | tf_op jit(solution)/shard_map/ppermute | solution.py:365
  131.2 3.9 %collective-permute-start.16 = (bf16[2,256,256]{2,1,0:T(8,128)(2,1)S(1)}, bf16[2,256,256]{2,1,0:T(8,128)(2,1)S(1)}, u32[]{:S(2)}, u32[]{:S(2)}) collective-permute-start(bf16[2,256,256]{2,1,0:T(8,128)(2,1)S(1)} %get-tuple-element.55), channel_id=1, source_target_pairs={{0,1},{1,2},{2,3},{4,5},{5,6},{6,7},{8,9},{9,10},{10,11},{12,13},{... | collective-permute-start | bytes 786440 | tf_op jit(solution)/shard_map/ppermute | solution.py:365
  138.4 3.1 %collective-permute-start.26 = (bf16[2,256,256]{2,1,0:T(8,128)(2,1)S(1)}, bf16[2,256,256]{2,1,0:T(8,128)(2,1)S(1)}, u32[]{:S(2)}, u32[]{:S(2)}) collective-permute-start(bf16[2,256,256]{2,1,0:T(8,128)(2,1)S(1)} %get-tuple-element.66), channel_id=1, source_target_pairs={{0,2},{1,3},{2,0},{3,1},{4,6},{5,7},{6,4},{7,5},{8,10},{9,11},{10,... | collective-permute-start | bytes 786440 | tf_op jit(solution)/shard_map/ppermute | solution.py:365
  145.1 4.4 %collective-permute-done.17.rd = bf16[2,256,256]{2,1,0:T(8,128)(2,1)S(1)} collective-permute-done((bf16[2,256,256]{2,1,0:T(8,128)(2,1)S(1)}, bf16[2,256,256]{2,1,0:T(8,128)(2,1)S(1)}, u32[]{:S(2)}, u32[]{:S(2)}) %collective-permute-start.17) | collective-permute-done | bytes 262176 | tf_op jit(solution)/shard_map/ppermute | solution.py:365
  153.3 2.8 %collective-permute-done.32.rf = bf16[2,256,256]{2,1,0:T(8,128)(2,1)S(1)} collective-permute-done((bf16[2,256,256]{2,1,0:T(8,128)(2,1)S(1)}, bf16[2,256,256]{2,1,0:T(8,128)(2,1)S(1)}, u32[]{:S(2)}, u32[]{:S(2)}) %collective-permute-start.32) | collective-permute-done | bytes 262176 | tf_op jit(solution)/shard_map/ppermute | solution.py:365
  156.1 3.0 %collective-permute-done.33.rn = bf16[2,256,256]{2,1,0:T(8,128)(2,1)S(1)} collective-permute-done((bf16[2,256,256]{2,1,0:T(8,128)(2,1)S(1)}, bf16[2,256,256]{2,1,0:T(8,128)(2,1)S(1)}, u32[]{:S(2)}, u32[]{:S(2)}) %collective-permute-start.33) | collective-permute-done | bytes 262176 | tf_op jit(solution)/shard_map/ppermute | solution.py:365
  166.6 6.5 %collective-permute-start.41 = (f32[512]{0:T(512)S(1)}, f32[512]{0:T(512)S(1)}, u32[]{:S(2)}, u32[]{:S(2)}) collective-permute-start(f32[512]{0:T(512)S(1)} %bitcast.28), channel_id=1, source_target_pairs={{0,16},{1,17},{2,18},{3,19},{4,20},{5,21},{6,22},{7,23},{8,24},{9,... | collective-permute-start | bytes 6152 | tf_op jit(solution)/shard_map/ppermute | solution.py:365
  178.0 7.3 %collective-permute-start.35 = (bf16[2,256,256]{2,1,0:T(8,128)(2,1)S(1)}, bf16[2,256,256]{2,1,0:T(8,128)(2,1)S(1)}, u32[]{:S(2)}, u32[]{:S(2)}) collective-permute-start(bf16[2,256,256]{2,1,0:T(8,128)(2,1)S(1)} %get-tuple-element.77), channel_id=1, source_target_pairs={{0,16},{4,20},{8,24},{9,25},{12,28},{13,29},{18,2},{19,3},{22,6},{... | collective-permute-start | bytes 786440 | tf_op jit(solution)/shard_map/ppermute | solution.py:365
  188.0 5.6 %collective-permute-done.35.l2 = bf16[2,256,256]{2,1,0:T(8,128)(2,1)S(1)} collective-permute-done((bf16[2,256,256]{2,1,0:T(8,128)(2,1)S(1)}, bf16[2,256,256]{2,1,0:T(8,128)(2,1)S(1)}, u32[]{:S(2)}, u32[]{:S(2)}) %collective-permute-start.35) | collective-permute-done | bytes 262176 | tf_op jit(solution)/shard_map/ppermute | solution.py:365
  (94 shorter events, 69.9 us)
Async XLA Ops:
  11.9 28.4 %collective-permute-start.8 = (bf16[512,1024]{1,0:T(8,128)(2,1)S(1)}, bf16[512,1024]{1,0:T(8,128)(2,1)S(1)}, u32[]{:S(2)}, u32[]{:S(2)}) collective-permute-start(bf16[512,1024]{1,0:T(8,128)(2,1)S(1)} %get-tuple-element.44.xa), channel_id=1, source_target_pairs={{0,1},{1,2},{2,3},{4,5},{5,6},{6,7},{8,9},{9,10},{10,11},{12,13},{... | collective-permute-start | bytes 3145736 | tf_op jit(solution)/shard_map/ppermute | solution.py:365
  16.8 26.8 %collective-permute-start.9 = (bf16[512,1024]{1,0:T(8,128)(2,1)S(1)}, bf16[512,1024]{1,0:T(8,128)(2,1)S(1)}, u32[]{:S(2)}, u32[]{:S(2)}) collective-permute-start(bf16[512,1024]{1,0:T(8,128)(2,1)S(1)} %get-tuple-element.45.xb), channel_id=1, source_target_pairs={{1,0},{2,1},{3,2},{5,4},{6,5},{7,6},{9,8},{10,9},{11,10},{13,12},{... | collective-permute-start | bytes 3145736 | tf_op jit(solution)/shard_map/ppermute | solution.py:365
  18.1 43.8 %collective-permute-start.27 = (bf16[1024,512]{1,0:T(8,128)(2,1)S(1)}, bf16[1024,512]{1,0:T(8,128)(2,1)S(1)}, u32[]{:S(2)}, u32[]{:S(2)}) collective-permute-start(bf16[1024,512]{1,0:T(8,128)(2,1)S(1)} %get-tuple-element.67), channel_id=1, source_target_pairs={{0,1},{3,2},{4,5},{7,6},{8,9},{11,10},{12,13},{15,14},{16,17},{19,... | collective-permute-start | bytes 3145736 | tf_op jit(solution)/shard_map/ppermute | solution.py:365
  26.1 14.9 %collective-permute-start.4 = (f32[2,1024]{1,0:T(2,128)S(1)}, f32[2,1024]{1,0:T(2,128)S(1)}, u32[]{:S(2)}, u32[]{:S(2)}) collective-permute-start(f32[2,1024]{1,0:T(2,128)S(1)} %pad_maximum_fusion.2), channel_id=1, source_target_pairs={{0,24},{1,25},{2,26},{3,27},{4,28},{5,29},{6,30},{7,31},{8,16},{9,... | collective-permute-start | bytes 24584 | tf_op jit(solution)/shard_map/ppermute | solution.py:365
  40.3 44.1 %collective-permute-start.21 = (bf16[512,1024]{1,0:T(8,128)(2,1)S(1)}, bf16[512,1024]{1,0:T(8,128)(2,1)S(1)}, u32[]{:S(2)}, u32[]{:S(2)}) collective-permute-start(bf16[512,1024]{1,0:T(8,128)(2,1)S(1)} %collective-permute-done.8.xa), channel_id=1, source_target_pairs={{1,2},{2,3},{5,6},{6,7},{9,10},{10,11},{13,14},{14,15},{17,18},{18... | collective-permute-start | bytes 3145736 | tf_op jit(solution)/shard_map/ppermute | solution.py:365
  43.6 41.2 %collective-permute-start.22 = (bf16[512,1024]{1,0:T(8,128)(2,1)S(1)}, bf16[512,1024]{1,0:T(8,128)(2,1)S(1)}, u32[]{:S(2)}, u32[]{:S(2)}) collective-permute-start(bf16[512,1024]{1,0:T(8,128)(2,1)S(1)} %collective-permute-done.9.xb), channel_id=1, source_target_pairs={{1,0},{2,1},{5,4},{6,5},{9,8},{10,9},{13,12},{14,13},{17,16},{18,1... | collective-permute-start | bytes 3145736 | tf_op jit(solution)/shard_map/ppermute | solution.py:365
  61.9 26.8 %collective-permute-start.28 = (bf16[1024,512]{1,0:T(8,128)(2,1)S(1)}, bf16[1024,512]{1,0:T(8,128)(2,1)S(1)}, u32[]{:S(2)}, u32[]{:S(2)}) collective-permute-start(bf16[1024,512]{1,0:T(8,128)(2,1)S(1)} %collective-permute-done.27.na), channel_id=1, source_target_pairs={{0,4},{1,5},{2,6},{3,7},{4,0},{5,1},{6,2},{7,3},{8,12},{9,13},{10,... | collective-permute-start | bytes 3145736 | tf_op jit(solution)/shard_map/ppermute | solution.py:365
  81.2 14.9 %collective-permute-start.13 = (bf16[2,2,256,256]{3,2,1,0:T(8,128)(2,1)S(1)}, bf16[2,2,256,256]{3,2,1,0:T(8,128)(2,1)S(1)}, u32[]{:S(2)}, u32[]{:S(2)}) collective-permute-start(bf16[2,2,256,256]{3,2,1,0:T(8,128)(2,1)S(1)} %get-tuple-element.51), channel_id=1, source_target_pairs={{0,8},{1,9},{2,10},{3,11},{4,12},{5,13},{6,14},{7,15},{8,0},{9,1},... | collective-permute-start | bytes 1572872 | tf_op jit(solution)/shard_map/ppermute | solution.py:365
  82.8 28.8 %collective-permute-start.14 = (bf16[2,2,256,256]{3,2,1,0:T(8,128)(2,1)S(1)}, bf16[2,2,256,256]{3,2,1,0:T(8,128)(2,1)S(1)}, u32[]{:S(2)}, u32[]{:S(2)}) collective-permute-start(bf16[2,2,256,256]{3,2,1,0:T(8,128)(2,1)S(1)} %get-tuple-element.52), channel_id=1, source_target_pairs={{0,16},{1,17},{2,18},{3,19},{4,20},{5,21},{6,22},{7,23},{8,24},{9,... | collective-permute-start | bytes 1572872 | tf_op jit(solution)/shard_map/ppermute | solution.py:365
  84.3 27.3 %collective-permute-start.15 = (bf16[2,2,256,256]{3,2,1,0:T(8,128)(2,1)S(1)}, bf16[2,2,256,256]{3,2,1,0:T(8,128)(2,1)S(1)}, u32[]{:S(2)}, u32[]{:S(2)}) collective-permute-start(bf16[2,2,256,256]{3,2,1,0:T(8,128)(2,1)S(1)} %get-tuple-element.53), channel_id=1, source_target_pairs={{0,24},{1,25},{2,26},{3,27},{4,28},{5,29},{6,30},{7,31},{8,16},{9,... | collective-permute-start | bytes 1572872 | tf_op jit(solution)/shard_map/ppermute | solution.py:365
  87.2 26.5 %collective-permute-start.23 = (bf16[1,2,256,256]{3,2,1,0:T(8,128)(2,1)S(1)}, bf16[1,2,256,256]{3,2,1,0:T(8,128)(2,1)S(1)}, u32[]{:S(2)}, u32[]{:S(2)}) collective-permute-start(bf16[1,2,256,256]{3,2,1,0:T(8,128)(2,1)S(1)} %get-tuple-element.62), channel_id=1, source_target_pairs={{0,8},{1,9},{2,10},{3,11},{4,12},{5,13},{6,14},{7,15},{8,0},{9,1},... | collective-permute-start | bytes 786440 | tf_op jit(solution)/shard_map/ppermute | solution.py:365
  88.8 34.0 %collective-permute-start.24 = (bf16[1,2,256,256]{3,2,1,0:T(8,128)(2,1)S(1)}, bf16[1,2,256,256]{3,2,1,0:T(8,128)(2,1)S(1)}, u32[]{:S(2)}, u32[]{:S(2)}) collective-permute-start(bf16[1,2,256,256]{3,2,1,0:T(8,128)(2,1)S(1)} %get-tuple-element.63), channel_id=1, source_target_pairs={{0,16},{1,17},{2,18},{3,19},{4,20},{5,21},{6,22},{7,23},{8,24},{9,... | collective-permute-start | bytes 786440 | tf_op jit(solution)/shard_map/ppermute | solution.py:365
  96.1 26.7 %collective-permute-start.25 = (bf16[1,2,256,256]{3,2,1,0:T(8,128)(2,1)S(1)}, bf16[1,2,256,256]{3,2,1,0:T(8,128)(2,1)S(1)}, u32[]{:S(2)}, u32[]{:S(2)}) collective-permute-start(bf16[1,2,256,256]{3,2,1,0:T(8,128)(2,1)S(1)} %get-tuple-element.64), channel_id=1, source_target_pairs={{0,24},{1,25},{2,26},{3,27},{4,28},{5,29},{6,30},{7,31},{8,16},{9,... | collective-permute-start | bytes 786440 | tf_op jit(solution)/shard_map/ppermute | solution.py:365
  111.6 19.6 %collective-permute-start.30 = (bf16[1,2,256,256]{3,2,1,0:T(8,128)(2,1)S(1)}, bf16[1,2,256,256]{3,2,1,0:T(8,128)(2,1)S(1)}, u32[]{:S(2)}, u32[]{:S(2)}) collective-permute-start(bf16[1,2,256,256]{3,2,1,0:T(8,128)(2,1)S(1)} %get-tuple-element.70), channel_id=1, source_target_pairs={{0,16},{1,17},{2,18},{3,19},{4,20},{5,21},{6,22},{7,23},{8,24},{9,... | collective-permute-start | bytes 786440 | tf_op jit(solution)/shard_map/ppermute | solution.py:365
  113.7 21.4 %collective-permute-start.31 = (bf16[1,2,256,256]{3,2,1,0:T(8,128)(2,1)S(1)}, bf16[1,2,256,256]{3,2,1,0:T(8,128)(2,1)S(1)}, u32[]{:S(2)}, u32[]{:S(2)}) collective-permute-start(bf16[1,2,256,256]{3,2,1,0:T(8,128)(2,1)S(1)} %get-tuple-element.71), channel_id=1, source_target_pairs={{0,24},{1,25},{2,26},{3,27},{4,28},{5,29},{6,30},{7,31},{8,16},{9,... | collective-permute-start | bytes 786440 | tf_op jit(solution)/shard_map/ppermute | solution.py:365
  122.8 15.6 %collective-permute-start.5 = (bf16[1,2,256,256]{3,2,1,0:T(8,128)(2,1)S(1)}, bf16[1,2,256,256]{3,2,1,0:T(8,128)(2,1)S(1)}, u32[]{:S(2)}, u32[]{:S(2)}) collective-permute-start(bf16[1,2,256,256]{3,2,1,0:T(8,128)(2,1)S(1)} %get-tuple-element.47), channel_id=1, source_target_pairs={{0,8},{1,9},{2,10},{3,11},{4,12},{5,13},{6,14},{7,15},{8,0},{9,1},... | collective-permute-start | bytes 786440 | tf_op jit(solution)/shard_map/ppermute | solution.py:365
  122.8 18.7 %collective-permute-start.6 = (bf16[1,2,256,256]{3,2,1,0:T(8,128)(2,1)S(1)}, bf16[1,2,256,256]{3,2,1,0:T(8,128)(2,1)S(1)}, u32[]{:S(2)}, u32[]{:S(2)}) collective-permute-start(bf16[1,2,256,256]{3,2,1,0:T(8,128)(2,1)S(1)} %get-tuple-element.48), channel_id=1, source_target_pairs={{0,16},{1,17},{2,18},{3,19},{4,20},{5,21},{6,22},{7,23},{8,24},{9,... | collective-permute-start | bytes 786440 | tf_op jit(solution)/shard_map/ppermute | solution.py:365
  124.9 17.9 %collective-permute-start.7 = (bf16[1,2,256,256]{3,2,1,0:T(8,128)(2,1)S(1)}, bf16[1,2,256,256]{3,2,1,0:T(8,128)(2,1)S(1)}, u32[]{:S(2)}, u32[]{:S(2)}) collective-permute-start(bf16[1,2,256,256]{3,2,1,0:T(8,128)(2,1)S(1)} %get-tuple-element.49), channel_id=1, source_target_pairs={{0,24},{1,25},{2,26},{3,27},{4,28},{5,29},{6,30},{7,31},{8,16},{9,... | collective-permute-start | bytes 786440 | tf_op jit(solution)/shard_map/ppermute | solution.py:365
  131.2 13.9 %collective-permute-start.16 = (bf16[2,256,256]{2,1,0:T(8,128)(2,1)S(1)}, bf16[2,256,256]{2,1,0:T(8,128)(2,1)S(1)}, u32[]{:S(2)}, u32[]{:S(2)}) collective-permute-start(bf16[2,256,256]{2,1,0:T(8,128)(2,1)S(1)} %get-tuple-element.55), channel_id=1, source_target_pairs={{0,1},{1,2},{2,3},{4,5},{5,6},{6,7},{8,9},{9,10},{10,11},{12,13},{... | collective-permute-start | bytes 786440 | tf_op jit(solution)/shard_map/ppermute | solution.py:365
  135.1 14.3 %collective-permute-start.17 = (bf16[2,256,256]{2,1,0:T(8,128)(2,1)S(1)}, bf16[2,256,256]{2,1,0:T(8,128)(2,1)S(1)}, u32[]{:S(2)}, u32[]{:S(2)}) collective-permute-start(bf16[2,256,256]{2,1,0:T(8,128)(2,1)S(1)} %get-tuple-element.56), channel_id=1, source_target_pairs={{1,0},{2,1},{3,2},{5,4},{6,5},{7,6},{9,8},{10,9},{11,10},{13,12},{... | collective-permute-start | bytes 786440 | tf_op jit(solution)/shard_map/ppermute | solution.py:365
  138.4 14.8 %collective-permute-start.26 = (bf16[2,256,256]{2,1,0:T(8,128)(2,1)S(1)}, bf16[2,256,256]{2,1,0:T(8,128)(2,1)S(1)}, u32[]{:S(2)}, u32[]{:S(2)}) collective-permute-start(bf16[2,256,256]{2,1,0:T(8,128)(2,1)S(1)} %get-tuple-element.66), channel_id=1, source_target_pairs={{0,2},{1,3},{2,0},{3,1},{4,6},{5,7},{6,4},{7,5},{8,10},{9,11},{10,... | collective-permute-start | bytes 786440 | tf_op jit(solution)/shard_map/ppermute | solution.py:365
  141.5 14.5 %collective-permute-start.32 = (bf16[2,256,256]{2,1,0:T(8,128)(2,1)S(1)}, bf16[2,256,256]{2,1,0:T(8,128)(2,1)S(1)}, u32[]{:S(2)}, u32[]{:S(2)}) collective-permute-start(bf16[2,256,256]{2,1,0:T(8,128)(2,1)S(1)} %get-tuple-element.72), channel_id=1, source_target_pairs={{1,3},{2,0},{5,7},{6,4},{9,11},{10,8},{13,15},{14,12},{17,23},{18,... | collective-permute-start | bytes 786440 | tf_op jit(solution)/shard_map/ppermute | solution.py:365
  142.8 16.2 %collective-permute-start.33 = (bf16[2,256,256]{2,1,0:T(8,128)(2,1)S(1)}, bf16[2,256,256]{2,1,0:T(8,128)(2,1)S(1)}, u32[]{:S(2)}, u32[]{:S(2)}) collective-permute-start(bf16[2,256,256]{2,1,0:T(8,128)(2,1)S(1)} %get-tuple-element.73), channel_id=1, source_target_pairs={{1,0},{2,3},{5,4},{6,7},{9,8},{10,11},{13,12},{14,15},{17,16},{18,... | collective-permute-start | bytes 786440 | tf_op jit(solution)/shard_map/ppermute | solution.py:365
  178.0 15.7 %collective-permute-start.35 = (bf16[2,256,256]{2,1,0:T(8,128)(2,1)S(1)}, bf16[2,256,256]{2,1,0:T(8,128)(2,1)S(1)}, u32[]{:S(2)}, u32[]{:S(2)}) collective-permute-start(bf16[2,256,256]{2,1,0:T(8,128)(2,1)S(1)} %get-tuple-element.77), channel_id=1, source_target_pairs={{0,16},{4,20},{8,24},{9,25},{12,28},{13,29},{18,2},{19,3},{22,6},{... | collective-permute-start | bytes 786440 | tf_op jit(solution)/shard_map/ppermute | solution.py:365
  (19 other events, 153.4 us)

commit v5 on v4

--- a/solution.py
+++ b/solution.py
@@ -164,7 +164,7 @@
     )
 
 
-def far_body(s_ref, xa, xb, y0, y1, st, *refs, total):
+def far_body(s_ref, xa, xb, y0, y1, st, first_tiles, *refs, total):
     xs, outs = refs[-1], refs[:-1]
     half = xa.shape[0]
     n = y0.shape[0] // 2
@@ -202,7 +202,7 @@
     )
 
 
-CHIP, CORE, PLANE, PLANES, LOW, LOWER, _, SHIFT, EARLY = range(9)
+CHIP, CORE, PLANE, PLANES, LOW, LOWER, _, SHIFT, _ = range(9)
 
 
 def turn_body(s_ref, own, r1, r2, r3, *outs, turns, keeps):
@@ -240,78 +240,63 @@
             o[i] = value
 
 
-def row_total(v):
-    return jnp.sum(v.T, axis=0, keepdims=True)
+def column_total(v):
+    return jnp.sum(v, axis=0, keepdims=True)
+
+
+def column_place(k, i, n):
+    return pl.ds(pl.multiple_of((i ^ (k % 2)) * n, n), n)
 
 
 def early_body(s_ref, t0, t1, ru, rd, *refs):
     outs, sums = refs[:-1], refs[-1]
     k, g = s_ref[CHIP], s_ref[PLANE]
     n = t0.shape[-1]
-    sums[...] = jnp.zeros_like(sums)
     for i in range(2):
-        lanes = slice(i * n, i * n + n)
         own = power(t0[0, i])
         same = lax.broadcasted_iota(jnp.int32, (n, n), 0) == lax.broadcasted_iota(
             jnp.int32, (n, n), 1
         )
         own = jnp.where(same & (k == 0), 0.0, own)
-        put_slot(outs, g ^ k, i, own.astype(jnp.bfloat16))
-        sums[pl.ds(g, 1), lanes] = row_total(own)
         low = power(t1[0, i] + decode(ru[i]))
         high = power(t1[1, i] + decode(rd[i]))
-
-        @pl.when(g > 0)
-        def _():
-            put_slot(outs, (g - 1) ^ k, i, low.astype(jnp.bfloat16))
-            sums[pl.ds(g - 1, 1), lanes] = row_total(low)
-
-        @pl.when(g < s_ref[PLANES] - 1)
-        def _():
-            put_slot(outs, (g + 1) ^ k, i, high.astype(jnp.bfloat16))
-            sums[pl.ds(g + 1, 1), lanes] = row_total(high)
+        has_low, has_high = g > 0, g < s_ref[PLANES] - 1
+        put_slot(outs, g ^ k, i, own.astype(jnp.bfloat16))
+        put_slot(outs, jnp.where(has_low, (g - 1) ^ k, -1), i, low.astype(jnp.bfloat16))
+        put_slot(outs, jnp.where(has_high, (g + 1) ^ k, -1), i, high.astype(jnp.bfloat16))
+        sums[0:1, column_place(k, i, n)] = (
+            column_total(own)
+            + jnp.where(has_low, column_total(low), 0.0)
+            + jnp.where(has_high, column_total(high), 0.0)
+        )
 
 
 def late_body(s_ref, t2, r2, rf, rn, before, *refs):
-    outs, sums = refs[:-1], refs[-1]
+    outs, sums = refs[4:-1], refs[-1]
     k, g = s_ref[CHIP], s_ref[PLANE]
     n = t2.shape[-1]
     outer = (g == 0) | (g == s_ref[PLANES] - 1)
-    sums[...] = before[...]
     for i in range(2):
-        lanes = slice(i * n, i * n + n)
+        at = column_place(k, i, n)
         two = power(t2[0, i] + decode(r2[i]))
+        three = power(decode(rf[i]) + decode(rn[i]))
         put_slot(outs, g ^ 2 ^ k, i, two.astype(jnp.bfloat16))
-        sums[pl.ds(g ^ 2, 1), lanes] = row_total(two)
-
-        @pl.when(outer)
-        def _():
-            three = power(decode(rf[i]) + decode(rn[i]))
-            put_slot(outs, g ^ 3 ^ k, i, three.astype(jnp.bfloat16))
-            sums[pl.ds(g ^ 3, 1), lanes] = row_total(three)
-
-
-def place_body(s_ref, e0, e1, e2, e3, l0, l1, l2, l3, out_ref):
+        put_slot(outs, jnp.where(outer, g ^ 3 ^ k, -1), i, three.astype(jnp.bfloat16))
+        sums[0:1, at] = (
+            before[0:1, at] + column_total(two) + jnp.where(outer, column_total(three), 0.0)
+        )
+
+
+def place_body(s_ref, t0, t1, t2, t3, out_ref):
     x = s_ref[SHIFT]
-    is_early = s_ref[EARLY]
-    early, late = (e0, e1, e2, e3), (l0, l1, l2, l3)
-    t = e0.shape[-1]
-
-    def place(tiles):
-        for i in range(2):
-            for c in range(4):
-                v = tiles[c ^ i][i]
-                for m in range(1, 4):
-                    v = jnp.where(x == m, tiles[c ^ i ^ m][i], v)
-                out_ref[i * t : i * t + t, c * t : c * t + t] = v.astype(jnp.float32)
-
-    @pl.when(is_early == 1)
-    def _():
-        place(early)
-
-    @pl.when(is_early == 0)
-    def _():
-        place(late)
+    tiles = (t0, t1, t2, t3)
+    t = t0.shape[-1]
+    for i in range(2):
+        for c in range(4):
+            v = tiles[c ^ i][i]
+            for m in range(1, 4):
+                v = jnp.where(x == m, tiles[c ^ i ^ m][i], v)
+            out_ref[i * t : i * t + t, c * t : c * t + t] = v.astype(jnp.float32)
 
 
 def pay_body(s_ref, a, *refs):
@@ -323,8 +308,13 @@
     out_n[...] = a[pl.ds(first, n)]
 
 
-def hold_body(a, out):
+def hold_body(a, sums, out, chip):
+    n = a.shape[0] // 2
     out[...] = a[...]
+    wide = a[...].astype(jnp.float32)
+    chip[0:1] = sums[0:1] + jnp.sum(wide[:n], axis=0, keepdims=True)
+    chip[1:2] = sums[1:2] + jnp.sum(wide[n:], axis=0, keepdims=True)
+    chip[2:3] = sums[2:3] + jnp.sum(wide * wide, axis=0, keepdims=True)
 
 
 def limit(mib):
@@ -369,8 +359,6 @@
     shape = jax.ShapeDtypeStruct
 
     last = n_genes - 1
-    own = normalize(counts, library)
-    oth = send(own, flip)
     info = jnp.stack(
         [
             k,
@@ -385,6 +373,8 @@
         ]
     ).astype(jnp.int32)
 
+    own = normalize(counts, library)
+    oth = send(own, flip)
     pay_in = pl.BlockSpec((rows, half), lambda i, sc: (0, sc[CORE]))
     pay_shapes = [shape((half, rows), bf16)] * 2 + [shape((rows, half), bf16)]
 
@@ -410,37 +400,36 @@
     widened = own.astype(f32)
     halves = jnp.sum(widened.reshape(2, half_cells, width), axis=1)
     squares = jnp.sum(widened * widened, axis=0)
-    local = jnp.concatenate([halves, squares[None]])
-    chip = local + send(local, flip)
+    oth, chip = pl.pallas_call(
+        hold_body,
+        in_specs=[whole()] * 2,
+        out_specs=[whole()] * 2,
+        out_shape=[shape(oth.shape, bf16), shape((3, width), f32)],
+        compiler_params=limit(14),
+        name="hold",
+    )(oth, jnp.concatenate([halves, squares[None]]))
     chip_halves = chip[:2]
-    pair = jnp.stack([chip[0] + chip[1], chip[2]])
-    around = [send(pair, lambda k, h, g, j=j: (k ^ j, h, g)) for j in (1, 2, 3)]
-    sums = (pair + around[0]) + (around[1] + around[2])
+    around = [send(chip, lambda k, h, g, j=j: (k ^ j, h, g)) for j in (1, 2, 3)]
+    every = (chip + around[0]) + (around[1] + around[2])
+    sums = [every[0] + every[1], every[2]]
     means = sums[0] / total
     variances = sums[1] / total - means * means
-    mine = jnp.concatenate(
+    packed = jnp.concatenate(
         [means[None], lax.rsqrt(variances + 1e-05)[None], chip_halves, jnp.zeros((4, width), f32)]
     )
-    afar = [send(mine, lambda k, h, g, d=d: (k, h, g ^ d)) for d in (1, 2, 3)]
-    own_stats = mine[None]
-    stats = jnp.stack([mine] + afar)
+    afar = [send(packed, lambda k, h, g, d=d: (k, h, g ^ d)) for d in (1, 2, 3)]
+    own_stats = packed[None]
+    stats = jnp.stack([packed] + afar)
     near = send(
         end, lambda k, h, g: (k, h, 1) if g == 0 else ((k, h, g - 1) if g == last else None)
     )
 
-    oth = pl.pallas_call(
-        hold_body,
-        in_specs=[whole()],
-        out_specs=whole(),
-        out_shape=shape(oth.shape, bf16),
-        compiler_params=limit(8),
-        name="hold",
-    )(oth)
-
-    def blocks(body, n, scratch, *operands):
+    def blocks(body, n, scratch, *operands, behind=0):
         return pl.pallas_call(
             functools.partial(body, total=total),
-            in_specs=[scalars()] + [whole()] * len(operands),
+            in_specs=[scalars()]
+            + [whole()] * (len(operands) - behind)
+            + [pl.BlockSpec(memory_space=pl.ANY)] * behind,
             out_specs=[whole()] * 4,
             out_shape=[shape((n, 2, tile, tile), f32)]
             + [shape((n, 2, tile, tile), bf16)] * 3,
@@ -455,7 +444,6 @@
     kept = (half, rows)
     w0 = blocks(diagonal_body, 1, [], pay_a, pay_b, own, oth, own_stats)
     w1 = blocks(near_body, 2, [], up1, dn1, own, oth, stats)
-    w2 = blocks(far_body, 1, [kept], up2, dn2, own, oth, stats)
     w3 = blocks(ends_body, 1, [kept, (rows, width)], up2, dn2, near, near_other, stats)
 
     def reduce_tiles(w):
@@ -476,6 +464,7 @@
         )(info, *parts)
 
     (t0,) = turn(reduce_tiles(w0), [None], [None])
+    w2 = blocks(far_body, 1, [kept], up2, dn2, own, oth, stats, t0, behind=1)
     t1, e_up, e_dn = turn(reduce_tiles(w1), [0, 1], [None, None])
     t2, e_two = turn(reduce_tiles(w2), [0], [None])
     _, e_three, k_three = turn(reduce_tiles(w3), [0], [1])
@@ -488,46 +477,30 @@
     r3f = send(e_three, side(lambda g: (g ^ 2) if inner(g) else None))
     r3n = send(k_three, lambda k, h, g: (k, h, g ^ 1) if inner(g) else None)
 
-    def finish(body, *operands):
+    def finish(body, *operands, over=0):
         return pl.pallas_call(
             body,
             in_specs=[scalars()] + [whole()] * len(operands),
+            input_output_aliases={1 + len(operands) - over + n: n for n in range(over)},
             out_specs=[whole()] * 5,
-            out_shape=[small] * 4 + [shape((n_genes, half), f32)],
+            out_shape=[small] * 4 + [shape((1, half), f32)],
             compiler_params=limit(10),
             name="finish_tiles",
         )(info, *operands)
 
-    *early, early_sums = finish(early_body, t0, t1, ru, rd)
-    *late, tile_sums = finish(late_body, t2, r2, r3f, r3n, early_sums)
-
-    is_early = lambda q, g: -1 <= q - g <= 1
-    got_early, got_late = [early[0]], [late[0]]
-    for j in range(1, 4):
-        got_early.append(
-            send(early[j], lambda k, h, g, j=j: (k ^ j, h, g) if is_early(k ^ j, g) else None)
-        )
-        got_late.append(
-            send(late[j], lambda k, h, g, j=j: (k ^ j, h, g) if not is_early(k ^ j, g) else None)
-        )
+    *close, close_sums = finish(early_body, t0, t1, ru, rd)
+    *tiles, tile_sums = finish(late_body, t2, r2, r3f, r3n, close_sums, *close, over=len(close))
+    got = [tiles[0]] + [send(tiles[j], lambda k, h, g, j=j: (k ^ j, h, g)) for j in (1, 2, 3)]
     adjacency = pl.pallas_call(
         place_body,
-        in_specs=[scalars()] + [whole()] * 8,
+        in_specs=[scalars()] + [whole()] * 4,
         out_specs=whole(),
         out_shape=shape((half, width), f32),
         compiler_params=limit(12),
         name="place_tiles",
-    )(info, *got_early, *got_late)
-    over = [send(tile_sums, lambda k, h, g, d=d: (k, h, g ^ d)) for d in (1, 2, 3)]
-    chip_sums = (tile_sums + over[0]) + (over[1] + over[2])
-
-    def rows_of(q):
-        return lax.dynamic_index_in_dim(chip_sums, q, 0, keepdims=False)
-
-    inside = [rows_of(k)] + [
-        send(rows_of(k ^ j), lambda k, h, g, j=j: (k ^ j, h, g)) for j in (1, 2, 3)
-    ]
-    connectivity = (inside[0] + inside[1]) + (inside[2] + inside[3])
+    )(info, *got)
+    sums = [send(tile_sums, lambda k, h, g, m=m: (g, h ^ (k // 2), k ^ m)) for m in range(4)]
+    connectivity = ((sums[0] + sums[1]) + (sums[2] + sums[3])).reshape(half)
     return (adjacency, connectivity)
 
 

time: 198 us -> 193 us (0.975)
  starting transfers between devices: 81.5 us -> 69.7 us
  waiting for transfers between devices: 78.2 us -> 84.5 us
    ppermute x43 -> x37, starting transfers between devices: 81.5 us -> 69.7 us  [send(): return lax.ppermute(x, AXES, perm(f))]
    ppermute x43 -> x37, waiting for transfers between devices: 78.2 us -> 84.5 us  [send(): return lax.ppermute(x, AXES, perm(f))]
  transfers between devices with their start and end apart: 43 -> 37, of which waited for: 20 -> 20; matrix products, arithmetic and copies ran while one was open for 1% -> 1% of each run, Pallas kernels for 12% -> 12%
where the time goes in v5:
time: 193 us; the launch traced here: 190 us
  waiting for transfers between devices  84.5 us (44%)
  starting transfers between devices  69.7 us (36%)
  Pallas kernels  28.6 us (15%)
  other arithmetic  5.84 us (3%)
    ppermute x37, waiting for transfers between devices, send(): return lax.ppermute(x, AXES, perm(f))  84.5 us
    ppermute x37, starting transfers between devices, send(): return lax.ppermute(x, AXES, perm(f))  69.7 us
    pallas_call x4, Pallas kernels, blocks(): pl.pallas_call(functools.partial(body, total=total), in_specs=[scalars()]...  12.6 us
    pallas_call x4, Pallas kernels, turn(): pl.pallas_call(functools.partial(turn_body, turns=turns, keeps=keeps), in...  5.84 us
    reduce_sum x1, other arithmetic, folded_shards(): halves = jnp.sum(widened.reshape(2, half_cells, width), axis=1)  3.96 us
  transfers between devices with their start and end apart: 37, of which 20 were waited for; matrix products, arithmetic and copies ran while one was open for 1% of the time, Pallas kernels for 12%

profile of v5, /device:TPU:0, one launch (start us, length us, event | category | flops | bytes accessed | tf_op | source)
XLA Modules:
  0.0 189.7 jit_solution(17296766046990644197)
XLA Ops:
  1.3 4.0 %bitcast_reduce_fusion = (f32[2,1024]{1,0:T(2,128)S(1)}, bf16[1024,1024]{1,0:T(8,128)(2,1)S(1)}) fusion(f32[1024]{0:T(1024)S(1)} %convert_divide_fusion, s32[1024,1024]{1,0:T(8,128)} %param.2), kind=kLoop, calls=%fused_computation | loop fusion | flops 5240832 | bytes 6303744 | tf_op jit(solution)/shard_map/reduce_sum | solution.py:401
  6.9 2.8 %collective-permute-done.a = bf16[1024,1024]{1,0:T(8,128)(2,1)} collective-permute-done((bf16[1024,1024]{1,0:T(8,128)(2,1)S(1)}, bf16[1024,1024]{1,0:T(8,128)(2,1)}, u32[]{:S(2)}, u32[]{:S(2)}) %collective-permute-start) | collective-permute-done | bytes 2097184 | tf_op jit(solution)/shard_map/ppermute | solution.py:355
  11.9 4.9 %collective-permute-start.1 = (bf16[512,1024]{1,0:T(8,128)(2,1)S(1)}, bf16[512,1024]{1,0:T(8,128)(2,1)S(1)}, u32[]{:S(2)}, u32[]{:S(2)}) collective-permute-start(bf16[512,1024]{1,0:T(8,128)(2,1)S(1)} %get-tuple-element.46.xa), channel_id=1, source_target_pairs={{0,1},{1,2},{2,3},{4,5},{5,6},{6,7},{8,9},{9,10},{10,11},{12,13},{... | collective-permute-start | bytes 3145736 | tf_op jit(solution)/shard_map/ppermute | solution.py:355
  18.1 4.6 %collective-permute-start.18 = (bf16[1024,512]{1,0:T(8,128)(2,1)S(1)}, bf16[1024,512]{1,0:T(8,128)(2,1)S(1)}, u32[]{:S(2)}, u32[]{:S(2)}) collective-permute-start(bf16[1024,512]{1,0:T(8,128)(2,1)S(1)} %get-tuple-element.60), channel_id=1, source_target_pairs={{0,1},{3,2},{4,5},{7,6},{8,9},{11,10},{12,13},{15,14},{16,17},{19,... | collective-permute-start | bytes 3145736 | tf_op jit(solution)/shard_map/ppermute | solution.py:355
  30.7 9.6 %collective-permute-done.1.xa = bf16[512,1024]{1,0:T(8,128)(2,1)S(1)} collective-permute-done((bf16[512,1024]{1,0:T(8,128)(2,1)S(1)}, bf16[512,1024]{1,0:T(8,128)(2,1)S(1)}, u32[]{:S(2)}, u32[]{:S(2)}) %collective-permute-start.1) | collective-permute-done | bytes 1048608 | tf_op jit(solution)/shard_map/ppermute | solution.py:355
  45.0 16.9 %collective-permute-done.18.na = bf16[1024,512]{1,0:T(8,128)(2,1)S(1)} collective-permute-done((bf16[1024,512]{1,0:T(8,128)(2,1)S(1)}, bf16[1024,512]{1,0:T(8,128)(2,1)S(1)}, u32[]{:S(2)}, u32[]{:S(2)}) %collective-permute-start.18) | collective-permute-done | bytes 1048608 | tf_op jit(solution)/shard_map/ppermute | solution.py:355
  61.9 3.4 %partial_blocks.4 = (f32[1,2,256,256]{3,2,1,0:T(8,128)S(1)}, bf16[1,2,256,256]{3,2,1,0:T(8,128)(2,1)S(1)}, bf16[1,2,256,256]{3,2,1,0:T(8,128)(2,1)S(1)}, bf16[1,2,256,256]{3,2,1,0:T(8,128)(2,1)S(1)}) custom-call(s32[9]{0:T(128)S(1)} %stack.58.s_ref, bf16[512,1024]{1,0:T(8,128)(2,1)S(1)} %get-tuple-element.46.xa, bf16[512,1024]{1,0:T(8,128)(2,1)S(1)} %get-tuple-element.47.xb, ...), custom_call_target="tpu_custom_call" | custom-call | tf_op jit(solution)/shard_map/partial_blocks/pallas_call | solution.py:428
  66.9 5.7 %collective-permute-start.10 = (f32[8,1024]{1,0:T(8,128)S(1)}, f32[8,1024]{1,0:T(8,128)S(1)}, u32[]{:S(2)}, u32[]{:S(2)}) collective-permute-start(f32[8,1024]{1,0:T(8,128)S(1)} %get-tuple-element.89), channel_id=1, source_target_pairs={{0,3},{1,2},{2,1},{3,0},{4,7},{5,6},{6,5},{7,4},{8,11},{9,10},{10,... | collective-permute-start | bytes 98312 | tf_op jit(solution)/shard_map/ppermute | solution.py:355
  74.5 3.3 %collective-permute-start.9 = (f32[8,1024]{1,0:T(8,128)S(1)}, f32[8,1024]{1,0:T(8,128)S(1)}, u32[]{:S(2)}, u32[]{:S(2)}) collective-permute-start(f32[8,1024]{1,0:T(8,128)S(1)} %get-tuple-element.89), channel_id=1, source_target_pairs={{0,2},{1,3},{2,0},{3,1},{4,6},{5,7},{6,4},{7,5},{8,10},{9,11},{10,... | collective-permute-start | bytes 98312 | tf_op jit(solution)/shard_map/ppermute | solution.py:355
  80.9 2.7 %collective-permute-done.8 = f32[8,1024]{1,0:T(8,128)S(1)} collective-permute-done((f32[8,1024]{1,0:T(8,128)S(1)}, f32[8,1024]{1,0:T(8,128)S(1)}, u32[]{:S(2)}, u32[]{:S(2)}) %collective-permute-start.8) | collective-permute-done | bytes 32800 | tf_op jit(solution)/shard_map/ppermute | solution.py:355
  85.6 4.0 %partial_blocks.7 = (f32[2,2,256,256]{3,2,1,0:T(8,128)S(1)}, bf16[2,2,256,256]{3,2,1,0:T(8,128)(2,1)S(1)}, bf16[2,2,256,256]{3,2,1,0:T(8,128)(2,1)S(1)}, bf16[2,2,256,256]{3,2,1,0:T(8,128)(2,1)S(1)}) custom-call(s32[9]{0:T(128)S(1)} %stack.58.s_ref, bf16[512,1024]{1,0:T(8,128)(2,1)S(1)} %collective-permute-done.1.xa, ...), custom_call_target="tpu_custom_call" | custom-call | tf_op jit(solution)/shard_map/partial_blocks/pallas_call | solution.py:428
  89.6 5.2 %collective-permute-done.12.r2 = bf16[1,2,256,256]{3,2,1,0:T(8,128)(2,1)S(1)} collective-permute-done((bf16[1,2,256,256]{3,2,1,0:T(8,128)(2,1)S(1)}, bf16[1,2,256,256]{3,2,1,0:T(8,128)(2,1)S(1)}, u32[]{:S(2)}, u32[]{:S(2)}) %collective-permute-start.12) | collective-permute-done | bytes 262176 | tf_op jit(solution)/shard_map/ppermute | solution.py:355
  106.5 3.0 %collective-permute-done.25.r1 = bf16[2,2,256,256]{3,2,1,0:T(8,128)(2,1)S(1)} collective-permute-done((bf16[2,2,256,256]{3,2,1,0:T(8,128)(2,1)S(1)}, bf16[2,2,256,256]{3,2,1,0:T(8,128)(2,1)S(1)}, u32[]{:S(2)}, u32[]{:S(2)}) %collective-permute-start.25) | collective-permute-done | bytes 524320 | tf_op jit(solution)/shard_map/ppermute | solution.py:355
  111.0 9.9 %collective-permute-done.26.r2 = bf16[2,2,256,256]{3,2,1,0:T(8,128)(2,1)S(1)} collective-permute-done((bf16[2,2,256,256]{3,2,1,0:T(8,128)(2,1)S(1)}, bf16[2,2,256,256]{3,2,1,0:T(8,128)(2,1)S(1)}, u32[]{:S(2)}, u32[]{:S(2)}) %collective-permute-start.26) | collective-permute-done | bytes 524320 | tf_op jit(solution)/shard_map/ppermute | solution.py:355
  123.3 3.0 %collective-permute-start.21 = (bf16[1,2,256,256]{3,2,1,0:T(8,128)(2,1)S(1)}, bf16[1,2,256,256]{3,2,1,0:T(8,128)(2,1)S(1)}, u32[]{:S(2)}, u32[]{:S(2)}) collective-permute-start(bf16[1,2,256,256]{3,2,1,0:T(8,128)(2,1)S(1)} %get-tuple-element.63), channel_id=1, source_target_pairs={{0,16},{1,17},{2,18},{3,19},{4,20},{5,21},{6,22},{7,23},{8,24},{9,... | collective-permute-start | bytes 786440 | tf_op jit(solution)/shard_map/ppermute | solution.py:355
  132.1 3.2 %collective-permute-start.28 = (bf16[2,256,256]{2,1,0:T(8,128)(2,1)S(1)}, bf16[2,256,256]{2,1,0:T(8,128)(2,1)S(1)}, u32[]{:S(2)}, u32[]{:S(2)}) collective-permute-start(bf16[2,256,256]{2,1,0:T(8,128)(2,1)S(1)} %get-tuple-element.72), channel_id=1, source_target_pairs={{0,1},{1,2},{2,3},{4,5},{5,6},{6,7},{8,9},{9,10},{10,11},{12,13},{... | collective-permute-start | bytes 786440 | tf_op jit(solution)/shard_map/ppermute | solution.py:355
  137.8 4.1 %collective-permute-start.17 = (bf16[2,256,256]{2,1,0:T(8,128)(2,1)S(1)}, bf16[2,256,256]{2,1,0:T(8,128)(2,1)S(1)}, u32[]{:S(2)}, u32[]{:S(2)}) collective-permute-start(bf16[2,256,256]{2,1,0:T(8,128)(2,1)S(1)} %get-tuple-element.59), channel_id=1, source_target_pairs={{0,2},{1,3},{2,0},{3,1},{4,6},{5,7},{6,4},{7,5},{8,10},{9,11},{10,... | collective-permute-start | bytes 786440 | tf_op jit(solution)/shard_map/ppermute | solution.py:355
  148.2 5.9 %collective-permute-done.17.r2 = bf16[2,256,256]{2,1,0:T(8,128)(2,1)S(1)} collective-permute-done((bf16[2,256,256]{2,1,0:T(8,128)(2,1)S(1)}, bf16[2,256,256]{2,1,0:T(8,128)(2,1)S(1)}, u32[]{:S(2)}, u32[]{:S(2)}) %collective-permute-start.17) | collective-permute-done | bytes 262176 | tf_op jit(solution)/shard_map/ppermute | solution.py:355
  154.1 2.8 %collective-permute-done.23.rf = bf16[2,256,256]{2,1,0:T(8,128)(2,1)S(1)} collective-permute-done((bf16[2,256,256]{2,1,0:T(8,128)(2,1)S(1)}, bf16[2,256,256]{2,1,0:T(8,128)(2,1)S(1)}, u32[]{:S(2)}, u32[]{:S(2)}) %collective-permute-start.23) | collective-permute-done | bytes 262176 | tf_op jit(solution)/shard_map/ppermute | solution.py:355
  156.9 5.5 %collective-permute-done.24.rn = bf16[2,256,256]{2,1,0:T(8,128)(2,1)S(1)} collective-permute-done((bf16[2,256,256]{2,1,0:T(8,128)(2,1)S(1)}, bf16[2,256,256]{2,1,0:T(8,128)(2,1)S(1)}, u32[]{:S(2)}, u32[]{:S(2)}) %collective-permute-start.24) | collective-permute-done | bytes 262176 | tf_op jit(solution)/shard_map/ppermute | solution.py:355
  164.6 7.8 %collective-permute-start.31 = (bf16[2,256,256]{2,1,0:T(8,128)(2,1)S(1)}, bf16[2,256,256]{2,1,0:T(8,128)(2,1)S(1)}, u32[]{:S(2)}, u32[]{:S(2)}) collective-permute-start(bf16[2,256,256]{2,1,0:T(8,128)(2,1)S(1)} %get-tuple-element.81), channel_id=1, source_target_pairs={{0,16},{1,17},{2,18},{3,19},{4,20},{5,21},{6,22},{7,23},{8,24},{9,... | collective-permute-start | bytes 786440 | tf_op jit(solution)/shard_map/ppermute | solution.py:355
  172.4 3.8 %collective-permute-start.36 = (f32[1,512]{1,0:T(1,128)S(1)}, f32[1,512]{1,0:T(1,128)S(1)}, u32[]{:S(2)}, u32[]{:S(2)}) collective-permute-start(f32[1,512]{1,0:T(1,128)S(1)} %get-tuple-element.83), channel_id=1, source_target_pairs={{0,3},{1,11},{2,19},{3,27},{4,7},{5,15},{6,23},{7,31},{8,2},{9,10}... | collective-permute-start | bytes 6152 | tf_op jit(solution)/shard_map/ppermute | solution.py:355
  178.3 5.1 %collective-permute-done.36 = f32[1,512]{1,0:T(1,128)S(1)} collective-permute-done((f32[1,512]{1,0:T(1,128)S(1)}, f32[1,512]{1,0:T(1,128)S(1)}, u32[]{:S(2)}, u32[]{:S(2)}) %collective-permute-start.36) | collective-permute-done | bytes 2080 | tf_op jit(solution)/shard_map/ppermute | solution.py:355
  183.4 3.6 %collective-permute-done.34 = f32[1,512]{1,0:T(1,128)S(1)} collective-permute-done((f32[1,512]{1,0:T(1,128)S(1)}, f32[1,512]{1,0:T(1,128)S(1)}, u32[]{:S(2)}, u32[]{:S(2)}) %collective-permute-start.34) | collective-permute-done | bytes 2080 | tf_op jit(solution)/shard_map/ppermute | solution.py:355
  (77 shorter events, 64.2 us)
Async XLA Ops:
  11.9 28.4 %collective-permute-start.1 = (bf16[512,1024]{1,0:T(8,128)(2,1)S(1)}, bf16[512,1024]{1,0:T(8,128)(2,1)S(1)}, u32[]{:S(2)}, u32[]{:S(2)}) collective-permute-start(bf16[512,1024]{1,0:T(8,128)(2,1)S(1)} %get-tuple-element.46.xa), channel_id=1, source_target_pairs={{0,1},{1,2},{2,3},{4,5},{5,6},{6,7},{8,9},{9,10},{10,11},{12,13},{... | collective-permute-start | bytes 3145736 | tf_op jit(solution)/shard_map/ppermute | solution.py:355
  16.8 26.8 %collective-permute-start.3 = (bf16[512,1024]{1,0:T(8,128)(2,1)S(1)}, bf16[512,1024]{1,0:T(8,128)(2,1)S(1)}, u32[]{:S(2)}, u32[]{:S(2)}) collective-permute-start(bf16[512,1024]{1,0:T(8,128)(2,1)S(1)} %get-tuple-element.47.xb), channel_id=1, source_target_pairs={{1,0},{2,1},{3,2},{5,4},{6,5},{7,6},{9,8},{10,9},{11,10},{13,12},{... | collective-permute-start | bytes 3145736 | tf_op jit(solution)/shard_map/ppermute | solution.py:355
  18.1 43.8 %collective-permute-start.18 = (bf16[1024,512]{1,0:T(8,128)(2,1)S(1)}, bf16[1024,512]{1,0:T(8,128)(2,1)S(1)}, u32[]{:S(2)}, u32[]{:S(2)}) collective-permute-start(bf16[1024,512]{1,0:T(8,128)(2,1)S(1)} %get-tuple-element.60), channel_id=1, source_target_pairs={{0,1},{3,2},{4,5},{7,6},{8,9},{11,10},{12,13},{15,14},{16,17},{19,... | collective-permute-start | bytes 3145736 | tf_op jit(solution)/shard_map/ppermute | solution.py:355
  26.9 14.1 %collective-permute-start.7 = (f32[3,1024]{1,0:T(4,128)S(1)}, f32[3,1024]{1,0:T(4,128)S(1)}, u32[]{:S(2)}, u32[]{:S(2)}) collective-permute-start(f32[3,1024]{1,0:T(4,128)S(1)} %get-tuple-element.49), channel_id=1, source_target_pairs={{0,24},{1,25},{2,26},{3,27},{4,28},{5,29},{6,30},{7,31},{8,16},{9,... | collective-permute-start | bytes 36872 | tf_op jit(solution)/shard_map/ppermute | solution.py:355
  40.3 56.5 %collective-permute-start.2 = (bf16[512,1024]{1,0:T(8,128)(2,1)S(1)}, bf16[512,1024]{1,0:T(8,128)(2,1)S(1)}, u32[]{:S(2)}, u32[]{:S(2)}) collective-permute-start(bf16[512,1024]{1,0:T(8,128)(2,1)S(1)} %collective-permute-done.1.xa), channel_id=1, source_target_pairs={{1,2},{2,3},{5,6},{6,7},{9,10},{10,11},{13,14},{14,15},{17,18},{18... | collective-permute-start | bytes 3145736 | tf_op jit(solution)/shard_map/ppermute | solution.py:355
  43.6 55.6 %collective-permute-start.4 = (bf16[512,1024]{1,0:T(8,128)(2,1)S(1)}, bf16[512,1024]{1,0:T(8,128)(2,1)S(1)}, u32[]{:S(2)}, u32[]{:S(2)}) collective-permute-start(bf16[512,1024]{1,0:T(8,128)(2,1)S(1)} %collective-permute-done.3.xb), channel_id=1, source_target_pairs={{1,0},{2,1},{5,4},{6,5},{9,8},{10,9},{13,12},{14,13},{17,16},{18,1... | collective-permute-start | bytes 3145736 | tf_op jit(solution)/shard_map/ppermute | solution.py:355
  61.9 40.5 %collective-permute-start.19 = (bf16[1024,512]{1,0:T(8,128)(2,1)S(1)}, bf16[1024,512]{1,0:T(8,128)(2,1)S(1)}, u32[]{:S(2)}, u32[]{:S(2)}) collective-permute-start(bf16[1024,512]{1,0:T(8,128)(2,1)S(1)} %collective-permute-done.18.na), channel_id=1, source_target_pairs={{0,4},{1,5},{2,6},{3,7},{4,0},{5,1},{6,2},{7,3},{8,12},{9,13},{10,... | collective-permute-start | bytes 3145736 | tf_op jit(solution)/shard_map/ppermute | solution.py:355
  65.3 19.7 %collective-permute-start.11 = (bf16[1,2,256,256]{3,2,1,0:T(8,128)(2,1)S(1)}, bf16[1,2,256,256]{3,2,1,0:T(8,128)(2,1)S(1)}, u32[]{:S(2)}, u32[]{:S(2)}) collective-permute-start(bf16[1,2,256,256]{3,2,1,0:T(8,128)(2,1)S(1)} %get-tuple-element.51), channel_id=1, source_target_pairs={{0,8},{1,9},{2,10},{3,11},{4,12},{5,13},{6,14},{7,15},{8,0},{9,1},... | collective-permute-start | bytes 786440 | tf_op jit(solution)/shard_map/ppermute | solution.py:355
  94.8 14.8 %collective-permute-start.25 = (bf16[2,2,256,256]{3,2,1,0:T(8,128)(2,1)S(1)}, bf16[2,2,256,256]{3,2,1,0:T(8,128)(2,1)S(1)}, u32[]{:S(2)}, u32[]{:S(2)}) collective-permute-start(bf16[2,2,256,256]{3,2,1,0:T(8,128)(2,1)S(1)} %get-tuple-element.68), channel_id=1, source_target_pairs={{0,8},{1,9},{2,10},{3,11},{4,12},{5,13},{6,14},{7,15},{8,0},{9,1},... | collective-permute-start | bytes 1572872 | tf_op jit(solution)/shard_map/ppermute | solution.py:355
  95.3 25.6 %collective-permute-start.26 = (bf16[2,2,256,256]{3,2,1,0:T(8,128)(2,1)S(1)}, bf16[2,2,256,256]{3,2,1,0:T(8,128)(2,1)S(1)}, u32[]{:S(2)}, u32[]{:S(2)}) collective-permute-start(bf16[2,2,256,256]{3,2,1,0:T(8,128)(2,1)S(1)} %get-tuple-element.69), channel_id=1, source_target_pairs={{0,16},{1,17},{2,18},{3,19},{4,20},{5,21},{6,22},{7,23},{8,24},{9,... | collective-permute-start | bytes 1572872 | tf_op jit(solution)/shard_map/ppermute | solution.py:355
  96.8 26.5 %collective-permute-start.27 = (bf16[2,2,256,256]{3,2,1,0:T(8,128)(2,1)S(1)}, bf16[2,2,256,256]{3,2,1,0:T(8,128)(2,1)S(1)}, u32[]{:S(2)}, u32[]{:S(2)}) collective-permute-start(bf16[2,2,256,256]{3,2,1,0:T(8,128)(2,1)S(1)} %get-tuple-element.70), channel_id=1, source_target_pairs={{0,24},{1,25},{2,26},{3,27},{4,28},{5,29},{6,30},{7,31},{8,16},{9,... | collective-permute-start | bytes 1572872 | tf_op jit(solution)/shard_map/ppermute | solution.py:355
  101.8 24.6 %collective-permute-start.14 = (bf16[1,2,256,256]{3,2,1,0:T(8,128)(2,1)S(1)}, bf16[1,2,256,256]{3,2,1,0:T(8,128)(2,1)S(1)}, u32[]{:S(2)}, u32[]{:S(2)}) collective-permute-start(bf16[1,2,256,256]{3,2,1,0:T(8,128)(2,1)S(1)} %get-tuple-element.55), channel_id=1, source_target_pairs={{0,8},{1,9},{2,10},{3,11},{4,12},{5,13},{6,14},{7,15},{8,0},{9,1},... | collective-permute-start | bytes 786440 | tf_op jit(solution)/shard_map/ppermute | solution.py:355
  102.4 29.7 %collective-permute-start.15 = (bf16[1,2,256,256]{3,2,1,0:T(8,128)(2,1)S(1)}, bf16[1,2,256,256]{3,2,1,0:T(8,128)(2,1)S(1)}, u32[]{:S(2)}, u32[]{:S(2)}) collective-permute-start(bf16[1,2,256,256]{3,2,1,0:T(8,128)(2,1)S(1)} %get-tuple-element.56), channel_id=1, source_target_pairs={{0,16},{1,17},{2,18},{3,19},{4,20},{5,21},{6,22},{7,23},{8,24},{9,... | collective-permute-start | bytes 786440 | tf_op jit(solution)/shard_map/ppermute | solution.py:355
  109.6 25.8 %collective-permute-start.16 = (bf16[1,2,256,256]{3,2,1,0:T(8,128)(2,1)S(1)}, bf16[1,2,256,256]{3,2,1,0:T(8,128)(2,1)S(1)}, u32[]{:S(2)}, u32[]{:S(2)}) collective-permute-start(bf16[1,2,256,256]{3,2,1,0:T(8,128)(2,1)S(1)} %get-tuple-element.57), channel_id=1, source_target_pairs={{0,24},{1,25},{2,26},{3,27},{4,28},{5,29},{6,30},{7,31},{8,16},{9,... | collective-permute-start | bytes 786440 | tf_op jit(solution)/shard_map/ppermute | solution.py:355
  120.9 16.9 %collective-permute-start.20 = (bf16[1,2,256,256]{3,2,1,0:T(8,128)(2,1)S(1)}, bf16[1,2,256,256]{3,2,1,0:T(8,128)(2,1)S(1)}, u32[]{:S(2)}, u32[]{:S(2)}) collective-permute-start(bf16[1,2,256,256]{3,2,1,0:T(8,128)(2,1)S(1)} %get-tuple-element.62), channel_id=1, source_target_pairs={{0,8},{1,9},{2,10},{3,11},{4,12},{5,13},{6,14},{7,15},{8,0},{9,1},... | collective-permute-start | bytes 786440 | tf_op jit(solution)/shard_map/ppermute | solution.py:355
  123.3 18.6 %collective-permute-start.21 = (bf16[1,2,256,256]{3,2,1,0:T(8,128)(2,1)S(1)}, bf16[1,2,256,256]{3,2,1,0:T(8,128)(2,1)S(1)}, u32[]{:S(2)}, u32[]{:S(2)}) collective-permute-start(bf16[1,2,256,256]{3,2,1,0:T(8,128)(2,1)S(1)} %get-tuple-element.63), channel_id=1, source_target_pairs={{0,16},{1,17},{2,18},{3,19},{4,20},{5,21},{6,22},{7,23},{8,24},{9,... | collective-permute-start | bytes 786440 | tf_op jit(solution)/shard_map/ppermute | solution.py:355
  126.4 15.8 %collective-permute-start.22 = (bf16[1,2,256,256]{3,2,1,0:T(8,128)(2,1)S(1)}, bf16[1,2,256,256]{3,2,1,0:T(8,128)(2,1)S(1)}, u32[]{:S(2)}, u32[]{:S(2)}) collective-permute-start(bf16[1,2,256,256]{3,2,1,0:T(8,128)(2,1)S(1)} %get-tuple-element.64), channel_id=1, source_target_pairs={{0,24},{1,25},{2,26},{3,27},{4,28},{5,29},{6,30},{7,31},{8,16},{9,... | collective-permute-start | bytes 786440 | tf_op jit(solution)/shard_map/ppermute | solution.py:355
  132.1 14.6 %collective-permute-start.28 = (bf16[2,256,256]{2,1,0:T(8,128)(2,1)S(1)}, bf16[2,256,256]{2,1,0:T(8,128)(2,1)S(1)}, u32[]{:S(2)}, u32[]{:S(2)}) collective-permute-start(bf16[2,256,256]{2,1,0:T(8,128)(2,1)S(1)} %get-tuple-element.72), channel_id=1, source_target_pairs={{0,1},{1,2},{2,3},{4,5},{5,6},{6,7},{8,9},{9,10},{10,11},{12,13},{... | collective-permute-start | bytes 786440 | tf_op jit(solution)/shard_map/ppermute | solution.py:355
  137.8 16.4 %collective-permute-start.17 = (bf16[2,256,256]{2,1,0:T(8,128)(2,1)S(1)}, bf16[2,256,256]{2,1,0:T(8,128)(2,1)S(1)}, u32[]{:S(2)}, u32[]{:S(2)}) collective-permute-start(bf16[2,256,256]{2,1,0:T(8,128)(2,1)S(1)} %get-tuple-element.59), channel_id=1, source_target_pairs={{0,2},{1,3},{2,0},{3,1},{4,6},{5,7},{6,4},{7,5},{8,10},{9,11},{10,... | collective-permute-start | bytes 786440 | tf_op jit(solution)/shard_map/ppermute | solution.py:355
  144.2 12.7 %collective-permute-start.23 = (bf16[2,256,256]{2,1,0:T(8,128)(2,1)S(1)}, bf16[2,256,256]{2,1,0:T(8,128)(2,1)S(1)}, u32[]{:S(2)}, u32[]{:S(2)}) collective-permute-start(bf16[2,256,256]{2,1,0:T(8,128)(2,1)S(1)} %get-tuple-element.65), channel_id=1, source_target_pairs={{1,3},{2,0},{5,7},{6,4},{9,11},{10,8},{13,15},{14,12},{17,23},{18,... | collective-permute-start | bytes 786440 | tf_op jit(solution)/shard_map/ppermute | solution.py:355
  145.5 17.0 %collective-permute-start.24 = (bf16[2,256,256]{2,1,0:T(8,128)(2,1)S(1)}, bf16[2,256,256]{2,1,0:T(8,128)(2,1)S(1)}, u32[]{:S(2)}, u32[]{:S(2)}) collective-permute-start(bf16[2,256,256]{2,1,0:T(8,128)(2,1)S(1)} %get-tuple-element.66), channel_id=1, source_target_pairs={{1,0},{2,3},{5,4},{6,7},{9,8},{10,11},{13,12},{14,15},{17,16},{18,... | collective-permute-start | bytes 786440 | tf_op jit(solution)/shard_map/ppermute | solution.py:355
  163.9 23.6 %collective-permute-start.30 = (bf16[2,256,256]{2,1,0:T(8,128)(2,1)S(1)}, bf16[2,256,256]{2,1,0:T(8,128)(2,1)S(1)}, u32[]{:S(2)}, u32[]{:S(2)}) collective-permute-start(bf16[2,256,256]{2,1,0:T(8,128)(2,1)S(1)} %get-tuple-element.80), channel_id=1, source_target_pairs={{0,8},{1,9},{2,10},{3,11},{4,12},{5,13},{6,14},{7,15},{8,0},{9,1},... | collective-permute-start | bytes 786440 | tf_op jit(solution)/shard_map/ppermute | solution.py:355
  164.6 22.9 %collective-permute-start.31 = (bf16[2,256,256]{2,1,0:T(8,128)(2,1)S(1)}, bf16[2,256,256]{2,1,0:T(8,128)(2,1)S(1)}, u32[]{:S(2)}, u32[]{:S(2)}) collective-permute-start(bf16[2,256,256]{2,1,0:T(8,128)(2,1)S(1)} %get-tuple-element.81), channel_id=1, source_target_pairs={{0,16},{1,17},{2,18},{3,19},{4,20},{5,21},{6,22},{7,23},{8,24},{9,... | collective-permute-start | bytes 786440 | tf_op jit(solution)/shard_map/ppermute | solution.py:355
  172.4 15.1 %collective-permute-start.32 = (bf16[2,256,256]{2,1,0:T(8,128)(2,1)S(1)}, bf16[2,256,256]{2,1,0:T(8,128)(2,1)S(1)}, u32[]{:S(2)}, u32[]{:S(2)}) collective-permute-start(bf16[2,256,256]{2,1,0:T(8,128)(2,1)S(1)} %get-tuple-element.82), channel_id=1, source_target_pairs={{0,24},{1,25},{2,26},{3,27},{4,28},{5,29},{6,30},{7,31},{8,16},{9,... | collective-permute-start | bytes 786440 | tf_op jit(solution)/shard_map/ppermute | solution.py:355
  (13 other events, 95.2 us)

commit v6 on v5

--- a/solution.py
+++ b/solution.py
@@ -111,17 +111,24 @@
     return lambda first, n: st[plane, :, pl.ds(first, n)]
 
 
-def diagonal_body(s_ref, xa, xb, y0, y1, st, *outs, total):
-    half = xa.shape[0]
+def stacked(products):
+    return jnp.concatenate(products, axis=0)
+
+
+def diagonal_body(s_ref, a0, a1, b0, b1, y0, y1, st, *outs, total):
+    half = 2 * a0.shape[0]
     n = y0.shape[0] // 2
 
     def product(first, w):
         lanes = pl.ds(first, w)
-        return (
-            plain(xa[:, :n], y0[:n, lanes])
-            + plain(xa[:, n:], y1[:n, lanes])
-            + plain(xb[:, :n], y0[n:, lanes])
-            + plain(xb[:, n:], y1[n:, lanes])
+        return stacked(
+            [
+                plain(xa[:, :n], y0[:n, lanes])
+                + plain(xa[:, n:], y1[:n, lanes])
+                + plain(xb[:, :n], y0[n:, lanes])
+                + plain(xb[:, n:], y1[n:, lanes])
+                for xa, xb in ((a0, b0), (a1, b1))
+            ]
         )
 
     put_tiles(
@@ -130,15 +137,17 @@
     )
 
 
-def near_body(s_ref, xa, xb, y0, y1, st, *outs, total):
-    half = xa.shape[0]
+def near_body(s_ref, a0, a1, b0, b1, y0, y1, st, *outs, total):
+    half = 2 * a0.shape[0]
     n = y0.shape[0] // 2
-    for blk, x in enumerate((xa, xb)):
+    for blk, xs in enumerate(((a0, a1), (b0, b1))):
         cells = slice(blk * n, blk * n + n)
 
         def product(first, w):
             lanes = pl.ds(first, w)
-            return plain(x[:, :n], y0[cells, lanes]) + plain(x[:, n:], y1[cells, lanes])
+            return stacked(
+                [plain(x[:, :n], y0[cells, lanes]) + plain(x[:, n:], y1[cells, lanes]) for x in xs]
+            )
 
         put_tiles(
             product, lambda v: v[2 + blk : 3 + blk], s_ref, blk,
@@ -147,14 +156,18 @@
         )
 
 
-def pick_far(s_ref, xa, xb, xs):
+def pick_far(s_ref, a0, a1, b0, b1, xs):
+    t = a0.shape[0]
+
     @pl.when(s_ref[LOW] == 0)
     def _():
-        xs[...] = xa[...]
+        xs[:t] = a0[...]
+        xs[t:] = a1[...]
 
     @pl.when(s_ref[LOW] == 1)
     def _():
-        xs[...] = xb[...]
+        xs[:t] = b0[...]
+        xs[t:] = b1[...]
 
 
 def put_far(s_ref, product, st, plane, outs, cells, half, total):
@@ -164,11 +177,11 @@
     )
 
 
-def far_body(s_ref, xa, xb, y0, y1, st, first_tiles, *refs, total):
+def far_body(s_ref, a0, a1, b0, b1, y0, y1, st, *refs, total):
     xs, outs = refs[-1], refs[:-1]
-    half = xa.shape[0]
+    half = 2 * a0.shape[0]
     n = y0.shape[0] // 2
-    pick_far(s_ref, xa, xb, xs)
+    pick_far(s_ref, a0, a1, b0, b1, xs)
     cells = pl.ds(pl.multiple_of(s_ref[LOW] * n, n), n)
 
     def product(first, w):
@@ -178,11 +191,11 @@
     put_far(s_ref, product, st, 0, outs, 2.0 * n, half, total)
 
 
-def ends_body(s_ref, xa, xb, na, nb, st, *refs, total):
+def ends_body(s_ref, a0, a1, b0, b1, na, nb, st, *refs, total):
     xs, ys, outs = refs[-2], refs[-1], refs[:-2]
-    half = xa.shape[0]
+    half = 2 * a0.shape[0]
     n = na.shape[0] // 2
-    pick_far(s_ref, xa, xb, xs)
+    pick_far(s_ref, a0, a1, b0, b1, xs)
 
     @pl.when(s_ref[CORE] == 0)
     def _():
@@ -300,10 +313,12 @@
 
 
 def pay_body(s_ref, a, *refs):
-    out_a, out_b, out_n = refs[-3:]
-    n = a.shape[0] // 2
-    out_a[...] = a[:n].T
-    out_b[...] = a[n:].T
+    a0, a1, b0, b1, out_n = refs[-5:]
+    n, t = a.shape[0] // 2, a.shape[1] // 2
+    a0[...] = a[:n, :t].T
+    a1[...] = a[:n, t:].T
+    b0[...] = a[n:, :t].T
+    b1[...] = a[n:, t:].T
     first = pl.multiple_of(jnp.where(s_ref[PLANE] == 0, n, 0), n)
     out_n[...] = a[pl.ds(first, n)]
 
@@ -376,7 +391,7 @@
     own = normalize(counts, library)
     oth = send(own, flip)
     pay_in = pl.BlockSpec((rows, half), lambda i, sc: (0, sc[CORE]))
-    pay_shapes = [shape((half, rows), bf16)] * 2 + [shape((rows, half), bf16)]
+    pay_shapes = [shape((tile, rows), bf16)] * 4 + [shape((rows, half), bf16)]
 
     def turn_payload(block, part, before):
         return pl.pallas_call(
@@ -385,7 +400,7 @@
                 num_scalar_prefetch=1,
                 grid=(1,),
                 in_specs=[pay_in] + [pl.BlockSpec(memory_space=pl.ANY)] * len(before),
-                out_specs=[pl.BlockSpec((half, half_cells), lambda i, sc: (0, part))] * 2
+                out_specs=[pl.BlockSpec((tile, half_cells), lambda i, sc: (0, part))] * 4
                 + [pl.BlockSpec((half_cells, half), lambda i, sc: (part, 0))],
             ),
             out_shape=pay_shapes,
@@ -394,9 +409,9 @@
             name="turn_payload",
         )(info, block, *before)
 
-    pay_a, pay_b, end = turn_payload(oth, 1, turn_payload(own, 0, []))
-    up1 = send(pay_a, lambda k, h, g: (k, h, g + 1))
-    dn1 = send(pay_b, lambda k, h, g: (k, h, g - 1))
+    *pay, end = turn_payload(oth, 1, turn_payload(own, 0, []))
+    up1 = [send(pay[i], lambda k, h, g: (k, h, g + 1)) for i in (0, 1)]
+    dn1 = [send(pay[2 + i], lambda k, h, g: (k, h, g - 1)) for i in (0, 1)]
     widened = own.astype(f32)
     halves = jnp.sum(widened.reshape(2, half_cells, width), axis=1)
     squares = jnp.sum(widened * widened, axis=0)
@@ -438,13 +453,13 @@
             name="partial_blocks",
         )(info, *operands)
 
-    up2 = send(up1, lambda k, h, g: (k, h, g + 1) if g > 0 else None)
-    dn2 = send(dn1, lambda k, h, g: (k, h, g - 1) if g < last else None)
+    up2 = [send(up1[i], lambda k, h, g: (k, h, g + 1) if g > 0 else None) for i in (0, 1)]
+    dn2 = [send(dn1[i], lambda k, h, g: (k, h, g - 1) if g < last else None) for i in (0, 1)]
     near_other = send(near, flip)
     kept = (half, rows)
-    w0 = blocks(diagonal_body, 1, [], pay_a, pay_b, own, oth, own_stats)
-    w1 = blocks(near_body, 2, [], up1, dn1, own, oth, stats)
-    w3 = blocks(ends_body, 1, [kept, (rows, width)], up2, dn2, near, near_other, stats)
+    w0 = blocks(diagonal_body, 1, [], *pay, own, oth, own_stats)
+    w1 = blocks(near_body, 2, [], *up1, *dn1, own, oth, stats)
+    w3 = blocks(ends_body, 1, [kept, (rows, width)], *up2, *dn2, near, near_other, stats)
 
     def reduce_tiles(w):
         return [w[0]] + [send(w[j], lambda k, h, g, j=j: (k ^ j, h, g)) for j in (1, 2, 3)]
@@ -464,7 +479,7 @@
         )(info, *parts)
 
     (t0,) = turn(reduce_tiles(w0), [None], [None])
-    w2 = blocks(far_body, 1, [kept], up2, dn2, own, oth, stats, t0, behind=1)
+    w2 = blocks(far_body, 1, [kept], *up2, *dn2, own, oth, stats)
     t1, e_up, e_dn = turn(reduce_tiles(w1), [0, 1], [None, None])
     t2, e_two = turn(reduce_tiles(w2), [0], [None])
     _, e_three, k_three = turn(reduce_tiles(w3), [0], [1])

time: 193 us -> 207 us (1.073); the launches traced: 190 us -> 207 us
  starting transfers between devices: 69.7 us -> 91.5 us
  waiting for transfers between devices: 84.5 us -> 79.3 us
    ppermute x37 -> x41, starting transfers between devices: 69.7 us -> 91.5 us  [send(): return lax.ppermute(x, AXES, perm(f))]
    ppermute x37 -> x41, waiting for transfers between devices: 84.5 us -> 79.3 us  [send(): return lax.ppermute(x, AXES, perm(f))]
  transfers between devices with their start and end apart: 37 -> 41, of which waited for: 20 -> 14; matrix products, arithmetic and copies ran while one was open for 1% -> 1% of each run, Pallas kernels for 12% -> 11%
where the time goes in v6:
time: 207 us
  starting transfers between devices  91.5 us (44%)
  waiting for transfers between devices  79.3 us (38%)
  Pallas kernels  28.8 us (14%)
  other arithmetic  5.84 us (3%)
    ppermute x41, starting transfers between devices, send(): return lax.ppermute(x, AXES, perm(f))  91.5 us
    ppermute x41, waiting for transfers between devices, send(): return lax.ppermute(x, AXES, perm(f))  79.3 us
    pallas_call x4, Pallas kernels, blocks(): pl.pallas_call(functools.partial(body, total=total), in_specs=[scalars()]...  12.8 us
    pallas_call x4, Pallas kernels, turn(): pl.pallas_call(functools.partial(turn_body, turns=turns, keeps=keeps), in...  5.84 us
  transfers between devices with their start and end apart: 41, of which 14 were waited for; matrix products, arithmetic and copies ran while one was open for 1% of the time, Pallas kernels for 11%

profile of v6, /device:TPU:0, one launch (start us, length us, event | category | flops | bytes accessed | tf_op | source)
XLA Modules:
  0.0 206.6 jit_solution(9701118453045142344)
XLA Ops:
  1.3 4.0 %bitcast_reduce_fusion = (f32[2,1024]{1,0:T(2,128)S(1)}, bf16[1024,1024]{1,0:T(8,128)(2,1)S(1)}) fusion(f32[1024]{0:T(1024)S(1)} %convert_divide_fusion, s32[1024,1024]{1,0:T(8,128)} %param.2), kind=kLoop, calls=%fused_computation | loop fusion | flops 5240832 | bytes 6303744 | tf_op jit(solution)/shard_map/reduce_sum | solution.py:416
  6.9 2.8 %collective-permute-done.a = bf16[1024,1024]{1,0:T(8,128)(2,1)} collective-permute-done((bf16[1024,1024]{1,0:T(8,128)(2,1)S(1)}, bf16[1024,1024]{1,0:T(8,128)(2,1)}, u32[]{:S(2)}, u32[]{:S(2)}) %collective-permute-start) | collective-permute-done | bytes 2097184 | tf_op jit(solution)/shard_map/ppermute | solution.py:370
  11.9 4.9 %collective-permute-start.19 = (bf16[1024,512]{1,0:T(8,128)(2,1)S(1)}, bf16[1024,512]{1,0:T(8,128)(2,1)S(1)}, u32[]{:S(2)}, u32[]{:S(2)}) collective-permute-start(bf16[1024,512]{1,0:T(8,128)(2,1)S(1)} %get-tuple-element.64), channel_id=1, source_target_pairs={{0,1},{3,2},{4,5},{7,6},{8,9},{11,10},{12,13},{15,14},{16,17},{19,... | collective-permute-start | bytes 3145736 | tf_op jit(solution)/shard_map/ppermute | solution.py:370
  24.4 3.4 %collective-permute-start.3 = (bf16[256,1024]{1,0:T(8,128)(2,1)S(1)}, bf16[256,1024]{1,0:T(8,128)(2,1)S(1)}, u32[]{:S(2)}, u32[]{:S(2)}) collective-permute-start(bf16[256,1024]{1,0:T(8,128)(2,1)S(1)} %get-tuple-element.53.a1), channel_id=1, source_target_pairs={{0,1},{1,2},{2,3},{4,5},{5,6},{6,7},{8,9},{9,10},{10,11},{12,13},{... | collective-permute-start | bytes 1572872 | tf_op jit(solution)/shard_map/ppermute | solution.py:370
  29.2 3.3 %collective-permute-start.12 = (f32[8,1024]{1,0:T(8,128)S(1)}, f32[8,1024]{1,0:T(8,128)S(1)}, u32[]{:S(2)}, u32[]{:S(2)}) collective-permute-start(f32[8,1024]{1,0:T(8,128)S(1)} %get-tuple-element.97), channel_id=1, source_target_pairs={{0,1},{1,0},{2,3},{3,2},{4,5},{5,4},{6,7},{7,6},{8,9},{9,8},{10,11... | collective-permute-start | bytes 98312 | tf_op jit(solution)/shard_map/ppermute | solution.py:370
  32.6 30.4 %collective-permute-done.12 = f32[8,1024]{1,0:T(8,128)S(1)} collective-permute-done((f32[8,1024]{1,0:T(8,128)S(1)}, f32[8,1024]{1,0:T(8,128)S(1)}, u32[]{:S(2)}, u32[]{:S(2)}) %collective-permute-start.12) | collective-permute-done | bytes 32800 | tf_op jit(solution)/shard_map/ppermute | solution.py:370
  62.9 5.1 %collective-permute-done.13 = f32[8,1024]{1,0:T(8,128)S(1)} collective-permute-done((f32[8,1024]{1,0:T(8,128)S(1)}, f32[8,1024]{1,0:T(8,128)S(1)}, u32[]{:S(2)}, u32[]{:S(2)}) %collective-permute-start.13) | collective-permute-done | bytes 32800 | tf_op jit(solution)/shard_map/ppermute | solution.py:370
  69.7 4.2 %collective-permute-done.14 = f32[8,1024]{1,0:T(8,128)S(1)} collective-permute-done((f32[8,1024]{1,0:T(8,128)S(1)}, f32[8,1024]{1,0:T(8,128)S(1)}, u32[]{:S(2)}, u32[]{:S(2)}) %collective-permute-start.14) | collective-permute-done | bytes 32800 | tf_op jit(solution)/shard_map/ppermute | solution.py:370
  77.9 8.4 %collective-permute-done.7.b1 = bf16[256,1024]{1,0:T(8,128)(2,1)S(1)} collective-permute-done((bf16[256,1024]{1,0:T(8,128)(2,1)S(1)}, bf16[256,1024]{1,0:T(8,128)(2,1)S(1)}, u32[]{:S(2)}, u32[]{:S(2)}) %collective-permute-start.7) | collective-permute-done | bytes 524320 | tf_op jit(solution)/shard_map/ppermute | solution.py:370
  87.6 4.1 %partial_blocks.7 = (f32[2,2,256,256]{3,2,1,0:T(8,128)S(1)}, bf16[2,2,256,256]{3,2,1,0:T(8,128)(2,1)S(1)}, bf16[2,2,256,256]{3,2,1,0:T(8,128)(2,1)S(1)}, bf16[2,2,256,256]{3,2,1,0:T(8,128)(2,1)S(1)}) custom-call(s32[9]{0:T(128)S(1)} %stack.58.s_ref, bf16[256,1024]{1,0:T(8,128)(2,1)S(1)} %collective-permute-done.1.a0, ...), custom_call_target="tpu_custom_call" | custom-call | tf_op jit(solution)/shard_map/partial_blocks/pallas_call | solution.py:443
  94.8 2.7 %collective-permute-done.6.b0 = bf16[256,1024]{1,0:T(8,128)(2,1)S(1)} collective-permute-done((bf16[256,1024]{1,0:T(8,128)(2,1)S(1)}, bf16[256,1024]{1,0:T(8,128)(2,1)S(1)}, u32[]{:S(2)}, u32[]{:S(2)}) %collective-permute-start.6) | collective-permute-done | bytes 524320 | tf_op jit(solution)/shard_map/ppermute | solution.py:370
  97.6 2.4 %collective-permute-start.31 = (bf16[2,2,256,256]{3,2,1,0:T(8,128)(2,1)S(1)}, bf16[2,2,256,256]{3,2,1,0:T(8,128)(2,1)S(1)}, u32[]{:S(2)}, u32[]{:S(2)}) collective-permute-start(bf16[2,2,256,256]{3,2,1,0:T(8,128)(2,1)S(1)} %get-tuple-element.78), channel_id=1, source_target_pairs={{0,24},{1,25},{2,26},{3,27},{4,28},{5,29},{6,30},{7,31},{8,16},{9,... | collective-permute-start | bytes 1572872 | tf_op jit(solution)/shard_map/ppermute | solution.py:370
  100.0 8.3 %collective-permute-done.8.b1 = bf16[256,1024]{1,0:T(8,128)(2,1)S(1)} collective-permute-done((bf16[256,1024]{1,0:T(8,128)(2,1)S(1)}, bf16[256,1024]{1,0:T(8,128)(2,1)S(1)}, u32[]{:S(2)}, u32[]{:S(2)}) %collective-permute-start.8) | collective-permute-done | bytes 524320 | tf_op jit(solution)/shard_map/ppermute | solution.py:370
  113.8 2.8 %partial_blocks.5 = (f32[1,2,256,256]{3,2,1,0:T(8,128)S(1)}, bf16[1,2,256,256]{3,2,1,0:T(8,128)(2,1)S(1)}, bf16[1,2,256,256]{3,2,1,0:T(8,128)(2,1)S(1)}, bf16[1,2,256,256]{3,2,1,0:T(8,128)(2,1)S(1)}) custom-call(s32[9]{0:T(128)S(1)} %stack.58.s_ref, bf16[256,1024]{1,0:T(8,128)(2,1)S(1)} %collective-permute-done.2.a0, ...), custom_call_target="tpu_custom_call" | custom-call | tf_op jit(solution)/shard_map/partial_blocks/pallas_call | solution.py:443
  122.4 3.5 %partial_blocks.6 = (f32[1,2,256,256]{3,2,1,0:T(8,128)S(1)}, bf16[1,2,256,256]{3,2,1,0:T(8,128)(2,1)S(1)}, bf16[1,2,256,256]{3,2,1,0:T(8,128)(2,1)S(1)}, bf16[1,2,256,256]{3,2,1,0:T(8,128)(2,1)S(1)}) custom-call(s32[9]{0:T(128)S(1)} %stack.58.s_ref, bf16[256,1024]{1,0:T(8,128)(2,1)S(1)} %get-tuple-element.52.a0, bf16[256,1024]{1,0:T(8,128)(2,1)S(1)} %get-tuple-element.53.a1, ...), custom_call_target="tpu_custom_call" | custom-call | tf_op jit(solution)/shard_map/partial_blocks/pallas_call | solution.py:443
  128.3 3.1 %collective-permute-done.21.r1 = bf16[1,2,256,256]{3,2,1,0:T(8,128)(2,1)S(1)} collective-permute-done((bf16[1,2,256,256]{3,2,1,0:T(8,128)(2,1)S(1)}, bf16[1,2,256,256]{3,2,1,0:T(8,128)(2,1)S(1)}, u32[]{:S(2)}, u32[]{:S(2)}) %collective-permute-start.21) | collective-permute-done | bytes 262176 | tf_op jit(solution)/shard_map/ppermute | solution.py:370
  136.9 19.1 %collective-permute-start.32 = (bf16[2,256,256]{2,1,0:T(8,128)(2,1)S(1)}, bf16[2,256,256]{2,1,0:T(8,128)(2,1)S(1)}, u32[]{:S(2)}, u32[]{:S(2)}) collective-permute-start(bf16[2,256,256]{2,1,0:T(8,128)(2,1)S(1)} %get-tuple-element.80), channel_id=1, source_target_pairs={{0,1},{1,2},{2,3},{4,5},{5,6},{6,7},{8,9},{9,10},{10,11},{12,13},{... | collective-permute-start | bytes 786440 | tf_op jit(solution)/shard_map/ppermute | solution.py:370
  159.4 4.5 %collective-permute-start.18 = (bf16[2,256,256]{2,1,0:T(8,128)(2,1)S(1)}, bf16[2,256,256]{2,1,0:T(8,128)(2,1)S(1)}, u32[]{:S(2)}, u32[]{:S(2)}) collective-permute-start(bf16[2,256,256]{2,1,0:T(8,128)(2,1)S(1)} %get-tuple-element.63), channel_id=1, source_target_pairs={{0,2},{1,3},{2,0},{3,1},{4,6},{5,7},{6,4},{7,5},{8,10},{9,11},{10,... | collective-permute-start | bytes 786440 | tf_op jit(solution)/shard_map/ppermute | solution.py:370
  168.9 6.8 %collective-permute-done.18.r2 = bf16[2,256,256]{2,1,0:T(8,128)(2,1)S(1)} collective-permute-done((bf16[2,256,256]{2,1,0:T(8,128)(2,1)S(1)}, bf16[2,256,256]{2,1,0:T(8,128)(2,1)S(1)}, u32[]{:S(2)}, u32[]{:S(2)}) %collective-permute-start.18) | collective-permute-done | bytes 262176 | tf_op jit(solution)/shard_map/ppermute | solution.py:370
  175.8 2.8 %collective-permute-done.24.rf = bf16[2,256,256]{2,1,0:T(8,128)(2,1)S(1)} collective-permute-done((bf16[2,256,256]{2,1,0:T(8,128)(2,1)S(1)}, bf16[2,256,256]{2,1,0:T(8,128)(2,1)S(1)}, u32[]{:S(2)}, u32[]{:S(2)}) %collective-permute-start.24) | collective-permute-done | bytes 262176 | tf_op jit(solution)/shard_map/ppermute | solution.py:370
  183.8 4.9 %collective-permute-start.35 = (bf16[2,256,256]{2,1,0:T(8,128)(2,1)S(1)}, bf16[2,256,256]{2,1,0:T(8,128)(2,1)S(1)}, u32[]{:S(2)}, u32[]{:S(2)}) collective-permute-start(bf16[2,256,256]{2,1,0:T(8,128)(2,1)S(1)} %get-tuple-element.89), channel_id=1, source_target_pairs={{0,16},{1,17},{2,18},{3,19},{4,20},{5,21},{6,22},{7,23},{8,24},{9,... | collective-permute-start | bytes 786440 | tf_op jit(solution)/shard_map/ppermute | solution.py:370
  189.4 4.2 %collective-permute-start.38 = (f32[1,512]{1,0:T(1,128)S(1)}, f32[1,512]{1,0:T(1,128)S(1)}, u32[]{:S(2)}, u32[]{:S(2)}) collective-permute-start(f32[1,512]{1,0:T(1,128)S(1)} %get-tuple-element.91), channel_id=1, source_target_pairs={{0,1},{1,9},{2,17},{3,25},{4,5},{5,13},{6,21},{7,29},{8,0},{9,8},{... | collective-permute-start | bytes 6152 | tf_op jit(solution)/shard_map/ppermute | solution.py:370
  193.6 3.2 %collective-permute-start.39 = (f32[1,512]{1,0:T(1,128)S(1)}, f32[1,512]{1,0:T(1,128)S(1)}, u32[]{:S(2)}, u32[]{:S(2)}) collective-permute-start(f32[1,512]{1,0:T(1,128)S(1)} %get-tuple-element.91), channel_id=1, source_target_pairs={{0,2},{1,10},{2,18},{3,26},{4,6},{5,14},{6,22},{7,30},{8,3},{9,11}... | collective-permute-start | bytes 6152 | tf_op jit(solution)/shard_map/ppermute | solution.py:370
  196.8 5.8 %collective-permute-start.40 = (f32[1,512]{1,0:T(1,128)S(1)}, f32[1,512]{1,0:T(1,128)S(1)}, u32[]{:S(2)}, u32[]{:S(2)}) collective-permute-start(f32[1,512]{1,0:T(1,128)S(1)} %get-tuple-element.91), channel_id=1, source_target_pairs={{0,3},{1,11},{2,19},{3,27},{4,7},{5,15},{6,23},{7,31},{8,2},{9,10}... | collective-permute-start | bytes 6152 | tf_op jit(solution)/shard_map/ppermute | solution.py:370
  (85 shorter events, 60.7 us)
Async XLA Ops:
  11.9 63.2 %collective-permute-start.19 = (bf16[1024,512]{1,0:T(8,128)(2,1)S(1)}, bf16[1024,512]{1,0:T(8,128)(2,1)S(1)}, u32[]{:S(2)}, u32[]{:S(2)}) collective-permute-start(bf16[1024,512]{1,0:T(8,128)(2,1)S(1)} %get-tuple-element.64), channel_id=1, source_target_pairs={{0,1},{3,2},{4,5},{7,6},{8,9},{11,10},{12,13},{15,14},{16,17},{19,... | collective-permute-start | bytes 3145736 | tf_op jit(solution)/shard_map/ppermute | solution.py:370
  23.0 52.2 %collective-permute-start.1 = (bf16[256,1024]{1,0:T(8,128)(2,1)S(1)}, bf16[256,1024]{1,0:T(8,128)(2,1)S(1)}, u32[]{:S(2)}, u32[]{:S(2)}) collective-permute-start(bf16[256,1024]{1,0:T(8,128)(2,1)S(1)} %get-tuple-element.52.a0), channel_id=1, source_target_pairs={{0,1},{1,2},{2,3},{4,5},{5,6},{6,7},{8,9},{9,10},{10,11},{12,13},{... | collective-permute-start | bytes 1572872 | tf_op jit(solution)/shard_map/ppermute | solution.py:370
  24.4 51.5 %collective-permute-start.3 = (bf16[256,1024]{1,0:T(8,128)(2,1)S(1)}, bf16[256,1024]{1,0:T(8,128)(2,1)S(1)}, u32[]{:S(2)}, u32[]{:S(2)}) collective-permute-start(bf16[256,1024]{1,0:T(8,128)(2,1)S(1)} %get-tuple-element.53.a1), channel_id=1, source_target_pairs={{0,1},{1,2},{2,3},{4,5},{5,6},{6,7},{8,9},{9,10},{10,11},{12,13},{... | collective-permute-start | bytes 1572872 | tf_op jit(solution)/shard_map/ppermute | solution.py:370
  27.8 48.8 %collective-permute-start.5 = (bf16[256,1024]{1,0:T(8,128)(2,1)S(1)}, bf16[256,1024]{1,0:T(8,128)(2,1)S(1)}, u32[]{:S(2)}, u32[]{:S(2)}) collective-permute-start(bf16[256,1024]{1,0:T(8,128)(2,1)S(1)} %get-tuple-element.54.b0), channel_id=1, source_target_pairs={{1,0},{2,1},{3,2},{5,4},{6,5},{7,6},{9,8},{10,9},{11,10},{13,12},{... | collective-permute-start | bytes 1572872 | tf_op jit(solution)/shard_map/ppermute | solution.py:370
  29.2 33.7 %collective-permute-start.12 = (f32[8,1024]{1,0:T(8,128)S(1)}, f32[8,1024]{1,0:T(8,128)S(1)}, u32[]{:S(2)}, u32[]{:S(2)}) collective-permute-start(f32[8,1024]{1,0:T(8,128)S(1)} %get-tuple-element.97), channel_id=1, source_target_pairs={{0,1},{1,0},{2,3},{3,2},{4,5},{5,4},{6,7},{7,6},{8,9},{9,8},{10,11... | collective-permute-start | bytes 98312 | tf_op jit(solution)/shard_map/ppermute | solution.py:370
  75.1 37.2 %collective-permute-start.20 = (bf16[1024,512]{1,0:T(8,128)(2,1)S(1)}, bf16[1024,512]{1,0:T(8,128)(2,1)S(1)}, u32[]{:S(2)}, u32[]{:S(2)}) collective-permute-start(bf16[1024,512]{1,0:T(8,128)(2,1)S(1)} %collective-permute-done.19.na), channel_id=1, source_target_pairs={{0,4},{1,5},{2,6},{3,7},{4,0},{5,1},{6,2},{7,3},{8,12},{9,13},{10,... | collective-permute-start | bytes 3145736 | tf_op jit(solution)/shard_map/ppermute | solution.py:370
  75.2 16.6 %collective-permute-start.2 = (bf16[256,1024]{1,0:T(8,128)(2,1)S(1)}, bf16[256,1024]{1,0:T(8,128)(2,1)S(1)}, u32[]{:S(2)}, u32[]{:S(2)}) collective-permute-start(bf16[256,1024]{1,0:T(8,128)(2,1)S(1)} %collective-permute-done.1.a0), channel_id=1, source_target_pairs={{1,2},{2,3},{5,6},{6,7},{9,10},{10,11},{13,14},{14,15},{17,18},{18... | collective-permute-start | bytes 1572872 | tf_op jit(solution)/shard_map/ppermute | solution.py:370
  75.9 17.4 %collective-permute-start.4 = (bf16[256,1024]{1,0:T(8,128)(2,1)S(1)}, bf16[256,1024]{1,0:T(8,128)(2,1)S(1)}, u32[]{:S(2)}, u32[]{:S(2)}) collective-permute-start(bf16[256,1024]{1,0:T(8,128)(2,1)S(1)} %collective-permute-done.3.a1), channel_id=1, source_target_pairs={{1,2},{2,3},{5,6},{6,7},{9,10},{10,11},{13,14},{14,15},{17,18},{18... | collective-permute-start | bytes 1572872 | tf_op jit(solution)/shard_map/ppermute | solution.py:370
  76.6 20.9 %collective-permute-start.6 = (bf16[256,1024]{1,0:T(8,128)(2,1)S(1)}, bf16[256,1024]{1,0:T(8,128)(2,1)S(1)}, u32[]{:S(2)}, u32[]{:S(2)}) collective-permute-start(bf16[256,1024]{1,0:T(8,128)(2,1)S(1)} %collective-permute-done.5.b0), channel_id=1, source_target_pairs={{1,0},{2,1},{5,4},{6,5},{9,8},{10,9},{13,12},{14,13},{17,16},{18,1... | collective-permute-start | bytes 1572872 | tf_op jit(solution)/shard_map/ppermute | solution.py:370
  86.3 22.0 %collective-permute-start.8 = (bf16[256,1024]{1,0:T(8,128)(2,1)S(1)}, bf16[256,1024]{1,0:T(8,128)(2,1)S(1)}, u32[]{:S(2)}, u32[]{:S(2)}) collective-permute-start(bf16[256,1024]{1,0:T(8,128)(2,1)S(1)} %collective-permute-done.7.b1), channel_id=1, source_target_pairs={{1,0},{2,1},{5,4},{6,5},{9,8},{10,9},{13,12},{14,13},{17,16},{18,1... | collective-permute-start | bytes 1572872 | tf_op jit(solution)/shard_map/ppermute | solution.py:370
  91.8 24.8 %collective-permute-start.29 = (bf16[2,2,256,256]{3,2,1,0:T(8,128)(2,1)S(1)}, bf16[2,2,256,256]{3,2,1,0:T(8,128)(2,1)S(1)}, u32[]{:S(2)}, u32[]{:S(2)}) collective-permute-start(bf16[2,2,256,256]{3,2,1,0:T(8,128)(2,1)S(1)} %get-tuple-element.76), channel_id=1, source_target_pairs={{0,8},{1,9},{2,10},{3,11},{4,12},{5,13},{6,14},{7,15},{8,0},{9,1},... | collective-permute-start | bytes 1572872 | tf_op jit(solution)/shard_map/ppermute | solution.py:370
  93.3 23.8 %collective-permute-start.30 = (bf16[2,2,256,256]{3,2,1,0:T(8,128)(2,1)S(1)}, bf16[2,2,256,256]{3,2,1,0:T(8,128)(2,1)S(1)}, u32[]{:S(2)}, u32[]{:S(2)}) collective-permute-start(bf16[2,2,256,256]{3,2,1,0:T(8,128)(2,1)S(1)} %get-tuple-element.77), channel_id=1, source_target_pairs={{0,16},{1,17},{2,18},{3,19},{4,20},{5,21},{6,22},{7,23},{8,24},{9,... | collective-permute-start | bytes 1572872 | tf_op jit(solution)/shard_map/ppermute | solution.py:370
  97.6 21.1 %collective-permute-start.31 = (bf16[2,2,256,256]{3,2,1,0:T(8,128)(2,1)S(1)}, bf16[2,2,256,256]{3,2,1,0:T(8,128)(2,1)S(1)}, u32[]{:S(2)}, u32[]{:S(2)}) collective-permute-start(bf16[2,2,256,256]{3,2,1,0:T(8,128)(2,1)S(1)} %get-tuple-element.78), channel_id=1, source_target_pairs={{0,24},{1,25},{2,26},{3,27},{4,28},{5,29},{6,30},{7,31},{8,16},{9,... | collective-permute-start | bytes 1572872 | tf_op jit(solution)/shard_map/ppermute | solution.py:370
  118.6 18.3 %collective-permute-start.22 = (bf16[1,2,256,256]{3,2,1,0:T(8,128)(2,1)S(1)}, bf16[1,2,256,256]{3,2,1,0:T(8,128)(2,1)S(1)}, u32[]{:S(2)}, u32[]{:S(2)}) collective-permute-start(bf16[1,2,256,256]{3,2,1,0:T(8,128)(2,1)S(1)} %get-tuple-element.67), channel_id=1, source_target_pairs={{0,16},{1,17},{2,18},{3,19},{4,20},{5,21},{6,22},{7,23},{8,24},{9,... | collective-permute-start | bytes 786440 | tf_op jit(solution)/shard_map/ppermute | solution.py:370
  120.2 35.9 %collective-permute-start.23 = (bf16[1,2,256,256]{3,2,1,0:T(8,128)(2,1)S(1)}, bf16[1,2,256,256]{3,2,1,0:T(8,128)(2,1)S(1)}, u32[]{:S(2)}, u32[]{:S(2)}) collective-permute-start(bf16[1,2,256,256]{3,2,1,0:T(8,128)(2,1)S(1)} %get-tuple-element.68), channel_id=1, source_target_pairs={{0,24},{1,25},{2,26},{3,27},{4,28},{5,29},{6,30},{7,31},{8,16},{9,... | collective-permute-start | bytes 786440 | tf_op jit(solution)/shard_map/ppermute | solution.py:370
  126.0 33.4 %collective-permute-start.26 = (bf16[1,2,256,256]{3,2,1,0:T(8,128)(2,1)S(1)}, bf16[1,2,256,256]{3,2,1,0:T(8,128)(2,1)S(1)}, u32[]{:S(2)}, u32[]{:S(2)}) collective-permute-start(bf16[1,2,256,256]{3,2,1,0:T(8,128)(2,1)S(1)} %get-tuple-element.72), channel_id=1, source_target_pairs={{0,8},{1,9},{2,10},{3,11},{4,12},{5,13},{6,14},{7,15},{8,0},{9,1},... | collective-permute-start | bytes 786440 | tf_op jit(solution)/shard_map/ppermute | solution.py:370
  126.8 37.2 %collective-permute-start.27 = (bf16[1,2,256,256]{3,2,1,0:T(8,128)(2,1)S(1)}, bf16[1,2,256,256]{3,2,1,0:T(8,128)(2,1)S(1)}, u32[]{:S(2)}, u32[]{:S(2)}) collective-permute-start(bf16[1,2,256,256]{3,2,1,0:T(8,128)(2,1)S(1)} %get-tuple-element.73), channel_id=1, source_target_pairs={{0,16},{1,17},{2,18},{3,19},{4,20},{5,21},{6,22},{7,23},{8,24},{9,... | collective-permute-start | bytes 786440 | tf_op jit(solution)/shard_map/ppermute | solution.py:370
  131.4 33.8 %collective-permute-start.28 = (bf16[1,2,256,256]{3,2,1,0:T(8,128)(2,1)S(1)}, bf16[1,2,256,256]{3,2,1,0:T(8,128)(2,1)S(1)}, u32[]{:S(2)}, u32[]{:S(2)}) collective-permute-start(bf16[1,2,256,256]{3,2,1,0:T(8,128)(2,1)S(1)} %get-tuple-element.74), channel_id=1, source_target_pairs={{0,24},{1,25},{2,26},{3,27},{4,28},{5,29},{6,30},{7,31},{8,16},{9,... | collective-permute-start | bytes 786440 | tf_op jit(solution)/shard_map/ppermute | solution.py:370
  136.9 30.6 %collective-permute-start.32 = (bf16[2,256,256]{2,1,0:T(8,128)(2,1)S(1)}, bf16[2,256,256]{2,1,0:T(8,128)(2,1)S(1)}, u32[]{:S(2)}, u32[]{:S(2)}) collective-permute-start(bf16[2,256,256]{2,1,0:T(8,128)(2,1)S(1)} %get-tuple-element.80), channel_id=1, source_target_pairs={{0,1},{1,2},{2,3},{4,5},{5,6},{6,7},{8,9},{9,10},{10,11},{12,13},{... | collective-permute-start | bytes 786440 | tf_op jit(solution)/shard_map/ppermute | solution.py:370
  159.4 16.4 %collective-permute-start.18 = (bf16[2,256,256]{2,1,0:T(8,128)(2,1)S(1)}, bf16[2,256,256]{2,1,0:T(8,128)(2,1)S(1)}, u32[]{:S(2)}, u32[]{:S(2)}) collective-permute-start(bf16[2,256,256]{2,1,0:T(8,128)(2,1)S(1)} %get-tuple-element.63), channel_id=1, source_target_pairs={{0,2},{1,3},{2,0},{3,1},{4,6},{5,7},{6,4},{7,5},{8,10},{9,11},{10,... | collective-permute-start | bytes 786440 | tf_op jit(solution)/shard_map/ppermute | solution.py:370
  165.2 15.6 %collective-permute-start.25 = (bf16[2,256,256]{2,1,0:T(8,128)(2,1)S(1)}, bf16[2,256,256]{2,1,0:T(8,128)(2,1)S(1)}, u32[]{:S(2)}, u32[]{:S(2)}) collective-permute-start(bf16[2,256,256]{2,1,0:T(8,128)(2,1)S(1)} %get-tuple-element.70), channel_id=1, source_target_pairs={{1,0},{2,3},{5,4},{6,7},{9,8},{10,11},{13,12},{14,15},{17,16},{18,... | collective-permute-start | bytes 786440 | tf_op jit(solution)/shard_map/ppermute | solution.py:370
  182.2 22.2 %collective-permute-start.34 = (bf16[2,256,256]{2,1,0:T(8,128)(2,1)S(1)}, bf16[2,256,256]{2,1,0:T(8,128)(2,1)S(1)}, u32[]{:S(2)}, u32[]{:S(2)}) collective-permute-start(bf16[2,256,256]{2,1,0:T(8,128)(2,1)S(1)} %get-tuple-element.88), channel_id=1, source_target_pairs={{0,8},{1,9},{2,10},{3,11},{4,12},{5,13},{6,14},{7,15},{8,0},{9,1},... | collective-permute-start | bytes 786440 | tf_op jit(solution)/shard_map/ppermute | solution.py:370
  183.8 20.7 %collective-permute-start.35 = (bf16[2,256,256]{2,1,0:T(8,128)(2,1)S(1)}, bf16[2,256,256]{2,1,0:T(8,128)(2,1)S(1)}, u32[]{:S(2)}, u32[]{:S(2)}) collective-permute-start(bf16[2,256,256]{2,1,0:T(8,128)(2,1)S(1)} %get-tuple-element.89), channel_id=1, source_target_pairs={{0,16},{1,17},{2,18},{3,19},{4,20},{5,21},{6,22},{7,23},{8,24},{9,... | collective-permute-start | bytes 786440 | tf_op jit(solution)/shard_map/ppermute | solution.py:370
  188.7 15.8 %collective-permute-start.36 = (bf16[2,256,256]{2,1,0:T(8,128)(2,1)S(1)}, bf16[2,256,256]{2,1,0:T(8,128)(2,1)S(1)}, u32[]{:S(2)}, u32[]{:S(2)}) collective-permute-start(bf16[2,256,256]{2,1,0:T(8,128)(2,1)S(1)} %get-tuple-element.90), channel_id=1, source_target_pairs={{0,24},{1,25},{2,26},{3,27},{4,28},{5,29},{6,30},{7,31},{8,16},{9,... | collective-permute-start | bytes 786440 | tf_op jit(solution)/shard_map/ppermute | solution.py:370
  (17 other events, 148.3 us)

commit v7 on v6

--- a/solution.py
+++ b/solution.py
@@ -137,23 +137,22 @@
     )
 
 
-def near_body(s_ref, a0, a1, b0, b1, y0, y1, st, *outs, total):
-    half = 2 * a0.shape[0]
+def near_body(s_ref, x0, x1, y0, y1, st, *outs, total, side):
+    half = 2 * x0.shape[0]
     n = y0.shape[0] // 2
-    for blk, xs in enumerate(((a0, a1), (b0, b1))):
-        cells = slice(blk * n, blk * n + n)
-
-        def product(first, w):
-            lanes = pl.ds(first, w)
-            return stacked(
-                [plain(x[:, :n], y0[cells, lanes]) + plain(x[:, n:], y1[cells, lanes]) for x in xs]
-            )
-
-        put_tiles(
-            product, lambda v: v[2 + blk : 3 + blk], s_ref, blk,
-            row_stats(s_ref, st, s_ref[LOWER + blk], half), column_stats(st, 0),
-            2.0 * n, total, outs,
+    cells = slice(side * n, side * n + n)
+
+    def product(first, w):
+        lanes = pl.ds(first, w)
+        return stacked(
+            [plain(x[:, :n], y0[cells, lanes]) + plain(x[:, n:], y1[cells, lanes]) for x in (x0, x1)]
         )
+
+    put_tiles(
+        product, lambda v: v[2 + side : 3 + side], s_ref, 0,
+        row_stats(s_ref, st, s_ref[LOWER + side], half), column_stats(st, 0),
+        2.0 * n, total, outs,
+    )
 
 
 def pick_far(s_ref, a0, a1, b0, b1, xs):
@@ -261,7 +260,7 @@
     return pl.ds(pl.multiple_of((i ^ (k % 2)) * n, n), n)
 
 
-def early_body(s_ref, t0, t1, ru, rd, *refs):
+def early_body(s_ref, t0, ta, tb, ru, rd, *refs):
     outs, sums = refs[:-1], refs[-1]
     k, g = s_ref[CHIP], s_ref[PLANE]
     n = t0.shape[-1]
@@ -271,8 +270,8 @@
             jnp.int32, (n, n), 1
         )
         own = jnp.where(same & (k == 0), 0.0, own)
-        low = power(t1[0, i] + decode(ru[i]))
-        high = power(t1[1, i] + decode(rd[i]))
+        low = power(ta[0, i] + decode(ru[i]))
+        high = power(tb[0, i] + decode(rd[i]))
         has_low, has_high = g > 0, g < s_ref[PLANES] - 1
         put_slot(outs, g ^ k, i, own.astype(jnp.bfloat16))
         put_slot(outs, jnp.where(has_low, (g - 1) ^ k, -1), i, low.astype(jnp.bfloat16))
@@ -284,20 +283,27 @@
         )
 
 
-def late_body(s_ref, t2, r2, rf, rn, before, *refs):
+def ends_finish_body(s_ref, rf, rn, before, *refs):
+    outs, sums = refs[4:-1], refs[-1]
+    k, g = s_ref[CHIP], s_ref[PLANE]
+    n = rf.shape[-1]
+    outer = (g == 0) | (g == s_ref[PLANES] - 1)
+    for i in range(2):
+        at = column_place(k, i, n)
+        three = power(decode(rf[i]) + decode(rn[i]))
+        put_slot(outs, jnp.where(outer, g ^ 3 ^ k, -1), i, three.astype(jnp.bfloat16))
+        sums[0:1, at] = before[0:1, at] + jnp.where(outer, column_total(three), 0.0)
+
+
+def late_body(s_ref, t2, r2, before, *refs):
     outs, sums = refs[4:-1], refs[-1]
     k, g = s_ref[CHIP], s_ref[PLANE]
     n = t2.shape[-1]
-    outer = (g == 0) | (g == s_ref[PLANES] - 1)
     for i in range(2):
         at = column_place(k, i, n)
         two = power(t2[0, i] + decode(r2[i]))
-        three = power(decode(rf[i]) + decode(rn[i]))
         put_slot(outs, g ^ 2 ^ k, i, two.astype(jnp.bfloat16))
-        put_slot(outs, jnp.where(outer, g ^ 3 ^ k, -1), i, three.astype(jnp.bfloat16))
-        sums[0:1, at] = (
-            before[0:1, at] + column_total(two) + jnp.where(outer, column_total(three), 0.0)
-        )
+        sums[0:1, at] = before[0:1, at] + column_total(two)
 
 
 def place_body(s_ref, t0, t1, t2, t3, out_ref):
@@ -439,9 +445,9 @@
         end, lambda k, h, g: (k, h, 1) if g == 0 else ((k, h, g - 1) if g == last else None)
     )
 
-    def blocks(body, n, scratch, *operands, behind=0):
+    def blocks(body, n, scratch, *operands, behind=0, **extra):
         return pl.pallas_call(
-            functools.partial(body, total=total),
+            functools.partial(body, total=total, **extra),
             in_specs=[scalars()]
             + [whole()] * (len(operands) - behind)
             + [pl.BlockSpec(memory_space=pl.ANY)] * behind,
@@ -458,7 +464,8 @@
     near_other = send(near, flip)
     kept = (half, rows)
     w0 = blocks(diagonal_body, 1, [], *pay, own, oth, own_stats)
-    w1 = blocks(near_body, 2, [], *up1, *dn1, own, oth, stats)
+    w1a = blocks(near_body, 1, [], *up1, own, oth, stats, side=0)
+    w1b = blocks(near_body, 1, [], *dn1, own, oth, stats, side=1)
     w3 = blocks(ends_body, 1, [kept, (rows, width)], *up2, *dn2, near, near_other, stats)
 
     def reduce_tiles(w):
@@ -480,7 +487,8 @@
 
     (t0,) = turn(reduce_tiles(w0), [None], [None])
     w2 = blocks(far_body, 1, [kept], *up2, *dn2, own, oth, stats)
-    t1, e_up, e_dn = turn(reduce_tiles(w1), [0, 1], [None, None])
+    ta, e_up = turn(reduce_tiles(w1a), [0], [None])
+    tb, e_dn = turn(reduce_tiles(w1b), [0], [None])
     t2, e_two = turn(reduce_tiles(w2), [0], [None])
     _, e_three, k_three = turn(reduce_tiles(w3), [0], [1])
 
@@ -490,7 +498,7 @@
     r2 = send(e_two, side(lambda g: g ^ 2))
     inner = lambda g: 0 < g < last
     r3f = send(e_three, side(lambda g: (g ^ 2) if inner(g) else None))
-    r3n = send(k_three, lambda k, h, g: (k, h, g ^ 1) if inner(g) else None)
+    r3n = send(k_three, lambda k, h, g: (k, h, g ^ 1))
 
     def finish(body, *operands, over=0):
         return pl.pallas_call(
@@ -503,8 +511,9 @@
             name="finish_tiles",
         )(info, *operands)
 
-    *close, close_sums = finish(early_body, t0, t1, ru, rd)
-    *tiles, tile_sums = finish(late_body, t2, r2, r3f, r3n, close_sums, *close, over=len(close))
+    *close, close_sums = finish(early_body, t0, ta, tb, ru, rd)
+    *most, most_sums = finish(ends_finish_body, r3f, r3n, close_sums, *close, over=len(close))
+    *tiles, tile_sums = finish(late_body, t2, r2, most_sums, *most, over=len(most))
     got = [tiles[0]] + [send(tiles[j], lambda k, h, g, j=j: (k ^ j, h, g)) for j in (1, 2, 3)]
     adjacency = pl.pallas_call(
         place_body,

time: 207 us -> 196 us (0.947)
  starting transfers between devices: 91.5 us -> 72.2 us
  waiting for transfers between devices: 79.3 us -> 85.1 us
    ppermute x41 -> x44, starting transfers between devices: 91.5 us -> 72.2 us  [send(): return lax.ppermute(x, AXES, perm(f))]
    ppermute x41 -> x44, waiting for transfers between devices: 79.3 us -> 85.1 us  [send(): return lax.ppermute(x, AXES, perm(f))]
    pallas_call x4 -> x5, Pallas kernels: 5.84 us -> 6.6 us  [turn(): pl.pallas_call(functools.partial(turn_body, turns=turns, keeps=keeps), in...]
    pallas_call x4 -> x5, Pallas kernels: 12.8 us -> 13.3 us  [blocks(): pl.pallas_call(functools.partial(body, total=total, **extra), in_specs=[s...]
  transfers between devices with their start and end apart: 41 -> 44, of which waited for: 14 -> 19; matrix products, arithmetic and copies ran while one was open for 1% -> 1% of each run, Pallas kernels for 11% -> 13%
where the time goes in v7:
time: 196 us; the launch traced here: 195 us
  waiting for transfers between devices  85.1 us (43%)
  starting transfers between devices  72.2 us (37%)
  Pallas kernels  30.6 us (16%)
  other arithmetic  5.84 us (3%)
    ppermute x44, waiting for transfers between devices, send(): return lax.ppermute(x, AXES, perm(f))  85.1 us
    ppermute x44, starting transfers between devices, send(): return lax.ppermute(x, AXES, perm(f))  72.2 us
    pallas_call x5, Pallas kernels, blocks(): pl.pallas_call(functools.partial(body, total=total, **extra), in_specs=[s...  13.3 us
    pallas_call x5, Pallas kernels, turn(): pl.pallas_call(functools.partial(turn_body, turns=turns, keeps=keeps), in...  6.6 us
    reduce_sum x1, other arithmetic, folded_shards(): halves = jnp.sum(widened.reshape(2, half_cells, width), axis=1)  3.96 us
  transfers between devices with their start and end apart: 44, of which 19 were waited for; matrix products, arithmetic and copies ran while one was open for 1% of the time, Pallas kernels for 13%

profile of v7, /device:TPU:0, one launch (start us, length us, event | category | flops | bytes accessed | tf_op | source)
XLA Modules:
  0.0 195.0 jit_solution(12871435254349697885)
XLA Ops:
  1.3 4.0 %bitcast_reduce_fusion = (f32[2,1024]{1,0:T(2,128)S(1)}, bf16[1024,1024]{1,0:T(8,128)(2,1)S(1)}) fusion(f32[1024]{0:T(1024)S(1)} %convert_divide_fusion, s32[1024,1024]{1,0:T(8,128)} %param.2), kind=kLoop, calls=%fused_computation | loop fusion | flops 5240832 | bytes 6303744 | tf_op jit(solution)/shard_map/reduce_sum | solution.py:422
  6.9 2.8 %collective-permute-done.a = bf16[1024,1024]{1,0:T(8,128)(2,1)} collective-permute-done((bf16[1024,1024]{1,0:T(8,128)(2,1)S(1)}, bf16[1024,1024]{1,0:T(8,128)(2,1)}, u32[]{:S(2)}, u32[]{:S(2)}) %collective-permute-start) | collective-permute-done | bytes 2097184 | tf_op jit(solution)/shard_map/ppermute | solution.py:376
  11.9 4.9 %collective-permute-start.19 = (bf16[1024,512]{1,0:T(8,128)(2,1)S(1)}, bf16[1024,512]{1,0:T(8,128)(2,1)S(1)}, u32[]{:S(2)}, u32[]{:S(2)}) collective-permute-start(bf16[1024,512]{1,0:T(8,128)(2,1)S(1)} %get-tuple-element.74), channel_id=1, source_target_pairs={{0,1},{3,2},{4,5},{7,6},{8,9},{11,10},{12,13},{15,14},{16,17},{19,... | collective-permute-start | bytes 3145736 | tf_op jit(solution)/shard_map/ppermute | solution.py:376
  26.3 3.0 %collective-permute-start.13 = (f32[8,1024]{1,0:T(8,128)S(1)}, f32[8,1024]{1,0:T(8,128)S(1)}, u32[]{:S(2)}, u32[]{:S(2)}) collective-permute-start(f32[8,1024]{1,0:T(8,128)S(1)} %get-tuple-element.117), channel_id=1, source_target_pairs={{0,2},{1,3},{2,0},{3,1},{4,6},{5,7},{6,4},{7,5},{8,10},{9,11},{10,... | collective-permute-start | bytes 98312 | tf_op jit(solution)/shard_map/ppermute | solution.py:376
  32.0 9.0 %collective-permute-done.12 = f32[8,1024]{1,0:T(8,128)S(1)} collective-permute-done((f32[8,1024]{1,0:T(8,128)S(1)}, f32[8,1024]{1,0:T(8,128)S(1)}, u32[]{:S(2)}, u32[]{:S(2)}) %collective-permute-start.12) | collective-permute-done | bytes 32800 | tf_op jit(solution)/shard_map/ppermute | solution.py:376
  41.0 4.4 %collective-permute-start.3 = (bf16[256,1024]{1,0:T(8,128)(2,1)S(1)}, bf16[256,1024]{1,0:T(8,128)(2,1)S(1)}, u32[]{:S(2)}, u32[]{:S(2)}) collective-permute-start(bf16[256,1024]{1,0:T(8,128)(2,1)S(1)} %get-tuple-element.63.a1), channel_id=1, source_target_pairs={{0,1},{1,2},{2,3},{4,5},{5,6},{6,7},{8,9},{9,10},{10,11},{12,13},{... | collective-permute-start | bytes 1572872 | tf_op jit(solution)/shard_map/ppermute | solution.py:376
  48.1 5.5 %collective-permute-done.1.x0 = bf16[256,1024]{1,0:T(8,128)(2,1)S(1)} collective-permute-done((bf16[256,1024]{1,0:T(8,128)(2,1)S(1)}, bf16[256,1024]{1,0:T(8,128)(2,1)S(1)}, u32[]{:S(2)}, u32[]{:S(2)}) %collective-permute-start.1) | collective-permute-done | bytes 524320 | tf_op jit(solution)/shard_map/ppermute | solution.py:376
  54.3 9.7 %collective-permute-done.3.x1 = bf16[256,1024]{1,0:T(8,128)(2,1)S(1)} collective-permute-done((bf16[256,1024]{1,0:T(8,128)(2,1)S(1)}, bf16[256,1024]{1,0:T(8,128)(2,1)S(1)}, u32[]{:S(2)}, u32[]{:S(2)}) %collective-permute-start.3) | collective-permute-done | bytes 524320 | tf_op jit(solution)/shard_map/ppermute | solution.py:376
  66.0 5.2 %collective-permute-done.7.x1 = bf16[256,1024]{1,0:T(8,128)(2,1)S(1)} collective-permute-done((bf16[256,1024]{1,0:T(8,128)(2,1)S(1)}, bf16[256,1024]{1,0:T(8,128)(2,1)S(1)}, u32[]{:S(2)}, u32[]{:S(2)}) %collective-permute-start.7) | collective-permute-done | bytes 524320 | tf_op jit(solution)/shard_map/ppermute | solution.py:376
  72.7 3.5 %partial_blocks.7 = (f32[1,2,256,256]{3,2,1,0:T(8,128)S(1)}, bf16[1,2,256,256]{3,2,1,0:T(8,128)(2,1)S(1)}, bf16[1,2,256,256]{3,2,1,0:T(8,128)(2,1)S(1)}, bf16[1,2,256,256]{3,2,1,0:T(8,128)(2,1)S(1)}) custom-call(s32[9]{0:T(128)S(1)} %stack.58.s_ref, bf16[256,1024]{1,0:T(8,128)(2,1)S(1)} %get-tuple-element.62.a0, bf16[256,1024]{1,0:T(8,128)(2,1)S(1)} %get-tuple-element.63.a1, ...), custom_call_target="tpu_custom_call" | custom-call | tf_op jit(solution)/shard_map/partial_blocks/pallas_call | solution.py:449
  84.0 9.0 %collective-permute-done.8.b1 = bf16[256,1024]{1,0:T(8,128)(2,1)S(1)} collective-permute-done((bf16[256,1024]{1,0:T(8,128)(2,1)S(1)}, bf16[256,1024]{1,0:T(8,128)(2,1)S(1)}, u32[]{:S(2)}, u32[]{:S(2)}) %collective-permute-start.8) | collective-permute-done | bytes 524320 | tf_op jit(solution)/shard_map/ppermute | solution.py:376
  98.5 2.6 %partial_blocks.6 = (f32[1,2,256,256]{3,2,1,0:T(8,128)S(1)}, bf16[1,2,256,256]{3,2,1,0:T(8,128)(2,1)S(1)}, bf16[1,2,256,256]{3,2,1,0:T(8,128)(2,1)S(1)}, bf16[1,2,256,256]{3,2,1,0:T(8,128)(2,1)S(1)}) custom-call(s32[9]{0:T(128)S(1)} %stack.58.s_ref, bf16[256,1024]{1,0:T(8,128)(2,1)S(1)} %collective-permute-done.2.a0, ...), custom_call_target="tpu_custom_call" | custom-call | tf_op jit(solution)/shard_map/partial_blocks/pallas_call | solution.py:449
  105.1 3.6 %collective-permute-done.29.r1 = bf16[1,2,256,256]{3,2,1,0:T(8,128)(2,1)S(1)} collective-permute-done((bf16[1,2,256,256]{3,2,1,0:T(8,128)(2,1)S(1)}, bf16[1,2,256,256]{3,2,1,0:T(8,128)(2,1)S(1)}, u32[]{:S(2)}, u32[]{:S(2)}) %collective-permute-start.29) | collective-permute-done | bytes 262176 | tf_op jit(solution)/shard_map/ppermute | solution.py:376
  112.6 3.3 %collective-permute-done.30.r2 = bf16[1,2,256,256]{3,2,1,0:T(8,128)(2,1)S(1)} collective-permute-done((bf16[1,2,256,256]{3,2,1,0:T(8,128)(2,1)S(1)}, bf16[1,2,256,256]{3,2,1,0:T(8,128)(2,1)S(1)}, u32[]{:S(2)}, u32[]{:S(2)}) %collective-permute-start.30) | collective-permute-done | bytes 262176 | tf_op jit(solution)/shard_map/ppermute | solution.py:376
  120.5 6.6 %collective-permute-done.22.r2 = bf16[1,2,256,256]{3,2,1,0:T(8,128)(2,1)S(1)} collective-permute-done((bf16[1,2,256,256]{3,2,1,0:T(8,128)(2,1)S(1)}, bf16[1,2,256,256]{3,2,1,0:T(8,128)(2,1)S(1)}, u32[]{:S(2)}, u32[]{:S(2)}) %collective-permute-start.22) | collective-permute-done | bytes 262176 | tf_op jit(solution)/shard_map/ppermute | solution.py:376
  134.6 9.4 %collective-permute-done.27.r2 = bf16[1,2,256,256]{3,2,1,0:T(8,128)(2,1)S(1)} collective-permute-done((bf16[1,2,256,256]{3,2,1,0:T(8,128)(2,1)S(1)}, bf16[1,2,256,256]{3,2,1,0:T(8,128)(2,1)S(1)}, u32[]{:S(2)}, u32[]{:S(2)}) %collective-permute-start.27) | collective-permute-done | bytes 262176 | tf_op jit(solution)/shard_map/ppermute | solution.py:376
  144.0 3.5 %collective-permute-start.35 = (bf16[2,256,256]{2,1,0:T(8,128)(2,1)S(1)}, bf16[2,256,256]{2,1,0:T(8,128)(2,1)S(1)}, u32[]{:S(2)}, u32[]{:S(2)}) collective-permute-start(bf16[2,256,256]{2,1,0:T(8,128)(2,1)S(1)} %get-tuple-element.95), channel_id=1, source_target_pairs={{0,1},{1,2},{2,3},{4,5},{5,6},{6,7},{8,9},{9,10},{10,11},{12,13},{... | collective-permute-start | bytes 786440 | tf_op jit(solution)/shard_map/ppermute | solution.py:376
  150.1 2.7 %collective-permute-start.25 = (bf16[2,256,256]{2,1,0:T(8,128)(2,1)S(1)}, bf16[2,256,256]{2,1,0:T(8,128)(2,1)S(1)}, u32[]{:S(2)}, u32[]{:S(2)}) collective-permute-start(bf16[2,256,256]{2,1,0:T(8,128)(2,1)S(1)} %get-tuple-element.80), channel_id=1, source_target_pairs={{0,1},{1,0},{2,3},{3,2},{4,5},{5,4},{6,7},{7,6},{8,9},{9,8},{10,11... | collective-permute-start | bytes 786440 | tf_op jit(solution)/shard_map/ppermute | solution.py:376
  156.0 4.0 %collective-permute-done.36.rd = bf16[2,256,256]{2,1,0:T(8,128)(2,1)S(1)} collective-permute-done((bf16[2,256,256]{2,1,0:T(8,128)(2,1)S(1)}, bf16[2,256,256]{2,1,0:T(8,128)(2,1)S(1)}, u32[]{:S(2)}, u32[]{:S(2)}) %collective-permute-start.36) | collective-permute-done | bytes 262176 | tf_op jit(solution)/shard_map/ppermute | solution.py:376
  161.3 6.9 %collective-permute-done.24.rf = bf16[2,256,256]{2,1,0:T(8,128)(2,1)S(1)} collective-permute-done((bf16[2,256,256]{2,1,0:T(8,128)(2,1)S(1)}, bf16[2,256,256]{2,1,0:T(8,128)(2,1)S(1)}, u32[]{:S(2)}, u32[]{:S(2)}) %collective-permute-start.24) | collective-permute-done | bytes 262176 | tf_op jit(solution)/shard_map/ppermute | solution.py:376
  173.5 3.6 %collective-permute-start.38 = (bf16[2,256,256]{2,1,0:T(8,128)(2,1)S(1)}, bf16[2,256,256]{2,1,0:T(8,128)(2,1)S(1)}, u32[]{:S(2)}, u32[]{:S(2)}) collective-permute-start(bf16[2,256,256]{2,1,0:T(8,128)(2,1)S(1)} %get-tuple-element.109), channel_id=1, source_target_pairs={{0,16},{1,17},{2,18},{3,19},{4,20},{5,21},{6,22},{7,23},{8,24},{9,... | collective-permute-start | bytes 786440 | tf_op jit(solution)/shard_map/ppermute | solution.py:376
  177.8 4.2 %collective-permute-start.41 = (f32[1,512]{1,0:T(1,128)S(1)}, f32[1,512]{1,0:T(1,128)S(1)}, u32[]{:S(2)}, u32[]{:S(2)}) collective-permute-start(f32[1,512]{1,0:T(1,128)S(1)} %get-tuple-element.111), channel_id=1, source_target_pairs={{0,1},{1,9},{2,17},{3,25},{4,5},{5,13},{6,21},{7,29},{8,0},{9,8},{... | collective-permute-start | bytes 6152 | tf_op jit(solution)/shard_map/ppermute | solution.py:376
  182.0 2.7 %collective-permute-start.42 = (f32[1,512]{1,0:T(1,128)S(1)}, f32[1,512]{1,0:T(1,128)S(1)}, u32[]{:S(2)}, u32[]{:S(2)}) collective-permute-start(f32[1,512]{1,0:T(1,128)S(1)} %get-tuple-element.111), channel_id=1, source_target_pairs={{0,2},{1,10},{2,18},{3,26},{4,6},{5,14},{6,22},{7,30},{8,3},{9,11}... | collective-permute-start | bytes 6152 | tf_op jit(solution)/shard_map/ppermute | solution.py:376
  184.7 6.3 %collective-permute-start.43 = (f32[1,512]{1,0:T(1,128)S(1)}, f32[1,512]{1,0:T(1,128)S(1)}, u32[]{:S(2)}, u32[]{:S(2)}) collective-permute-start(f32[1,512]{1,0:T(1,128)S(1)} %get-tuple-element.111), channel_id=1, source_target_pairs={{0,3},{1,11},{2,19},{3,27},{4,7},{5,15},{6,23},{7,31},{8,2},{9,10}... | collective-permute-start | bytes 6152 | tf_op jit(solution)/shard_map/ppermute | solution.py:376
  (94 shorter events, 73.6 us)
Async XLA Ops:
  11.9 36.1 %collective-permute-start.19 = (bf16[1024,512]{1,0:T(8,128)(2,1)S(1)}, bf16[1024,512]{1,0:T(8,128)(2,1)S(1)}, u32[]{:S(2)}, u32[]{:S(2)}) collective-permute-start(bf16[1024,512]{1,0:T(8,128)(2,1)S(1)} %get-tuple-element.74), channel_id=1, source_target_pairs={{0,1},{3,2},{4,5},{7,6},{8,9},{11,10},{12,13},{15,14},{16,17},{19,... | collective-permute-start | bytes 3145736 | tf_op jit(solution)/shard_map/ppermute | solution.py:376
  26.3 19.1 %collective-permute-start.13 = (f32[8,1024]{1,0:T(8,128)S(1)}, f32[8,1024]{1,0:T(8,128)S(1)}, u32[]{:S(2)}, u32[]{:S(2)}) collective-permute-start(f32[8,1024]{1,0:T(8,128)S(1)} %get-tuple-element.117), channel_id=1, source_target_pairs={{0,2},{1,3},{2,0},{3,1},{4,6},{5,7},{6,4},{7,5},{8,10},{9,11},{10,... | collective-permute-start | bytes 98312 | tf_op jit(solution)/shard_map/ppermute | solution.py:376
  30.7 22.9 %collective-permute-start.1 = (bf16[256,1024]{1,0:T(8,128)(2,1)S(1)}, bf16[256,1024]{1,0:T(8,128)(2,1)S(1)}, u32[]{:S(2)}, u32[]{:S(2)}) collective-permute-start(bf16[256,1024]{1,0:T(8,128)(2,1)S(1)} %get-tuple-element.62.a0), channel_id=1, source_target_pairs={{0,1},{1,2},{2,3},{4,5},{5,6},{6,7},{8,9},{9,10},{10,11},{12,13},{... | collective-permute-start | bytes 1572872 | tf_op jit(solution)/shard_map/ppermute | solution.py:376
  41.0 23.0 %collective-permute-start.3 = (bf16[256,1024]{1,0:T(8,128)(2,1)S(1)}, bf16[256,1024]{1,0:T(8,128)(2,1)S(1)}, u32[]{:S(2)}, u32[]{:S(2)}) collective-permute-start(bf16[256,1024]{1,0:T(8,128)(2,1)S(1)} %get-tuple-element.63.a1), channel_id=1, source_target_pairs={{0,1},{1,2},{2,3},{4,5},{5,6},{6,7},{8,9},{9,10},{10,11},{12,13},{... | collective-permute-start | bytes 1572872 | tf_op jit(solution)/shard_map/ppermute | solution.py:376
  45.4 19.3 %collective-permute-start.5 = (bf16[256,1024]{1,0:T(8,128)(2,1)S(1)}, bf16[256,1024]{1,0:T(8,128)(2,1)S(1)}, u32[]{:S(2)}, u32[]{:S(2)}) collective-permute-start(bf16[256,1024]{1,0:T(8,128)(2,1)S(1)} %get-tuple-element.64.b0), channel_id=1, source_target_pairs={{1,0},{2,1},{3,2},{5,4},{6,5},{7,6},{9,8},{10,9},{11,10},{13,12},{... | collective-permute-start | bytes 1572872 | tf_op jit(solution)/shard_map/ppermute | solution.py:376
  46.7 24.5 %collective-permute-start.7 = (bf16[256,1024]{1,0:T(8,128)(2,1)S(1)}, bf16[256,1024]{1,0:T(8,128)(2,1)S(1)}, u32[]{:S(2)}, u32[]{:S(2)}) collective-permute-start(bf16[256,1024]{1,0:T(8,128)(2,1)S(1)} %get-tuple-element.65.b1), channel_id=1, source_target_pairs={{1,0},{2,1},{3,2},{5,4},{6,5},{7,6},{9,8},{10,9},{11,10},{13,12},{... | collective-permute-start | bytes 1572872 | tf_op jit(solution)/shard_map/ppermute | solution.py:376
  48.0 49.8 %collective-permute-start.20 = (bf16[1024,512]{1,0:T(8,128)(2,1)S(1)}, bf16[1024,512]{1,0:T(8,128)(2,1)S(1)}, u32[]{:S(2)}, u32[]{:S(2)}) collective-permute-start(bf16[1024,512]{1,0:T(8,128)(2,1)S(1)} %collective-permute-done.19.na), channel_id=1, source_target_pairs={{0,4},{1,5},{2,6},{3,7},{4,0},{5,1},{6,2},{7,3},{8,12},{9,13},{10,... | collective-permute-start | bytes 3145736 | tf_op jit(solution)/shard_map/ppermute | solution.py:376
  53.6 25.0 %collective-permute-start.2 = (bf16[256,1024]{1,0:T(8,128)(2,1)S(1)}, bf16[256,1024]{1,0:T(8,128)(2,1)S(1)}, u32[]{:S(2)}, u32[]{:S(2)}) collective-permute-start(bf16[256,1024]{1,0:T(8,128)(2,1)S(1)} %collective-permute-done.1.x0), channel_id=1, source_target_pairs={{1,2},{2,3},{5,6},{6,7},{9,10},{10,11},{13,14},{14,15},{17,18},{18... | collective-permute-start | bytes 1572872 | tf_op jit(solution)/shard_map/ppermute | solution.py:376
  64.7 17.8 %collective-permute-start.6 = (bf16[256,1024]{1,0:T(8,128)(2,1)S(1)}, bf16[256,1024]{1,0:T(8,128)(2,1)S(1)}, u32[]{:S(2)}, u32[]{:S(2)}) collective-permute-start(bf16[256,1024]{1,0:T(8,128)(2,1)S(1)} %collective-permute-done.5.x0), channel_id=1, source_target_pairs={{1,0},{2,1},{5,4},{6,5},{9,8},{10,9},{13,12},{14,13},{17,16},{18,1... | collective-permute-start | bytes 1572872 | tf_op jit(solution)/shard_map/ppermute | solution.py:376
  71.2 21.8 %collective-permute-start.8 = (bf16[256,1024]{1,0:T(8,128)(2,1)S(1)}, bf16[256,1024]{1,0:T(8,128)(2,1)S(1)}, u32[]{:S(2)}, u32[]{:S(2)}) collective-permute-start(bf16[256,1024]{1,0:T(8,128)(2,1)S(1)} %collective-permute-done.7.x1), channel_id=1, source_target_pairs={{1,0},{2,1},{5,4},{6,5},{9,8},{10,9},{13,12},{14,13},{17,16},{18,1... | collective-permute-start | bytes 1572872 | tf_op jit(solution)/shard_map/ppermute | solution.py:376
  78.6 22.4 %collective-permute-start.26 = (bf16[1,2,256,256]{3,2,1,0:T(8,128)(2,1)S(1)}, bf16[1,2,256,256]{3,2,1,0:T(8,128)(2,1)S(1)}, u32[]{:S(2)}, u32[]{:S(2)}) collective-permute-start(bf16[1,2,256,256]{3,2,1,0:T(8,128)(2,1)S(1)} %get-tuple-element.82), channel_id=1, source_target_pairs={{0,8},{1,9},{2,10},{3,11},{4,12},{5,13},{6,14},{7,15},{8,0},{9,1},... | collective-permute-start | bytes 786440 | tf_op jit(solution)/shard_map/ppermute | solution.py:376
  80.2 21.5 %collective-permute-start.32 = (bf16[1,2,256,256]{3,2,1,0:T(8,128)(2,1)S(1)}, bf16[1,2,256,256]{3,2,1,0:T(8,128)(2,1)S(1)}, u32[]{:S(2)}, u32[]{:S(2)}) collective-permute-start(bf16[1,2,256,256]{3,2,1,0:T(8,128)(2,1)S(1)} %get-tuple-element.91), channel_id=1, source_target_pairs={{0,8},{1,9},{2,10},{3,11},{4,12},{5,13},{6,14},{7,15},{8,0},{9,1},... | collective-permute-start | bytes 786440 | tf_op jit(solution)/shard_map/ppermute | solution.py:376
  82.5 21.6 %collective-permute-start.33 = (bf16[1,2,256,256]{3,2,1,0:T(8,128)(2,1)S(1)}, bf16[1,2,256,256]{3,2,1,0:T(8,128)(2,1)S(1)}, u32[]{:S(2)}, u32[]{:S(2)}) collective-permute-start(bf16[1,2,256,256]{3,2,1,0:T(8,128)(2,1)S(1)} %get-tuple-element.92), channel_id=1, source_target_pairs={{0,16},{1,17},{2,18},{3,19},{4,20},{5,21},{6,22},{7,23},{8,24},{9,... | collective-permute-start | bytes 786440 | tf_op jit(solution)/shard_map/ppermute | solution.py:376
  104.6 22.5 %collective-permute-start.22 = (bf16[1,2,256,256]{3,2,1,0:T(8,128)(2,1)S(1)}, bf16[1,2,256,256]{3,2,1,0:T(8,128)(2,1)S(1)}, u32[]{:S(2)}, u32[]{:S(2)}) collective-permute-start(bf16[1,2,256,256]{3,2,1,0:T(8,128)(2,1)S(1)} %get-tuple-element.77), channel_id=1, source_target_pairs={{0,16},{1,17},{2,18},{3,19},{4,20},{5,21},{6,22},{7,23},{8,24},{9,... | collective-permute-start | bytes 786440 | tf_op jit(solution)/shard_map/ppermute | solution.py:376
  108.8 19.8 %collective-permute-start.23 = (bf16[1,2,256,256]{3,2,1,0:T(8,128)(2,1)S(1)}, bf16[1,2,256,256]{3,2,1,0:T(8,128)(2,1)S(1)}, u32[]{:S(2)}, u32[]{:S(2)}) collective-permute-start(bf16[1,2,256,256]{3,2,1,0:T(8,128)(2,1)S(1)} %get-tuple-element.78), channel_id=1, source_target_pairs={{0,24},{1,25},{2,26},{3,27},{4,28},{5,29},{6,30},{7,31},{8,16},{9,... | collective-permute-start | bytes 786440 | tf_op jit(solution)/shard_map/ppermute | solution.py:376
  115.9 28.1 %collective-permute-start.27 = (bf16[1,2,256,256]{3,2,1,0:T(8,128)(2,1)S(1)}, bf16[1,2,256,256]{3,2,1,0:T(8,128)(2,1)S(1)}, u32[]{:S(2)}, u32[]{:S(2)}) collective-permute-start(bf16[1,2,256,256]{3,2,1,0:T(8,128)(2,1)S(1)} %get-tuple-element.83), channel_id=1, source_target_pairs={{0,16},{1,17},{2,18},{3,19},{4,20},{5,21},{6,22},{7,23},{8,24},{9,... | collective-permute-start | bytes 786440 | tf_op jit(solution)/shard_map/ppermute | solution.py:376
  116.4 31.1 %collective-permute-start.15 = (bf16[1,2,256,256]{3,2,1,0:T(8,128)(2,1)S(1)}, bf16[1,2,256,256]{3,2,1,0:T(8,128)(2,1)S(1)}, u32[]{:S(2)}, u32[]{:S(2)}) collective-permute-start(bf16[1,2,256,256]{3,2,1,0:T(8,128)(2,1)S(1)} %get-tuple-element.69), channel_id=1, source_target_pairs={{0,8},{1,9},{2,10},{3,11},{4,12},{5,13},{6,14},{7,15},{8,0},{9,1},... | collective-permute-start | bytes 786440 | tf_op jit(solution)/shard_map/ppermute | solution.py:376
  120.0 28.8 %collective-permute-start.16 = (bf16[1,2,256,256]{3,2,1,0:T(8,128)(2,1)S(1)}, bf16[1,2,256,256]{3,2,1,0:T(8,128)(2,1)S(1)}, u32[]{:S(2)}, u32[]{:S(2)}) collective-permute-start(bf16[1,2,256,256]{3,2,1,0:T(8,128)(2,1)S(1)} %get-tuple-element.70), channel_id=1, source_target_pairs={{0,16},{1,17},{2,18},{3,19},{4,20},{5,21},{6,22},{7,23},{8,24},{9,... | collective-permute-start | bytes 786440 | tf_op jit(solution)/shard_map/ppermute | solution.py:376
  127.2 22.9 %collective-permute-start.17 = (bf16[1,2,256,256]{3,2,1,0:T(8,128)(2,1)S(1)}, bf16[1,2,256,256]{3,2,1,0:T(8,128)(2,1)S(1)}, u32[]{:S(2)}, u32[]{:S(2)}) collective-permute-start(bf16[1,2,256,256]{3,2,1,0:T(8,128)(2,1)S(1)} %get-tuple-element.71), channel_id=1, source_target_pairs={{0,24},{1,25},{2,26},{3,27},{4,28},{5,29},{6,30},{7,31},{8,16},{9,... | collective-permute-start | bytes 786440 | tf_op jit(solution)/shard_map/ppermute | solution.py:376
  128.6 25.4 %collective-permute-start.28 = (bf16[1,2,256,256]{3,2,1,0:T(8,128)(2,1)S(1)}, bf16[1,2,256,256]{3,2,1,0:T(8,128)(2,1)S(1)}, u32[]{:S(2)}, u32[]{:S(2)}) collective-permute-start(bf16[1,2,256,256]{3,2,1,0:T(8,128)(2,1)S(1)} %get-tuple-element.84), channel_id=1, source_target_pairs={{0,24},{1,25},{2,26},{3,27},{4,28},{5,29},{6,30},{7,31},{8,16},{9,... | collective-permute-start | bytes 786440 | tf_op jit(solution)/shard_map/ppermute | solution.py:376
  148.8 19.4 %collective-permute-start.24 = (bf16[2,256,256]{2,1,0:T(8,128)(2,1)S(1)}, bf16[2,256,256]{2,1,0:T(8,128)(2,1)S(1)}, u32[]{:S(2)}, u32[]{:S(2)}) collective-permute-start(bf16[2,256,256]{2,1,0:T(8,128)(2,1)S(1)} %get-tuple-element.79), channel_id=1, source_target_pairs={{1,3},{2,0},{5,7},{6,4},{9,11},{10,8},{13,15},{14,12},{17,23},{18,... | collective-permute-start | bytes 786440 | tf_op jit(solution)/shard_map/ppermute | solution.py:376
  150.1 18.1 %collective-permute-start.25 = (bf16[2,256,256]{2,1,0:T(8,128)(2,1)S(1)}, bf16[2,256,256]{2,1,0:T(8,128)(2,1)S(1)}, u32[]{:S(2)}, u32[]{:S(2)}) collective-permute-start(bf16[2,256,256]{2,1,0:T(8,128)(2,1)S(1)} %get-tuple-element.80), channel_id=1, source_target_pairs={{0,1},{1,0},{2,3},{3,2},{4,5},{5,4},{6,7},{7,6},{8,9},{9,8},{10,11... | collective-permute-start | bytes 786440 | tf_op jit(solution)/shard_map/ppermute | solution.py:376
  172.0 20.9 %collective-permute-start.37 = (bf16[2,256,256]{2,1,0:T(8,128)(2,1)S(1)}, bf16[2,256,256]{2,1,0:T(8,128)(2,1)S(1)}, u32[]{:S(2)}, u32[]{:S(2)}) collective-permute-start(bf16[2,256,256]{2,1,0:T(8,128)(2,1)S(1)} %get-tuple-element.108), channel_id=1, source_target_pairs={{0,8},{1,9},{2,10},{3,11},{4,12},{5,13},{6,14},{7,15},{8,0},{9,1},... | collective-permute-start | bytes 786440 | tf_op jit(solution)/shard_map/ppermute | solution.py:376
  173.5 19.4 %collective-permute-start.38 = (bf16[2,256,256]{2,1,0:T(8,128)(2,1)S(1)}, bf16[2,256,256]{2,1,0:T(8,128)(2,1)S(1)}, u32[]{:S(2)}, u32[]{:S(2)}) collective-permute-start(bf16[2,256,256]{2,1,0:T(8,128)(2,1)S(1)} %get-tuple-element.109), channel_id=1, source_target_pairs={{0,16},{1,17},{2,18},{3,19},{4,20},{5,21},{6,22},{7,23},{8,24},{9,... | collective-permute-start | bytes 786440 | tf_op jit(solution)/shard_map/ppermute | solution.py:376
  (20 other events, 218.5 us)
